TPU v7x, 256 devices: a whole 4x4x8 slice. The times are simulated.
256 devices in a mesh: gx: 32 (over z, x_hi, core), gy: 8 (over x_lo, y).
Axes of the slice: x: 4 (x_hi: 2, x_lo: 2; x = x_hi * 2 + x_lo), y: 4, z: 8, core: 2. Of those that a mesh axis runs over, the one named last changes fastest.
Arguments:
- positions: float32 [3, 12, 64, 128, 256], P(None, None, 'gx', 'gy'), may hold values from 0 to 1
- velocities: float32 [3, 12, 64, 128, 256], P(None, None, 'gx', 'gy'), may hold values from -6 to 6
- thermal: float32 [3, 12, 64, 128, 256], P(None, None, 'gx', 'gy'), may hold values from -6 to 6
- offsets: int32 [12, 64, 128, 256], P(None, 'gx', 'gy'), may hold values from 0 to 7
- occupancy: int32 [12, 64, 128, 256], P(None, 'gx', 'gy'), may hold values from 0 to 1, as said below
- shift_codes: int32 [3], replicated, may hold values from 0 to 7
Outputs:
- new_velocities: float32 [3, 12, 64, 128, 256], P(None, None, 'gx', 'gy')
Inputs may be any that keep to these rules, and one draw needn't show every extreme that they name: `occupancy`: the particles of a storage cell occupy its first slots; every storage cell holds 8 to 12 particles.
All inputs are finite; a program needn't handle non-finite values.
Results may differ from a plain program's by a relative error of at most 0.0001.
Values sent between devices are 32-bit elements; how exact they have to be, the bound alone decides.
No kernel may reach another device: no remote copies, remote signals or barrier semaphores. Data moves between devices by JAX's collectives and lax.ppermute only.
A program may use at most 64 MiB of HBM per device.

v0:
```python
import functools

import jax
import jax.numpy as jnp
from jax import lax
from jax.experimental import pallas as pl
from jax.experimental.pallas import tpu as pltpu
from jax.sharding import PartitionSpec as P

STEPS = 3
RIDGE = 0.5
GROUPS = 8
F32 = jnp.float32


def bits(code):
    return code // 4, code // 2 % 2, code % 2


def cross(u, v):
    return [
        u[1] * v[2] - u[2] * v[1],
        u[2] * v[0] - u[0] * v[2],
        u[0] * v[1] - u[1] * v[0],
    ]


def plus(terms):
    total = None
    for term in terms:
        total = term if total is None else total + term
    return total


def accumulate(value_ref, code_ref, count, out_ref, lanes, start, per_block, with_count):
    slots = code_ref.shape[0]
    names = (["n"] if with_count else []) + list(range(count))
    for first in range(0, len(names), per_block):
        block = names[first : first + per_block]
        for base in (0, 4):
            sums = [[None] * 4 for _ in block]
            for slot in range(slots):
                code = code_ref[slot]
                masks = [code == base + g for g in range(4)]
                for at, name in enumerate(block):
                    for g in range(4):
                        if name == "n":
                            part = jnp.where(masks[g], 1.0, 0.0)
                        else:
                            part = jnp.where(masks[g], value_ref[name, slot], 0.0)
                        old = sums[at][g]
                        sums[at][g] = part if old is None else old + part
            for at in range(len(block)):
                for g in range(4):
                    out_ref[base + g, start + first + at, 0, :, lanes] = sums[at][g]


def store_codes(offsets, occupancy, code_ref, lanes):
    for slot in range(offsets.shape[0]):
        code_ref[slot] = jnp.where(
            occupancy[slot, 0, :, lanes] == 1, offsets[slot, 0, :, lanes], GROUPS
        )


def first_sums_kernel(pos, vel, thermal, offsets, occupancy, geo, wsum, value_ref, code_ref):
    slots = offsets.shape[0]
    for half in range(pos.shape[4] // 128):
        lanes = pl.ds(half * 128, 128)
        store_codes(offsets, occupancy, code_ref, lanes)
        for slot in range(slots):
            p = [pos[c, slot, 0, :, lanes] for c in range(3)]
            w = [vel[c, slot, 0, :, lanes] - thermal[c, slot, 0, :, lanes] for c in range(3)]
            seconds = [p[0] * p[0], p[1] * p[1], p[2] * p[2], p[0] * p[1], p[0] * p[2], p[1] * p[2]]
            for at, value in enumerate(p + seconds + w + cross(p, w)):
                value_ref[at, slot] = value
        accumulate(value_ref, code_ref, 9, geo, lanes, 0, 5, True)
        accumulate(value_ref.at[pl.ds(9, 6)], code_ref, 6, wsum, lanes, 0, 6, False)


def later_sums_kernel(pos, thermal, offsets, occupancy, dsum1, dsum2, value_ref, code_ref):
    slots = offsets.shape[0]
    for half in range(pos.shape[4] // 128):
        lanes = pl.ds(half * 128, 128)
        store_codes(offsets, occupancy, code_ref, lanes)
        for slot in range(slots):
            p = [pos[c, slot, 0, :, lanes] for c in range(3)]
            hot = [
                [thermal[c, (slot + s) % slots, 0, :, lanes] for c in range(3)] for s in range(3)
            ]
            for s in range(2):
                d = [hot[s][c] - hot[s + 1][c] for c in range(3)]
                for at, value in enumerate(d + cross(p, d)):
                    value_ref[6 * s + at, slot] = value
        accumulate(value_ref.at[pl.ds(0, 6)], code_ref, 6, dsum1, lanes, 0, 6, False)
        accumulate(value_ref.at[pl.ds(6, 6)], code_ref, 6, dsum2, lanes, 0, 6, False)


def roll(value, amount):
    return pltpu.roll(value, amount % value.shape[-1], value.ndim - 1)


def frame_sums(geo, wsum, o, code, row):
    bx, by, bz = bits(code)
    n = geo[o, 0, row]
    s = [geo[o, 1 + c, row] for c in range(3)]
    m = [geo[o, 4 + c, row] for c in range(6)]
    w = [wsum[o, c, row] for c in range(3)]
    l = [wsum[o, 3 + c, row] for c in range(3)]
    b = (bx, by, bz)
    q = [s[c] + n if b[c] else s[c] for c in range(3)]
    qq = []
    for at, (i, j) in enumerate(((0, 0), (1, 1), (2, 2), (0, 1), (0, 2), (1, 2))):
        value = m[at]
        if b[i]:
            value = value + s[j]
        if b[j]:
            value = value + q[i]
        qq.append(value)
    if bx:
        l = [l[0], l[1] - w[2], l[2] + w[1]]
    if by:
        l = [l[0] + w[2], l[1], l[2] - w[0]]
    if bz:
        l = [l[0] - w[1], l[1] + w[0], l[2]]
    return [n] + q + w + l + qq


def expand(geo, wsum, shift, rows, yup, ydn, part, shifted):
    cols = geo.shape[3]
    shifted[cols:, :] = jnp.zeros_like(shifted[cols:, :])
    for by in range(2):
        for bz in range(2):
            low = 2 * by + bz
            for bx in range(2):
                code = 4 * bx + low
                o = code ^ shift
                for row in range(2):
                    values = frame_sums(geo, wsum, o, code, row)
                    for v in range(16):
                        if bx == 1 and row == 1:
                            part[by, bz, 1, v] += values[v]
                        else:
                            part[by, bz, row + 1 - bx, v] = values[v]
    for r in range(3):
        for v in range(16):
            near = part[0, 0, r, v] + roll(part[0, 1, r, v], -1)
            beyond = part[1, 0, r, v] + roll(part[1, 1, r, v], -1)
            shifted[:cols, :] = beyond
            main = near + shifted[1 : cols + 1, :]
            rows[r][v] = main
            rows[r][16, v : v + 1, :] = beyond[0:1]
            yup[r, v : v + 1, :] = main[cols - 1 : cols]
            ydn[r, v : v + 1, :] = beyond[0:1]


def expand_kernel(codes, geo, wsum, row0, row1, row2, yup, ydn, part, shifted):
    expand(geo, wsum, codes[0], (row0, row1, row2), yup, ydn, part, shifted)


def fold_row(row, r, yprev, ynext, out):
    last = row.shape[1] - 1
    out[...] = row[...]
    out[16] = row[16] + yprev[r]
    for v in range(16):
        out[v, last : last + 1, :] = row[v, last : last + 1, :] + ynext[r, v : v + 1, :]


def fold_kernel(row0, row2, yprev, ynext, out0, out2):
    fold_row(row0, 0, yprev, ynext, out0)
    fold_row(row2, 2, yprev, ynext, out2)


def solve(sums):
    inverse = 1.0 / jnp.maximum(sums[0], 1.0)
    first = sums[1:4]
    flow = sums[4:7]
    centre = [value * inverse for value in first]
    drift = [value * inverse for value in flow]
    moment = cross(centre, flow)
    torque = [sums[7 + c] - moment[c] for c in range(3)]
    mxx = sums[10] - first[0] * centre[0]
    myy = sums[11] - first[1] * centre[1]
    mzz = sums[12] - first[2] * centre[2]
    kxy = first[0] * centre[1] - sums[13]
    kxz = first[0] * centre[2] - sums[14]
    kyz = first[1] * centre[2] - sums[15]
    kxx = myy + mzz + RIDGE
    kyy = mxx + mzz + RIDGE
    kzz = mxx + myy + RIDGE
    adj_xx = kyy * kzz - kyz * kyz
    adj_yy = kxx * kzz - kxz * kxz
    adj_zz = kxx * kyy - kxy * kxy
    adj_xy = kxz * kyz - kxy * kzz
    adj_xz = kxy * kyz - kxz * kyy
    adj_yz = kxy * kxz - kxx * kyz
    scale = 1.0 / (kxx * adj_xx + kxy * adj_xy + kxz * adj_xz)
    spin = [
        (adj_xx * torque[0] + adj_xy * torque[1] + adj_xz * torque[2]) * scale,
        (adj_xy * torque[0] + adj_yy * torque[1] + adj_yz * torque[2]) * scale,
        (adj_xz * torque[0] + adj_yz * torque[1] + adj_zz * torque[2]) * scale,
    ]
    turned = cross(spin, centre)
    return [drift[c] - turned[c] for c in range(3)] + spin


def fill_table(own0, row1, own2, yprev, ynext, xprev, xnext, total, table):
    cols = row1.shape[1]
    fold_row(row1, 1, yprev, ynext, total)
    for r in range(3):
        if r == 0:
            read = lambda v, at: own0[v, at, :] + xprev[v, at, :]
        elif r == 1:
            read = lambda v, at: total[v, at, :]
        else:
            read = lambda v, at: own2[v, at, :] + xnext[v, at, :]
        for t in range(cols // 8):
            state = solve([read(v, pl.ds(8 * t, 8)) for v in range(16)])
            for v in range(6):
                table[0, v, r, 8 + 8 * t : 16 + 8 * t, :] = state[v]
                table[1, v, r, 8 + 8 * t : 16 + 8 * t, :] = roll(state[v], 1)
        state = solve([read(16, pl.ds(v, 1)) for v in range(16)])
        for v in range(6):
            wide = jnp.broadcast_to(state[v], (8, state[v].shape[1]))
            table[0, v, r, 0:8, :] = wide
            table[1, v, r, 0:8, :] = roll(wide, 1)


def shift_a(a, spin, b):
    a = list(a)
    if b[0]:
        a = [a[0], a[1] + spin[2], a[2] - spin[1]]
    if b[1]:
        a = [a[0] - spin[2], a[1], a[2] + spin[0]]
    if b[2]:
        a = [a[0] + spin[1], a[1] - spin[0], a[2]]
    return a


def update_groups(geo, dsum, shift, table, wsum):
    cols = geo.shape[3]
    for code in range(GROUPS):
        bx, by, bz = bits(code)
        o = code ^ shift
        for row in range(2):
            for t in range(cols // 8):
                at = pl.ds(8 * t, 8)
                from_col = 8 + 8 * t - by
                values = [table[bz, v, row + 1 - bx, from_col : from_col + 8, :] for v in range(6)]
                spin = values[3:]
                a = shift_a(values[:3], spin, (bx, by, bz))
                n = geo[o, 0, row, at, :]
                s = [geo[o, 1 + c, row, at, :] for c in range(3)]
                xx, yy, zz, xy, xz, yz = [geo[o, 4 + c, row, at, :] for c in range(6)]
                turn = cross(spin, s)
                arm = cross(s, a)
                own = [
                    (yy + zz) * spin[0] - xy * spin[1] - xz * spin[2],
                    (xx + zz) * spin[1] - xy * spin[0] - yz * spin[2],
                    (xx + yy) * spin[2] - xz * spin[0] - yz * spin[1],
                ]
                for c in range(3):
                    wsum[o, c, row, at, :] = dsum[o, c, row, at, :] + n * a[c] + turn[c]
                    wsum[o, 3 + c, row, at, :] = dsum[o, 3 + c, row, at, :] + arm[c] + own[c]


def step_kernel(
    codes, geo, dsum, own0, mid, own2, yprev, ynext, xprev, xnext,
    row0, row1, row2, yup, ydn, total, table, wsum, part, shifted,
):
    fill_table(own0, mid, own2, yprev, ynext, xprev, xnext, total, table)
    update_groups(geo, dsum, codes[0], table, wsum)
    expand(geo, wsum, codes[1], (row0, row1, row2), yup, ydn, part, shifted)


def last_kernel(own0, mid, own2, yprev, ynext, xprev, xnext, table, total):
    fill_table(own0, mid, own2, yprev, ynext, xprev, xnext, total, table)


def pick(mask, yes, no):
    return [jnp.where(mask, y, n) for y, n in zip(yes, no)]


def particles_kernel(codes, table, pos, thermal, offsets, occupancy, out, variants):
    slots = offsets.shape[0]
    row = pl.program_id(0)
    tile = pl.program_id(1)
    for half in range(pos.shape[4] // 128):
        lanes = pl.ds(half * 128, 128)
        for code in range(GROUPS):
            bx, by, bz = bits(code)
            values = [
                table[bz, v, row + 1 - bx, pl.ds(8 * tile, 16), lanes][8 - by : 16 - by]
                for v in range(6)
            ]
            values[:3] = shift_a(values[:3], values[3:], (bx, by, bz))
            for v in range(6):
                variants[code, v] = values[v]
        for slot in range(slots):
            k = offsets[slot, 0, :, lanes] ^ codes[0]
            isx, isy, isz = (k & 4) != 0, (k & 2) != 0, (k & 1) != 0
            used = occupancy[slot, 0, :, lanes] == 1
            state = []
            for v in range(6):
                level = [jnp.where(isx, variants[4 + i, v], variants[i, v]) for i in range(4)]
                level = [jnp.where(isy, level[2 + i], level[i]) for i in range(2)]
                state.append(jnp.where(isz, level[1], level[0]))
            p = [pos[c, slot, 0, :, lanes] for c in range(3)]
            turn = cross(state[3:], p)
            for c in range(3):
                fresh = thermal[c, (slot + STEPS - 1) % slots, 0, :, lanes] + (state[c] + turn[c])
                out[c, slot, 0, :, lanes] = jnp.where(used, fresh, 0.0)


VMEM = pl.BlockSpec(memory_space=pltpu.VMEM)
SMEM = pl.BlockSpec(memory_space=pltpu.SMEM)


def shape(*dims):
    return jax.ShapeDtypeStruct(dims, F32)


def big_spec(lead):
    return pl.BlockSpec((*lead, 1, 8, 256), lambda r, t: (*([0] * len(lead)), r, t, 0))


def local(positions, velocities, thermal, offsets, occupancy, shift_codes):
    slots, rows, cols, depth = offsets.shape
    grid = (rows, cols // 8)
    vec = big_spec((3, slots))
    flat = big_spec((slots,))
    group = lambda count: pltpu.VMEM((GROUPS, count, rows, cols, depth), F32)
    group_shape = lambda count: shape(GROUPS, count, rows, cols, depth)
    group_spec = lambda count: big_spec((GROUPS, count))
    scratch = lambda count: [
        pltpu.VMEM((count, slots, 8, 128), F32),
        pltpu.VMEM((slots, 8, 128), jnp.int32),
    ]

    geo, wsum = pl.pallas_call(
        first_sums_kernel,
        grid=grid,
        in_specs=[vec, vec, vec, flat, flat],
        out_specs=[group_spec(10), group_spec(6)],
        out_shape=[group_shape(10), group_shape(6)],
        scratch_shapes=scratch(15),
        name="first_sums",
    )(positions, velocities, thermal, offsets, occupancy)

    row_shape = shape(17, cols, depth)
    col_shape = shape(3, 16, depth)
    expand_out = [row_shape] * 3 + [col_shape] * 2
    expand_scratch = [
        pltpu.VMEM((2, 2, 3, 16, cols, depth), F32),
        pltpu.VMEM((cols + 8, depth), F32),
    ]
    total = pltpu.VMEM((17, cols, depth), F32)
    table_shape = (2, 6, 3, cols + 8, depth)

    row0, row1, row2, yup, ydn = pl.pallas_call(
        expand_kernel,
        in_specs=[SMEM, VMEM, VMEM],
        out_specs=[VMEM] * 5,
        out_shape=expand_out,
        scratch_shapes=expand_scratch,
        name="expand",
    )(shift_codes[0:1], geo, wsum)

    def ring(axis, by):
        count = lax.axis_size(axis)
        return [(i, (i + by) % count) for i in range(count)]

    dsums = None
    for step in range(STEPS):
        yprev = lax.ppermute(yup, "gy", ring("gy", 1))
        ynext = lax.ppermute(ydn, "gy", ring("gy", -1))
        if dsums is None:
            dsums = pl.pallas_call(
                later_sums_kernel,
                grid=grid,
                in_specs=[vec, vec, flat, flat],
                out_specs=[group_spec(6), group_spec(6)],
                out_shape=[group_shape(6), group_shape(6)],
                scratch_shapes=scratch(12),
                name="later_sums",
            )(positions, thermal, offsets, occupancy)
        own0, own2 = pl.pallas_call(
            fold_kernel,
            in_specs=[VMEM] * 4,
            out_specs=[VMEM] * 2,
            out_shape=[row_shape] * 2,
            name="fold",
        )(row0, row2, yprev, ynext)
        xprev = lax.ppermute(own2, "gx", ring("gx", 1))
        xnext = lax.ppermute(own0, "gx", ring("gx", -1))
        if step + 1 < STEPS:
            row0, row1, row2, yup, ydn = pl.pallas_call(
                step_kernel,
                in_specs=[SMEM] + [VMEM] * 9,
                out_specs=[VMEM] * 5,
                out_shape=expand_out,
                scratch_shapes=[total, pltpu.VMEM(table_shape, F32), group(6)] + expand_scratch,
                name="step",
            )(shift_codes[step : step + 2], geo, dsums[step], own0, row1, own2, yprev, ynext, xprev, xnext)

    table = pl.pallas_call(
        last_kernel,
        in_specs=[VMEM] * 7,
        out_specs=VMEM,
        out_shape=shape(*table_shape),
        scratch_shapes=[total],
        name="last",
    )(own0, row1, own2, yprev, ynext, xprev, xnext)

    return pl.pallas_call(
        particles_kernel,
        grid=grid,
        in_specs=[SMEM, VMEM, vec, vec, flat, flat],
        out_specs=vec,
        out_shape=shape(3, slots, rows, cols, depth),
        scratch_shapes=[pltpu.VMEM((GROUPS, 6, 8, 128), F32)],
        name="particles",
    )(shift_codes[STEPS - 1 : STEPS], table, positions, thermal, offsets, occupancy)


def solution(mesh):
    in_specs = (
        P(None, None, "gx", "gy", None),
        P(None, None, "gx", "gy", None),
        P(None, None, "gx", "gy", None),
        P(None, "gx", "gy", None),
        P(None, "gx", "gy", None),
        P(),
    )
    out_specs = P(None, None, "gx", "gy", None)
    return jax.shard_map(local, mesh=mesh, in_specs=in_specs, out_specs=out_specs, check_vma=False)
```

profile of v0, /device:TPU:1, one launch (start us, length us, event | category | flops | bytes accessed | tf_op | source)
XLA Modules:
  0.0 97.1 jit_solution(2012560250497997445)
XLA Ops:
  0.0 1.4 %fusion = (s32[1]{0:T(128)}, s32[1]{0:T(128)}) fusion(s32[3]{0:T(128)} %param.11), kind=kLoop, calls=%fused_computation | loop fusion | bytes 16 | tf_op jit(solution)/shard_map/slice | solution.py:366
  1.4 7.2 %first_sums.1 = (f32[8,10,2,16,256]{4,3,2,1,0:T(8,128)}, f32[8,6,2,16,256]{4,3,2,1,0:T(8,128)}) custom-call(f32[3,12,2,16,256]{4,3,2,1,0:T(8,128)} %pos.5, f32[3,12,2,16,256]{4,3,2,1,0:T(8,128)} %vel.1, f32[3,12,2,16,256]{4,3,2,1,0:T(8,128)} %thermal.5, s32[12,2,16,256]{3,2,1,0:T(8,128)} %offsets.5, s32[12,2,16,256]{3,2,1,0:T(8,128)} %occupancy.5), custom_call_target="tpu_custom_call" | custom-call | tf_op jit(solution)/shard_map/first_sums/pallas_call | solution.py:339
  8.6 4.2 %expand.1 = (f32[17,16,256]{2,1,0:T(8,128)}, f32[17,16,256]{2,1,0:T(8,128)}, f32[17,16,256]{2,1,0:T(8,128)}, f32[3,16,256]{2,1,0:T(8,128)}, f32[3,16,256]{2,1,0:T(8,128)}) custom-call(s32[1]{0:T(128)} %get-tuple-element.55.codes, f32[8,10,2,16,256]{4,3,2,1,0:T(8,128)} %get-tuple-element.30.geo, f32[8,6,2,16,256]{4,3,2,1,0:T(8,128)} %get-tuple-element.33.wsum), custom_call_target="tpu_custom_call" | custom-call | tf_op jit(solution)/shard_map/expand/pallas_call | solution.py:359
  12.8 2.1 %collective-permute-start = (f32[3,16,256]{2,1,0:T(8,128)}, f32[3,16,256]{2,1,0:T(8,128)S(1)}, u32[]{:S(2)}, u32[]{:S(2)}) collective-permute-start(f32[3,16,256]{2,1,0:T(8,128)} %get-tuple-element.36), channel_id=1, source_target_pairs={{0,1},{1,2},{2,3},{3,4},{4,5},{5,6},{6,7},{7,0},{8,9},{9,10},{10,1... | collective-permute-start | bytes 147464 | tf_op jit(solution)/shard_map/ppermute | solution.py:374
  14.9 2.4 %collective-permute-start.1 = (f32[3,16,256]{2,1,0:T(8,128)}, f32[3,16,256]{2,1,0:T(8,128)S(1)}, u32[]{:S(2)}, u32[]{:S(2)}) collective-permute-start(f32[3,16,256]{2,1,0:T(8,128)} %get-tuple-element.37), channel_id=1, source_target_pairs={{0,7},{1,0},{2,1},{3,2},{4,3},{5,4},{6,5},{7,6},{8,15},{9,8},{10,9... | collective-permute-start | bytes 147464 | tf_op jit(solution)/shard_map/ppermute | solution.py:375
  17.3 1.7 %collective-permute-done.yprev = f32[3,16,256]{2,1,0:T(8,128)S(1)} collective-permute-done((f32[3,16,256]{2,1,0:T(8,128)}, f32[3,16,256]{2,1,0:T(8,128)S(1)}, u32[]{:S(2)}, u32[]{:S(2)}) %collective-permute-start) | collective-permute-done | bytes 49184 | tf_op jit(solution)/shard_map/ppermute | solution.py:374
  19.0 0.6 copy-done.6
  19.6 1.9 %fold.3 = (f32[17,16,256]{2,1,0:T(8,128)}, f32[17,16,256]{2,1,0:T(8,128)}) custom-call(f32[17,16,256]{2,1,0:T(8,128)} %get-tuple-element.34.row0, f32[17,16,256]{2,1,0:T(8,128)} %get-tuple-element.35.row2, f32[3,16,256]{2,1,0:T(8,128)} %copy-done.6, f32[3,16,256]{2,1,0:T(8,128)} %copy-done.8), custom_call_target="tpu_custom_call" | custom-call | tf_op jit(solution)/shard_map/fold/pallas_call | solution.py:386
  21.5 4.4 %collective-permute-start.2 = (f32[17,16,256]{2,1,0:T(8,128)}, f32[17,16,256]{2,1,0:T(8,128)S(1)}, u32[]{:S(2)}, u32[]{:S(2)}) collective-permute-start(f32[17,16,256]{2,1,0:T(8,128)} %get-tuple-element.40.own2), channel_id=1, source_target_pairs={{0,8},{8,16},{16,24},{24,32},{32,40},{40,48},{48,56},{56,64},{64,7... | collective-permute-start | bytes 835592 | tf_op jit(solution)/shard_map/ppermute | solution.py:393
  25.9 6.1 %later_sums.1 = (f32[8,6,2,16,256]{4,3,2,1,0:T(8,128)}, f32[8,6,2,16,256]{4,3,2,1,0:T(8,128)}) custom-call(f32[3,12,2,16,256]{4,3,2,1,0:T(8,128)} %pos.5, f32[3,12,2,16,256]{4,3,2,1,0:T(8,128)} %thermal.5, s32[12,2,16,256]{3,2,1,0:T(8,128)} %offsets.5, s32[12,2,16,256]{3,2,1,0:T(8,128)} %occupancy.5), custom_call_target="tpu_custom_call" | custom-call | tf_op jit(solution)/shard_map/later_sums/pallas_call | solution.py:377
  32.5 4.0 %collective-permute-done.3.xnext = f32[17,16,256]{2,1,0:T(8,128)S(1)} collective-permute-done((f32[17,16,256]{2,1,0:T(8,128)}, f32[17,16,256]{2,1,0:T(8,128)S(1)}, u32[]{:S(2)}, u32[]{:S(2)}) %collective-permute-start.3) | collective-permute-done | bytes 278560 | tf_op jit(solution)/shard_map/ppermute | solution.py:394
  36.6 0.7 copy-done.2
  37.2 5.3 %step.2 = (f32[17,16,256]{2,1,0:T(8,128)}, f32[17,16,256]{2,1,0:T(8,128)}, f32[17,16,256]{2,1,0:T(8,128)}, f32[3,16,256]{2,1,0:T(8,128)}, f32[3,16,256]{2,1,0:T(8,128)}) custom-call(s32[2]{0:T(128)} %get-tuple-element.57.codes, f32[8,10,2,16,256]{4,3,2,1,0:T(8,128)} %get-tuple-element.30.geo, f32[8,6,2,16,256]{4,3,2,1,0:T(8,128)} %get-tuple-element.32.dsum, ...), custom_call_target="tpu_custom_call" | custom-call | tf_op jit(solution)/shard_map/step/pallas_call | solution.py:396
  42.5 0.6 collective-permute-start.4
  43.1 3.0 %collective-permute-start.5 = (f32[3,16,256]{2,1,0:T(8,128)}, f32[3,16,256]{2,1,0:T(8,128)S(1)}, u32[]{:S(2)}, u32[]{:S(2)}) collective-permute-start(f32[3,16,256]{2,1,0:T(8,128)} %get-tuple-element.44), channel_id=1, source_target_pairs={{0,7},{1,0},{2,1},{3,2},{4,3},{5,4},{6,5},{7,6},{8,15},{9,8},{10,9... | collective-permute-start | bytes 147464 | tf_op jit(solution)/shard_map/ppermute | solution.py:375
  46.1 1.7 %collective-permute-done.4.yprev = f32[3,16,256]{2,1,0:T(8,128)S(1)} collective-permute-done((f32[3,16,256]{2,1,0:T(8,128)}, f32[3,16,256]{2,1,0:T(8,128)S(1)}, u32[]{:S(2)}, u32[]{:S(2)}) %collective-permute-start.4) | collective-permute-done | bytes 49184 | tf_op jit(solution)/shard_map/ppermute | solution.py:374
  48.4 1.9 %fold.4 = (f32[17,16,256]{2,1,0:T(8,128)}, f32[17,16,256]{2,1,0:T(8,128)}) custom-call(f32[17,16,256]{2,1,0:T(8,128)} %get-tuple-element.41.row0, f32[17,16,256]{2,1,0:T(8,128)} %get-tuple-element.42.row2, f32[3,16,256]{2,1,0:T(8,128)} %copy-done.7, f32[3,16,256]{2,1,0:T(8,128)} %copy-done.9), custom_call_target="tpu_custom_call" | custom-call | tf_op jit(solution)/shard_map/fold/pallas_call | solution.py:386
  50.3 1.5 %collective-permute-start.6 = (f32[17,16,256]{2,1,0:T(8,128)}, f32[17,16,256]{2,1,0:T(8,128)S(1)}, u32[]{:S(2)}, u32[]{:S(2)}) collective-permute-start(f32[17,16,256]{2,1,0:T(8,128)} %get-tuple-element.47.own2), channel_id=1, source_target_pairs={{0,8},{8,16},{16,24},{24,32},{32,40},{40,48},{48,56},{56,64},{64,7... | collective-permute-start | bytes 835592 | tf_op jit(solution)/shard_map/ppermute | solution.py:393
  52.0 3.6 %collective-permute-done.6.xprev = f32[17,16,256]{2,1,0:T(8,128)S(1)} collective-permute-done((f32[17,16,256]{2,1,0:T(8,128)}, f32[17,16,256]{2,1,0:T(8,128)S(1)}, u32[]{:S(2)}, u32[]{:S(2)}) %collective-permute-start.6) | collective-permute-done | bytes 278560 | tf_op jit(solution)/shard_map/ppermute | solution.py:393
  55.6 6.9 %collective-permute-done.7.xnext = f32[17,16,256]{2,1,0:T(8,128)S(1)} collective-permute-done((f32[17,16,256]{2,1,0:T(8,128)}, f32[17,16,256]{2,1,0:T(8,128)S(1)}, u32[]{:S(2)}, u32[]{:S(2)}) %collective-permute-start.7) | collective-permute-done | bytes 278560 | tf_op jit(solution)/shard_map/ppermute | solution.py:394
  62.4 0.7 copy-done.3
  63.2 5.3 %step.3 = (f32[17,16,256]{2,1,0:T(8,128)}, f32[17,16,256]{2,1,0:T(8,128)}, f32[17,16,256]{2,1,0:T(8,128)}, f32[3,16,256]{2,1,0:T(8,128)}, f32[3,16,256]{2,1,0:T(8,128)}) custom-call(s32[2]{0:T(128)} %get-tuple-element.58.codes, f32[8,10,2,16,256]{4,3,2,1,0:T(8,128)} %get-tuple-element.30.geo, f32[8,6,2,16,256]{4,3,2,1,0:T(8,128)} %get-tuple-element.31.dsum, ...), custom_call_target="tpu_custom_call" | custom-call | tf_op jit(solution)/shard_map/step/pallas_call | solution.py:396
  68.7 3.3 %collective-permute-start.9 = (f32[3,16,256]{2,1,0:T(8,128)}, f32[3,16,256]{2,1,0:T(8,128)S(1)}, u32[]{:S(2)}, u32[]{:S(2)}) collective-permute-start(f32[3,16,256]{2,1,0:T(8,128)} %get-tuple-element.51), channel_id=1, source_target_pairs={{0,7},{1,0},{2,1},{3,2},{4,3},{5,4},{6,5},{7,6},{8,15},{9,8},{10,9... | collective-permute-start | bytes 147464 | tf_op jit(solution)/shard_map/ppermute | solution.py:375
  72.0 2.5 %collective-permute-done.8.yprev = f32[3,16,256]{2,1,0:T(8,128)S(1)} collective-permute-done((f32[3,16,256]{2,1,0:T(8,128)}, f32[3,16,256]{2,1,0:T(8,128)S(1)}, u32[]{:S(2)}, u32[]{:S(2)}) %collective-permute-start.8) | collective-permute-done | bytes 49184 | tf_op jit(solution)/shard_map/ppermute | solution.py:374
  74.5 0.6 copy-done.10
  75.1 1.9 %fold.5 = (f32[17,16,256]{2,1,0:T(8,128)}, f32[17,16,256]{2,1,0:T(8,128)}) custom-call(f32[17,16,256]{2,1,0:T(8,128)} %get-tuple-element.48.row0, f32[17,16,256]{2,1,0:T(8,128)} %get-tuple-element.49.row2, f32[3,16,256]{2,1,0:T(8,128)} %copy-done.10, f32[3,16,256]{2,1,0:T(8,128)} %copy-done.11), custom_call_target="tpu_custom_call" | custom-call | tf_op jit(solution)/shard_map/fold/pallas_call | solution.py:386
  77.0 0.7 collective-permute-start.10
  77.7 6.8 %collective-permute-done.10.xprev = f32[17,16,256]{2,1,0:T(8,128)S(1)} collective-permute-done((f32[17,16,256]{2,1,0:T(8,128)}, f32[17,16,256]{2,1,0:T(8,128)S(1)}, u32[]{:S(2)}, u32[]{:S(2)}) %collective-permute-start.10) | collective-permute-done | bytes 278560 | tf_op jit(solution)/shard_map/ppermute | solution.py:393
  84.5 3.9 %collective-permute-done.11.xnext = f32[17,16,256]{2,1,0:T(8,128)S(1)} collective-permute-done((f32[17,16,256]{2,1,0:T(8,128)}, f32[17,16,256]{2,1,0:T(8,128)S(1)}, u32[]{:S(2)}, u32[]{:S(2)}) %collective-permute-start.11) | collective-permute-done | bytes 278560 | tf_op jit(solution)/shard_map/ppermute | solution.py:394
  88.4 0.7 copy-done.5
  89.1 2.6 %last.1.table = f32[2,6,3,24,256]{4,3,2,1,0:T(8,128)} custom-call(f32[17,16,256]{2,1,0:T(8,128)} %get-tuple-element.52.own0, f32[17,16,256]{2,1,0:T(8,128)} %get-tuple-element.53.mid, f32[17,16,256]{2,1,0:T(8,128)} %get-tuple-element.54.own2, f32[3,16,256]{2,1,0:T(8,128)} %copy-done.10, f32[3,16,256]{2,1,0:T(8,128)} %copy-done.11, f32[17,16,256]{2,1,0:T(8,128)} %copy-done.4, ...), custom_call_target="tpu_custom_call" | custom-call | tf_op jit(solution)/shard_map/last/pallas_call | solution.py:405
  91.7 5.4 %particles.1 = f32[3,12,2,16,256]{4,3,2,1,0:T(8,128)} custom-call(s32[1]{0:T(128)} %get-tuple-element.56.codes, f32[2,6,3,24,256]{4,3,2,1,0:T(8,128)} %last.1.table, f32[3,12,2,16,256]{4,3,2,1,0:T(8,128)} %pos.5, f32[3,12,2,16,256]{4,3,2,1,0:T(8,128)} %thermal.5, s32[12,2,16,256]{3,2,1,0:T(8,128)} %offsets.5, s32[12,2,16,256]{3,2,1,0:T(8,128)} %occupancy.5), custom_call_target="tpu_custom_call" | custom-call | tf_op jit(solution)/shard_map/particles/pallas_call | solution.py:414
  (30 shorter events, 1.8 us)
Async XLA Ops:
  12.8 6.2 %collective-permute-start = (f32[3,16,256]{2,1,0:T(8,128)}, f32[3,16,256]{2,1,0:T(8,128)S(1)}, u32[]{:S(2)}, u32[]{:S(2)}) collective-permute-start(f32[3,16,256]{2,1,0:T(8,128)} %get-tuple-element.36), channel_id=1, source_target_pairs={{0,1},{1,2},{2,3},{3,4},{4,5},{5,6},{6,7},{7,0},{8,9},{9,10},{10,1... | collective-permute-start | bytes 147464 | tf_op jit(solution)/shard_map/ppermute | solution.py:374
  14.9 4.1 %collective-permute-start.1 = (f32[3,16,256]{2,1,0:T(8,128)}, f32[3,16,256]{2,1,0:T(8,128)S(1)}, u32[]{:S(2)}, u32[]{:S(2)}) collective-permute-start(f32[3,16,256]{2,1,0:T(8,128)} %get-tuple-element.37), channel_id=1, source_target_pairs={{0,7},{1,0},{2,1},{3,2},{4,3},{5,4},{6,5},{7,6},{8,15},{9,8},{10,9... | collective-permute-start | bytes 147464 | tf_op jit(solution)/shard_map/ppermute | solution.py:375
  19.0 0.6 copy-start.6
  19.0 0.6 copy-start.8
  21.5 11.0 %collective-permute-start.2 = (f32[17,16,256]{2,1,0:T(8,128)}, f32[17,16,256]{2,1,0:T(8,128)S(1)}, u32[]{:S(2)}, u32[]{:S(2)}) collective-permute-start(f32[17,16,256]{2,1,0:T(8,128)} %get-tuple-element.40.own2), channel_id=1, source_target_pairs={{0,8},{8,16},{16,24},{24,32},{32,40},{40,48},{48,56},{56,64},{64,7... | collective-permute-start | bytes 835592 | tf_op jit(solution)/shard_map/ppermute | solution.py:393
  25.9 6.1 %copy-start.12 = (s32[3]{0:T(128)S(1)}, s32[3]{0:T(128)}, u32[]{:S(2)}) copy-start(s32[3]{0:T(128)} %param.11) | copy-start | bytes 40
  25.9 10.7 %collective-permute-start.3 = (f32[17,16,256]{2,1,0:T(8,128)}, f32[17,16,256]{2,1,0:T(8,128)S(1)}, u32[]{:S(2)}, u32[]{:S(2)}) collective-permute-start(f32[17,16,256]{2,1,0:T(8,128)} %get-tuple-element.38.own0), channel_id=1, source_target_pairs={{0,248},{8,0},{16,8},{24,16},{32,24},{40,32},{48,40},{56,48},{64,5... | collective-permute-start | bytes 835592 | tf_op jit(solution)/shard_map/ppermute | solution.py:394
  32.5 4.0 %copy-start = (f32[17,16,256]{2,1,0:T(8,128)}, f32[17,16,256]{2,1,0:T(8,128)S(1)}, u32[]{:S(2)}) copy-start(f32[17,16,256]{2,1,0:T(8,128)S(1)} %collective-permute-done.2.xprev) | copy-start | bytes 835588
  36.5 0.7 copy-start.2
  42.5 5.3 %collective-permute-start.4 = (f32[3,16,256]{2,1,0:T(8,128)}, f32[3,16,256]{2,1,0:T(8,128)S(1)}, u32[]{:S(2)}, u32[]{:S(2)}) collective-permute-start(f32[3,16,256]{2,1,0:T(8,128)} %get-tuple-element.43), channel_id=1, source_target_pairs={{0,1},{1,2},{2,3},{3,4},{4,5},{5,6},{6,7},{7,0},{8,9},{9,10},{10,1... | collective-permute-start | bytes 147464 | tf_op jit(solution)/shard_map/ppermute | solution.py:374
  43.1 4.6 %collective-permute-start.5 = (f32[3,16,256]{2,1,0:T(8,128)}, f32[3,16,256]{2,1,0:T(8,128)S(1)}, u32[]{:S(2)}, u32[]{:S(2)}) collective-permute-start(f32[3,16,256]{2,1,0:T(8,128)} %get-tuple-element.44), channel_id=1, source_target_pairs={{0,7},{1,0},{2,1},{3,2},{4,3},{5,4},{6,5},{7,6},{8,15},{9,8},{10,9... | collective-permute-start | bytes 147464 | tf_op jit(solution)/shard_map/ppermute | solution.py:375
  47.8 0.6 copy-start.7
  47.8 0.6 copy-start.9
  50.3 5.3 %collective-permute-start.6 = (f32[17,16,256]{2,1,0:T(8,128)}, f32[17,16,256]{2,1,0:T(8,128)S(1)}, u32[]{:S(2)}, u32[]{:S(2)}) collective-permute-start(f32[17,16,256]{2,1,0:T(8,128)} %get-tuple-element.47.own2), channel_id=1, source_target_pairs={{0,8},{8,16},{16,24},{24,32},{32,40},{40,48},{48,56},{56,64},{64,7... | collective-permute-start | bytes 835592 | tf_op jit(solution)/shard_map/ppermute | solution.py:393
  51.8 10.7 %collective-permute-start.7 = (f32[17,16,256]{2,1,0:T(8,128)}, f32[17,16,256]{2,1,0:T(8,128)S(1)}, u32[]{:S(2)}, u32[]{:S(2)}) collective-permute-start(f32[17,16,256]{2,1,0:T(8,128)} %get-tuple-element.45.own0), channel_id=1, source_target_pairs={{0,248},{8,0},{16,8},{24,16},{32,24},{40,32},{48,40},{56,48},{64,5... | collective-permute-start | bytes 835592 | tf_op jit(solution)/shard_map/ppermute | solution.py:394
  55.6 6.9 %copy-start.1 = (f32[17,16,256]{2,1,0:T(8,128)}, f32[17,16,256]{2,1,0:T(8,128)S(1)}, u32[]{:S(2)}) copy-start(f32[17,16,256]{2,1,0:T(8,128)S(1)} %collective-permute-done.6.xprev) | copy-start | bytes 835588
  62.4 0.7 copy-start.3
  68.4 6.0 %collective-permute-start.8 = (f32[3,16,256]{2,1,0:T(8,128)}, f32[3,16,256]{2,1,0:T(8,128)S(1)}, u32[]{:S(2)}, u32[]{:S(2)}) collective-permute-start(f32[3,16,256]{2,1,0:T(8,128)} %get-tuple-element.50), channel_id=1, source_target_pairs={{0,1},{1,2},{2,3},{3,4},{4,5},{5,6},{6,7},{7,0},{8,9},{9,10},{10,1... | collective-permute-start | bytes 147464 | tf_op jit(solution)/shard_map/ppermute | solution.py:374
  68.7 5.8 %collective-permute-start.9 = (f32[3,16,256]{2,1,0:T(8,128)}, f32[3,16,256]{2,1,0:T(8,128)S(1)}, u32[]{:S(2)}, u32[]{:S(2)}) collective-permute-start(f32[3,16,256]{2,1,0:T(8,128)} %get-tuple-element.51), channel_id=1, source_target_pairs={{0,7},{1,0},{2,1},{3,2},{4,3},{5,4},{6,5},{7,6},{8,15},{9,8},{10,9... | collective-permute-start | bytes 147464 | tf_op jit(solution)/shard_map/ppermute | solution.py:375
  74.5 0.6 copy-start.10
  74.5 0.6 copy-start.11
  77.0 7.5 %collective-permute-start.10 = (f32[17,16,256]{2,1,0:T(8,128)}, f32[17,16,256]{2,1,0:T(8,128)S(1)}, u32[]{:S(2)}, u32[]{:S(2)}) collective-permute-start(f32[17,16,256]{2,1,0:T(8,128)} %get-tuple-element.54.own2), channel_id=1, source_target_pairs={{0,8},{8,16},{16,24},{24,32},{32,40},{40,48},{48,56},{56,64},{64,7... | collective-permute-start | bytes 835592 | tf_op jit(solution)/shard_map/ppermute | solution.py:393
  77.7 10.7 %collective-permute-start.11 = (f32[17,16,256]{2,1,0:T(8,128)}, f32[17,16,256]{2,1,0:T(8,128)S(1)}, u32[]{:S(2)}, u32[]{:S(2)}) collective-permute-start(f32[17,16,256]{2,1,0:T(8,128)} %get-tuple-element.52.own0), channel_id=1, source_target_pairs={{0,248},{8,0},{16,8},{24,16},{32,24},{40,32},{48,40},{56,48},{64,5... | collective-permute-start | bytes 835592 | tf_op jit(solution)/shard_map/ppermute | solution.py:394
  84.5 3.9 %copy-start.4 = (f32[17,16,256]{2,1,0:T(8,128)}, f32[17,16,256]{2,1,0:T(8,128)S(1)}, u32[]{:S(2)}) copy-start(f32[17,16,256]{2,1,0:T(8,128)S(1)} %collective-permute-done.10.xprev) | copy-start | bytes 835588
  88.4 0.7 copy-start.5
where the time goes:
time: 97.6 us; the launch traced here: 97.1 us
  Pallas kernels  41.7 us (43%)
  waiting for transfers between devices  31 us (32%)
  starting transfers between devices  18.4 us (19%)
  local copies, waits for them, and re-layouts  6.04 us (6%)
    ppermute x3, waiting for transfers between devices, local(): xnext = lax.ppermute(own0, 'gx', ring('gx', -1))  14.7 us
    pallas_call x2, Pallas kernels, local(): pl.pallas_call(step_kernel, in_specs=[SMEM] + [VMEM] * 9, out_specs=[VMEM...  10.6 us
    ppermute x3, waiting for transfers between devices, local(): xprev = lax.ppermute(own2, 'gx', ring('gx', 1))  10.4 us
    ppermute x3, starting transfers between devices, local(): ynext = lax.ppermute(ydn, 'gy', ring('gy', -1))  8.63 us
    pallas_call x1, Pallas kernels, local(): pl.pallas_call(first_sums_kernel, grid=grid, in_specs=[vec, vec, vec, fla...  7.18 us
    ppermute x3, starting transfers between devices, local(): xprev = lax.ppermute(own2, 'gx', ring('gx', 1))  6.52 us
    pallas_call x1, Pallas kernels, local(): pl.pallas_call(later_sums_kernel, grid=grid, in_specs=[vec, vec, flat, fl...  6.05 us
    ppermute x3, waiting for transfers between devices, local(): yprev = lax.ppermute(yup, 'gy', ring('gy', 1))  5.84 us
  transfers between devices with their start and end apart: 12, of which 8 were waited for; matrix products, arithmetic and copies ran while one was open for 1% of the time, Pallas kernels for 6%

commit v1 on v0

v1 whole, which is shorter than its diff:
```python
import functools

import jax
import jax.numpy as jnp
from jax import lax
from jax.experimental import pallas as pl
from jax.experimental.pallas import tpu as pltpu
from jax.sharding import PartitionSpec as P


STEPS = 3
RIDGE = 0.5
GROUPS = 8
F32 = jnp.float32


def bits(code):
    return code // 4, code // 2 % 2, code % 2


def cross(u, v):
    return [
        u[1] * v[2] - u[2] * v[1],
        u[2] * v[0] - u[0] * v[2],
        u[0] * v[1] - u[1] * v[0],
    ]


def plus(terms):
    total = None
    for term in terms:
        total = term if total is None else total + term
    return total


def accumulate(value_ref, codes, groups, names, store):
    sums = [[None] * len(groups) for _ in names]
    for slot, code in enumerate(codes):
        masks = [code == group for group in groups]
        for at, name in enumerate(names):
            value = 1.0 if name is None else value_ref[name, slot]
            for g, mask in enumerate(masks):
                part = jnp.where(mask, value, 0.0)
                old = sums[at][g]
                sums[at][g] = part if old is None else old + part
    for at in range(len(names)):
        for g in range(len(groups)):
            store(at, g, sums[at][g])


def moments(p, w):
    seconds = [p[0] * p[0], p[1] * p[1], p[2] * p[2], p[0] * p[1], p[0] * p[2], p[1] * p[2]]
    return p + seconds + w + cross(p, w)


def chunk_sums(pos, rel, code, value, geo, wsum, groups, row, at, lanes):
    slots = code.shape[0]
    for slot in range(slots):
        p = [pos[c, slot, row, at, lanes] for c in range(3)]
        w = [rel[c, slot, row, at, lanes] for c in range(3)]
        for name, term in enumerate(moments(p, w)):
            value[name, slot] = term
    codes = [code[slot, row, at, lanes] for slot in range(slots)]

    def store_first(index, g, total):
        geo[groups[g], index, row, at, lanes] = total

    def store_second(index, g, total):
        if index < 2:
            geo[groups[g], 8 + index, row, at, lanes] = total
        else:
            wsum[groups[g], index - 2, row, at, lanes] = total

    accumulate(value, codes, groups, [None] + list(range(7)), store_first)
    accumulate(value, codes, groups, list(range(7, 15)), store_second)


def halves(depth):
    return [pl.ds(128 * half, 128) for half in range(depth // 128)]


def four(by, shift):
    return [(4 * bx + 2 * by + bz) ^ shift for bx in range(2) for bz in range(2)]


def near_sums_kernel(
    shifts_in, pos_in, vel_in, thermal_in, offsets_in, occupancy_in,
    pos, thermal, rel, code, geo, wsum, yup, ydn,
    vel, offsets, occupancy, value, ends, shifts, sems, shift_sem,
):
    slots, rows, cols, depth = code.shape
    pairs = [(pos_in, pos), (vel_in, vel), (thermal_in, thermal)]
    flats = [(offsets_in, offsets), (occupancy_in, occupancy)]
    chunks = [(row, tile) for row in range(rows) for tile in range(cols // 8)]
    shift_copy = pltpu.make_async_copy(shifts_in, shifts, shift_sem)
    shift_copy.start()
    copies = []
    for index, (row, tile) in enumerate(chunks):
        at = pl.ds(8 * tile, 8)
        group = []
        for source, target in pairs:
            group.append((source.at[:, :, row, at, :], target.at[:, :, row, at, :]))
        for source, target in flats:
            group.append((source.at[:, row, at, :], target.at[:, row, at, :]))
        copies.append(
            [pltpu.make_async_copy(*ends_, sems.at[index, n]) for n, ends_ in enumerate(group)]
        )
        for copy in copies[-1]:
            copy.start()
    shift_copy.wait()
    for index, (row, tile) in enumerate(chunks):
        at = pl.ds(8 * tile, 8)
        for copy in copies[index]:
            copy.wait()
        groups = four(1 if tile == 0 else 0, shifts[0])
        for lanes in halves(depth):
            for slot in range(slots):
                code[slot, row, at, lanes] = jnp.where(
                    occupancy[slot, row, at, lanes] == 1, offsets[slot, row, at, lanes], GROUPS
                )
                for c in range(3):
                    rel[c, slot, row, at, lanes] = (
                        vel[c, slot, row, at, lanes] - thermal[c, slot, row, at, lanes]
                    )
            chunk_sums(pos, rel, code, value, geo, wsum, groups, row, at, lanes)
    for out, by, col in ((yup, 0, cols - 1), (ydn, 1, 0)):
        for bz in range(2):
            for bx in range(2):
                frame = 4 * bx + 2 * by + bz
                o = frame ^ shifts[0]
                for row in range(rows):
                    own = geo_frame(geo, o, frame, row, pl.ds(col, 1))
                    own.update(vel_frame(wsum, o, frame, row, pl.ds(col, 1)))
                    for v in range(16):
                        if bx == 1 and row == 1:
                            ends[bz, 1, v : v + 1, :] += own[v]
                        else:
                            ends[bz, row + 1 - bx, v : v + 1, :] = own[v]
        for r in range(3):
            out[r] = ends[0, r] + roll(ends[1, r], -1)


def rest_sums_kernel(
    shifts, pos, rel, code, geo_near, wsum_near, geo, wsum, row0, row1, row2, value, part, shifted
):
    _, rows, cols, depth = code.shape
    for row in range(rows):
        for tile in range(cols // 8):
            at = pl.ds(8 * tile, 8)
            far = 0 if tile == 0 else 1
            for o in four(1 - far, shifts[0]):
                for v in range(10):
                    geo[o, v, row, at, :] = geo_near[o, v, row, at, :]
                for v in range(6):
                    wsum[o, v, row, at, :] = wsum_near[o, v, row, at, :]
            groups = four(far, shifts[0])
            for lanes in halves(depth):
                chunk_sums(pos, rel, code, value, geo, wsum, groups, row, at, lanes)
    outs = (row0, row1, row2)
    expand(lambda *where: geo_frame(geo, *where), GEO, shifts[0], outs, None, None, part, shifted)
    expand(lambda *where: vel_frame(wsum, *where), VEL, shifts[0], outs, None, None, part, shifted)


def change_sums_kernel(step, pos, thermal, code, dsum, value):
    slots, rows, cols, depth = code.shape
    tiles = cols // 8

    def chunk(index, carry):
        row = index // tiles
        at = pl.ds(pl.multiple_of(8 * (index % tiles), 8), 8)
        for lanes in halves(depth):
            for slot in range(slots):
                p = [pos[c, slot, row, at, lanes] for c in range(3)]
                d = [
                    thermal[c, (slot + step) % slots, row, at, lanes]
                    - thermal[c, (slot + step + 1) % slots, row, at, lanes]
                    for c in range(3)
                ]
                for name, term in enumerate(d + cross(p, d)):
                    value[name, slot] = term
            codes = [code[slot, row, at, lanes] for slot in range(slots)]
            for base in (0, 4):

                def store(index, g, total):
                    dsum[base + g, index, row, at, lanes] = total

                accumulate(value, codes, range(base, base + 4), list(range(6)), store)
        return carry

    lax.fori_loop(0, rows * tiles, chunk, 0)


def roll(value, amount):
    return pltpu.roll(value, amount % value.shape[-1], value.ndim - 1)


GEO = (0, 1, 2, 3, 10, 11, 12, 13, 14, 15)
VEL = (4, 5, 6, 7, 8, 9)


def geo_frame(geo, o, frame, row, at):
    b = bits(frame)
    n = geo[o, 0, row, at, :]
    s = [geo[o, 1 + c, row, at, :] for c in range(3)]
    q = [s[c] + n if b[c] else s[c] for c in range(3)]
    out = {0: n, 1: q[0], 2: q[1], 3: q[2]}
    for k, (i, j) in enumerate(((0, 0), (1, 1), (2, 2), (0, 1), (0, 2), (1, 2))):
        value = geo[o, 4 + k, row, at, :]
        if b[i]:
            value = value + s[j]
        if b[j]:
            value = value + q[i]
        out[10 + k] = value
    return out


def vel_frame(wsum, o, frame, row, at):
    bx, by, bz = bits(frame)
    w = [wsum[o, c, row, at, :] for c in range(3)]
    l = [wsum[o, 3 + c, row, at, :] for c in range(3)]
    if bx:
        l = [l[0], l[1] - w[2], l[2] + w[1]]
    if by:
        l = [l[0] + w[2], l[1], l[2] - w[0]]
    if bz:
        l = [l[0] - w[1], l[1] + w[0], l[2]]
    return dict(zip(VEL, w + l))


def expand(frame_of, names, shift, rows, yup, ydn, part, shifted):
    cols = rows[0].shape[1]
    every = pl.ds(0, cols)
    for by in range(2):
        for bz in range(2):
            for bx in range(2):
                frame = 4 * bx + 2 * by + bz
                for row in range(2):
                    values = frame_of(frame ^ shift, frame, row, every)
                    for v in names:
                        if bx == 1 and row == 1:
                            part[by, bz, 1, v] += values[v]
                        else:
                            part[by, bz, row + 1 - bx, v] = values[v]
    for r in range(3):
        for v in names:
            near = part[0, 0, r, v] + roll(part[0, 1, r, v], -1)
            beyond = part[1, 0, r, v] + roll(part[1, 1, r, v], -1)
            shifted[r, v, cols:, :] = jnp.zeros((8, beyond.shape[1]), F32)
            shifted[r, v, :cols, :] = beyond
            main = near + shifted[r, v, 1 : cols + 1, :]
            rows[r][v] = main
            rows[r][16, v : v + 1, :] = beyond[0:1]
            if yup is not None:
                yup[r, v : v + 1, :] = main[cols - 1 : cols]
                ydn[r, v : v + 1, :] = beyond[0:1]


def geometry_kernel(step, shifts, geo, row0, row1, row2, yup, ydn, part, shifted):
    outs = (row0, row1, row2)
    expand(
        lambda *where: geo_frame(geo, *where), GEO, shifts[step], outs, yup, ydn, part, shifted
    )


def corner_kernel(yprev, ynext, low, high):
    for out, r in ((low, 0), (high, 2)):
        out[0] = yprev[r]
        out[1] = ynext[r]


def complete_row(row, ends, out):
    last = out.shape[1] - 1
    for v in range(16):
        out[v] = plus([part[v] for part in row])
    out[16] = plus([part[16] for part in row] + [low for low, _ in ends])
    add = plus([high for _, high in ends])
    for v in range(16):
        out[v, last : last + 1, :] += add[v : v + 1]


def solve(sums):
    inverse = 1.0 / jnp.maximum(sums[0], 1.0)
    first = sums[1:4]
    flow = sums[4:7]
    centre = [value * inverse for value in first]
    drift = [value * inverse for value in flow]
    moment = cross(centre, flow)
    torque = [sums[7 + c] - moment[c] for c in range(3)]
    mxx = sums[10] - first[0] * centre[0]
    myy = sums[11] - first[1] * centre[1]
    mzz = sums[12] - first[2] * centre[2]
    kxy = first[0] * centre[1] - sums[13]
    kxz = first[0] * centre[2] - sums[14]
    kyz = first[1] * centre[2] - sums[15]
    kxx = myy + mzz + RIDGE
    kyy = mxx + mzz + RIDGE
    kzz = mxx + myy + RIDGE
    adj_xx = kyy * kzz - kyz * kyz
    adj_yy = kxx * kzz - kxz * kxz
    adj_zz = kxx * kyy - kxy * kxy
    adj_xy = kxz * kyz - kxy * kzz
    adj_xz = kxy * kyz - kxz * kyy
    adj_yz = kxy * kxz - kxx * kyz
    scale = 1.0 / (kxx * adj_xx + kxy * adj_xy + kxz * adj_xz)
    spin = [
        (adj_xx * torque[0] + adj_xy * torque[1] + adj_xz * torque[2]) * scale,
        (adj_xy * torque[0] + adj_yy * torque[1] + adj_yz * torque[2]) * scale,
        (adj_xz * torque[0] + adj_yz * torque[1] + adj_zz * torque[2]) * scale,
    ]
    turned = cross(spin, centre)
    return [drift[c] - turned[c] for c in range(3)] + spin


def fill_table(own, around, table, total):
    yprev, ynext, xprev, xnext, cprev, cnext = around
    cols = own[0].shape[1]
    for r in range(3):
        row, ends = [own[r]], [(yprev[r], ynext[r])]
        if r != 1:
            row.append(xprev if r == 0 else xnext)
            corner = cprev if r == 0 else cnext
            ends.append((corner[0], corner[1]))
        complete_row(row, ends, total)
        for t in range(cols // 8):
            at = pl.ds(8 * t, 8)
            state = solve([total[v, at, :] for v in range(16)])
            for v in range(6):
                table[0, v, r, 8 + 8 * t : 16 + 8 * t, :] = state[v]
                table[1, v, r, 8 + 8 * t : 16 + 8 * t, :] = roll(state[v], 1)
        state = solve([total[16, v : v + 1, :] for v in range(16)])
        for v in range(6):
            wide = jnp.broadcast_to(state[v], (8, state[v].shape[1]))
            table[0, v, r, 0:8, :] = wide
            table[1, v, r, 0:8, :] = roll(wide, 1)


def shift_a(a, spin, b):
    a = list(a)
    if b[0]:
        a = [a[0], a[1] + spin[2], a[2] - spin[1]]
    if b[1]:
        a = [a[0] - spin[2], a[1], a[2] + spin[0]]
    if b[2]:
        a = [a[0] + spin[1], a[1] - spin[0], a[2]]
    return a


def update_groups(geo, dsum, shift, table, wsum):
    cols = geo.shape[3]
    for code in range(GROUPS):
        bx, by, bz = bits(code)
        o = code ^ shift
        for row in range(2):
            for t in range(cols // 8):
                at = pl.ds(8 * t, 8)
                from_col = 8 + 8 * t - by
                values = [table[bz, v, row + 1 - bx, from_col : from_col + 8, :] for v in range(6)]
                spin = values[3:]
                a = shift_a(values[:3], spin, (bx, by, bz))
                n = geo[o, 0, row, at, :]
                s = [geo[o, 1 + c, row, at, :] for c in range(3)]
                xx, yy, zz, xy, xz, yz = [geo[o, 4 + c, row, at, :] for c in range(6)]
                turn = cross(spin, s)
                arm = cross(s, a)
                own = [
                    (yy + zz) * spin[0] - xy * spin[1] - xz * spin[2],
                    (xx + zz) * spin[1] - xy * spin[0] - yz * spin[2],
                    (xx + yy) * spin[2] - xz * spin[0] - yz * spin[1],
                ]
                for c in range(3):
                    wsum[o, c, row, at, :] = dsum[o, c, row, at, :] + n * a[c] + turn[c]
                    wsum[o, 3 + c, row, at, :] = dsum[o, 3 + c, row, at, :] + arm[c] + own[c]


def step_kernel(
    step, shifts, geo, dsum, own0, own1, own2, yprev, ynext, xprev, xnext, cprev, cnext,
    geo0, geo1, geo2, geoup, geodn,
    row0, row1, row2, yup, ydn, total, table, wsum, part, shifted,
):
    fill_table((own0, own1, own2), (yprev, ynext, xprev, xnext, cprev, cnext), table, total)
    update_groups(geo, dsum, shifts[step], table, wsum)
    rows = (row0, row1, row2)
    for target, source in zip(rows, (geo0, geo1, geo2)):
        for v in GEO:
            target[v] = source[v]
        target[16] = source[16]
    yup[...] = geoup[...]
    ydn[...] = geodn[...]
    expand(lambda *where: vel_frame(wsum, *where), VEL, shifts[step + 1], rows, yup, ydn, part, shifted)


def last_kernel(own0, own1, own2, yprev, ynext, xprev, xnext, cprev, cnext, table, total):
    fill_table((own0, own1, own2), (yprev, ynext, xprev, xnext, cprev, cnext), table, total)


def particles_kernel(shifts, table, pos, thermal, code, out, variants):
    slots = code.shape[0]
    row = pl.program_id(0)
    tile = pl.program_id(1)
    for half in range(pos.shape[4] // 128):
        lanes = pl.ds(half * 128, 128)
        for frame in range(GROUPS):
            bx, by, bz = bits(frame)
            values = [
                table[bz, v, row + 1 - bx, pl.ds(8 * tile, 16), lanes][8 - by : 16 - by]
                for v in range(6)
            ]
            values[:3] = shift_a(values[:3], values[3:], (bx, by, bz))
            for v in range(6):
                variants[frame, v] = values[v]
        for slot in range(slots):
            base = code[slot, 0, :, lanes]
            k = base ^ shifts[STEPS - 1]
            isx, isy, isz = (k & 4) != 0, (k & 2) != 0, (k & 1) != 0
            used = base < GROUPS
            state = []
            for v in range(6):
                level = [jnp.where(isx, variants[4 + i, v], variants[i, v]) for i in range(4)]
                level = [jnp.where(isy, level[2 + i], level[i]) for i in range(2)]
                state.append(jnp.where(isz, level[1], level[0]))
            p = [pos[c, slot, 0, :, lanes] for c in range(3)]
            turn = cross(state[3:], p)
            for c in range(3):
                fresh = thermal[c, (slot + STEPS - 1) % slots, 0, :, lanes] + (state[c] + turn[c])
                out[c, slot, 0, :, lanes] = jnp.where(used, fresh, 0.0)


VMEM = pl.BlockSpec(memory_space=pltpu.VMEM)
SMEM = pl.BlockSpec(memory_space=pltpu.SMEM)
HBM = pl.BlockSpec(memory_space=pltpu.HBM)


def in_hbm(value):
    return pltpu.with_memory_space_constraint(value, pltpu.HBM)


def params(mib):
    return pltpu.CompilerParams(vmem_limit_bytes=mib * 2**20)


def shape(*dims):
    return jax.ShapeDtypeStruct(dims, F32)


def big_spec(lead):
    return pl.BlockSpec((*lead, 1, 8, 256), lambda r, t: (*([0] * len(lead)), r, t, 0))


def local(positions, velocities, thermal, offsets, occupancy, shift_codes):
    slots, rows, cols, depth = offsets.shape
    grid = (rows, cols // 8)
    vec = big_spec((3, slots))
    flat = big_spec((slots,))
    group = lambda count: pltpu.VMEM((GROUPS, count, rows, cols, depth), F32)
    group_shape = lambda count: shape(GROUPS, count, rows, cols, depth)
    value = lambda count: pltpu.VMEM((count, slots, 8, 128), F32)
    vec_shape = shape(3, slots, rows, cols, depth)
    flat_shape = jax.ShapeDtypeStruct((slots, rows, cols, depth), jnp.int32)
    row_shape = shape(17, cols, depth)
    col_shape = shape(3, 16, depth)
    expand_out = [row_shape] * 3 + [col_shape] * 2
    expand_scratch = [
        pltpu.VMEM((2, 2, 3, 16, cols, depth), F32),
        pltpu.VMEM((3, 16, cols + 8, depth), F32),
    ]
    total = pltpu.VMEM((17, cols, depth), F32)
    table_shape = (2, 6, 3, cols + 8, depth)

    pos, hot, rel, code, geo_near, wsum_near, yup, ydn = pl.pallas_call(
        near_sums_kernel,
        in_specs=[HBM] * 6,
        out_specs=[VMEM] * 8,
        out_shape=[vec_shape] * 3 + [flat_shape, group_shape(10), group_shape(6)] + [col_shape] * 2,
        scratch_shapes=[
            pltpu.VMEM(vec_shape.shape, F32),
            pltpu.VMEM(flat_shape.shape, jnp.int32),
            pltpu.VMEM(flat_shape.shape, jnp.int32),
            value(15),
            pltpu.VMEM((2, 3, 16, depth), F32),
            pltpu.SMEM((STEPS,), jnp.int32),
            pltpu.SemaphoreType.DMA((rows * cols // 8, 5)),
            pltpu.SemaphoreType.DMA,
        ],
        compiler_params=params(16),
        name="near_sums",
    )(*map(in_hbm, (shift_codes, positions, velocities, thermal, offsets, occupancy)))

    def ring(axis, by):
        count = lax.axis_size(axis)
        return [(i, (i + by) % count) for i in range(count)]

    def change_sums(step):
        return pl.pallas_call(
            functools.partial(change_sums_kernel, step),
            in_specs=[VMEM] * 3,
            out_specs=VMEM,
            out_shape=group_shape(6),
            scratch_shapes=[value(6)],
            compiler_params=params(8),
            name="change_sums",
        )(pos, hot, code)

    def geometry(step):
        return pl.pallas_call(
            functools.partial(geometry_kernel, step),
            in_specs=[SMEM, VMEM],
            out_specs=[VMEM] * 5,
            out_shape=expand_out,
            scratch_shapes=expand_scratch,
            compiler_params=params(12),
            name="geometry",
        )(shift_codes, geo)

    def send(value, axis, by):
        return lax.ppermute(value, axis, ring(axis, by))

    for step in range(STEPS):
        yprev = send(yup, "gy", 1)
        ynext = send(ydn, "gy", -1)
        if step == 0:
            geo, _, row0, row1, row2 = pl.pallas_call(
                rest_sums_kernel,
                in_specs=[SMEM] + [VMEM] * 5,
                out_specs=[VMEM] * 5,
                out_shape=[group_shape(10), group_shape(6)] + [row_shape] * 3,
                scratch_shapes=[value(15)] + expand_scratch,
                compiler_params=params(16),
                name="rest_sums",
            )(shift_codes, pos, rel, code, geo_near, wsum_near)
        xprev = send(row2, "gx", 1)
        xnext = send(row0, "gx", -1)
        low, high = pl.pallas_call(
            corner_kernel,
            in_specs=[VMEM] * 2,
            out_specs=[VMEM] * 2,
            out_shape=[shape(2, 16, depth)] * 2,
            compiler_params=params(2),
            name="corners",
        )(yprev, ynext)
        cprev = send(high, "gx", 1)
        cnext = send(low, "gx", -1)
        found = (row0, row1, row2, yprev, ynext, xprev, xnext, cprev, cnext)
        if step + 1 < STEPS:
            dsum = change_sums(step)
            ahead = geometry(step + 1)
            row0, row1, row2, yup, ydn = pl.pallas_call(
                functools.partial(step_kernel, step),
                in_specs=[SMEM] + [VMEM] * 16,
                out_specs=[VMEM] * 5,
                out_shape=expand_out,
                scratch_shapes=[total, pltpu.VMEM(table_shape, F32), group(6)] + expand_scratch,
                compiler_params=params(16),
                name="step",
            )(shift_codes, geo, dsum, *found, *ahead)

    table = pl.pallas_call(
        last_kernel,
        in_specs=[VMEM] * 9,
        out_specs=VMEM,
        out_shape=shape(*table_shape),
        scratch_shapes=[total],
        compiler_params=params(6),
        name="last",
    )(*found)

    return pl.pallas_call(
        particles_kernel,
        grid=grid,
        in_specs=[SMEM, VMEM, vec, vec, flat],
        out_specs=vec,
        out_shape=vec_shape,
        scratch_shapes=[pltpu.VMEM((GROUPS, 6, 8, 128), F32)],
        compiler_params=params(12),
        name="particles",
    )(shift_codes, table, pos, hot, code)


def solution(mesh):
    in_specs = (
        P(None, None, "gx", "gy", None),
        P(None, None, "gx", "gy", None),
        P(None, None, "gx", "gy", None),
        P(None, "gx", "gy", None),
        P(None, "gx", "gy", None),
        P(),
    )
    out_specs = P(None, None, "gx", "gy", None)
    return jax.shard_map(local, mesh=mesh, in_specs=in_specs, out_specs=out_specs, check_vma=False)
```

time: 97.6 us -> 77.3 us (0.79)
  the two profiles are of different devices: /device:TPU:1 before, /device:TPU:26 now
where the time goes in v1:
time: 77.3 us; the launch traced here: 77.2 us
  starting transfers between devices  37.3 us (48%)
  Pallas kernels  22 us (28%)
  waiting for transfers between devices  17.7 us (23%)
    ppermute x18, starting transfers between devices, send(): return lax.ppermute(value, axis, ring(axis, by))  37.3 us
    ppermute x18, waiting for transfers between devices, send(): return lax.ppermute(value, axis, ring(axis, by))  17.7 us
    pallas_call x1, Pallas kernels, local(): pl.pallas_call(rest_sums_kernel, in_specs=[SMEM] + [VMEM] * 5, out_specs=...  4.68 us
    pallas_call x2, Pallas kernels, local(): pl.pallas_call(functools.partial(step_kernel, step), in_specs=[SMEM] + [V...  4.27 us
    pallas_call x1, Pallas kernels, local(): pl.pallas_call(near_sums_kernel, in_specs=[HBM] * 6, out_specs=[VMEM] * 8...  3.94 us
    pallas_call x2, Pallas kernels, change_sums(): pl.pallas_call(functools.partial(change_sums_kernel, step), in_specs=[VME...  3.81 us
    pallas_call x1, Pallas kernels, local(): pl.pallas_call(particles_kernel, grid=grid, in_specs=[SMEM, VMEM, vec, ve...  2.99 us
    pallas_call x2, Pallas kernels, geometry(): pl.pallas_call(functools.partial(geometry_kernel, step), in_specs=[SMEM,...  1.89 us
  transfers between devices with their start and end apart: 18, of which 7 were waited for; matrix products, arithmetic and copies ran while one was open for 0% of the time, Pallas kernels for 7%

profile of v1, /device:TPU:26, one launch (start us, length us, event | category | flops | bytes accessed | tf_op | source)
XLA Modules:
  0.0 77.2 jit_solution(1948633924992692741)
XLA Ops:
  0.0 3.9 %near_sums.1 = (f32[3,12,2,16,256]{4,3,2,1,0:T(8,128)S(1)}, f32[3,12,2,16,256]{4,3,2,1,0:T(8,128)S(1)}, f32[3,12,2,16,256]{4,3,2,1,0:T(8,128)S(1)}, s32[12,2,16,...) custom-call(s32[3]{0:T(128)} %shifts.11, ...), custom_call_target="tpu_custom_call" | custom-call | tf_op jit(solution)/shard_map/near_sums/pallas_call | solution.py:469
  4.0 4.7 %rest_sums.1 = (f32[8,10,2,16,256]{4,3,2,1,0:T(8,128)S(1)}, f32[8,6,2,16,256]{4,3,2,1,0:T(8,128)}, f32[17,16,256]{2,1,0:T(8,128)S(1)}, f32[17,16,256]{2,1,0:T(8,128)S(1)}, f32[17,16,256]{2,1,0:T(8,128)S(1)}) custom-call(s32[3]{0:T(128)S(1)} %copy-done, f32[3,12,2,16,256]{4,3,2,1,0:T(8,128)S(1)} %get-tuple-element.43.pos, ...), custom_call_target="tpu_custom_call" | custom-call | tf_op jit(solution)/shard_map/rest_sums/pallas_call | solution.py:521
  8.6 6.9 %collective-permute-start.3 = (f32[17,16,256]{2,1,0:T(8,128)S(1)}, f32[17,16,256]{2,1,0:T(8,128)S(1)}, u32[]{:S(2)}, u32[]{:S(2)}) collective-permute-start(f32[17,16,256]{2,1,0:T(8,128)S(1)} %get-tuple-element.50.own0), channel_id=1, source_target_pairs={{0,248},{8,0},{16,8},{24,16},{32,24},{40,32},{48,40},{56,48},{64,5... | collective-permute-start | bytes 835592 | tf_op jit(solution)/shard_map/ppermute | solution.py:515
  15.5 1.1 %collective-permute-start = (f32[3,16,256]{2,1,0:T(8,128)S(1)}, f32[3,16,256]{2,1,0:T(8,128)S(1)}, u32[]{:S(2)}, u32[]{:S(2)}) collective-permute-start(f32[3,16,256]{2,1,0:T(8,128)S(1)} %get-tuple-element.53), channel_id=1, source_target_pairs={{0,1},{1,2},{2,3},{3,4},{4,5},{5,6},{6,7},{7,0},{8,9},{9,10},{10,1... | collective-permute-start | bytes 147464 | tf_op jit(solution)/shard_map/ppermute | solution.py:515
  16.6 0.9 %collective-permute-start.1 = (f32[3,16,256]{2,1,0:T(8,128)S(1)}, f32[3,16,256]{2,1,0:T(8,128)S(1)}, u32[]{:S(2)}, u32[]{:S(2)}) collective-permute-start(f32[3,16,256]{2,1,0:T(8,128)S(1)} %get-tuple-element.54), channel_id=1, source_target_pairs={{0,7},{1,0},{2,1},{3,2},{4,3},{5,4},{6,5},{7,6},{8,15},{9,8},{10,9... | collective-permute-start | bytes 147464 | tf_op jit(solution)/shard_map/ppermute | solution.py:515
  17.5 2.1 %collective-permute-done.yprev = f32[3,16,256]{2,1,0:T(8,128)S(1)} collective-permute-done((f32[3,16,256]{2,1,0:T(8,128)S(1)}, f32[3,16,256]{2,1,0:T(8,128)S(1)}, u32[]{:S(2)}, u32[]{:S(2)}) %collective-permute-start) | collective-permute-done | bytes 49184 | tf_op jit(solution)/shard_map/ppermute | solution.py:515
  19.6 3.2 %collective-permute-done.1.ynext = f32[3,16,256]{2,1,0:T(8,128)S(1)} collective-permute-done((f32[3,16,256]{2,1,0:T(8,128)S(1)}, f32[3,16,256]{2,1,0:T(8,128)S(1)}, u32[]{:S(2)}, u32[]{:S(2)}) %collective-permute-start.1) | collective-permute-done | bytes 49184 | tf_op jit(solution)/shard_map/ppermute | solution.py:515
  22.8 0.0 collective-permute-start.4
  22.8 5.4 %collective-permute-start.5 = (f32[2,16,256]{2,1,0:T(8,128)S(1)}, f32[2,16,256]{2,1,0:T(8,128)S(1)}, u32[]{:S(2)}, u32[]{:S(2)}) collective-permute-start(f32[2,16,256]{2,1,0:T(8,128)S(1)} %get-tuple-element.56), channel_id=1, source_target_pairs={{0,248},{8,0},{16,8},{24,16},{32,24},{40,32},{48,40},{56,48},{64,5... | collective-permute-start | bytes 98312 | tf_op jit(solution)/shard_map/ppermute | solution.py:515
  28.2 0.9 %geometry.2 = (f32[17,16,256]{2,1,0:T(8,128)S(1)}, f32[17,16,256]{2,1,0:T(8,128)S(1)}, f32[17,16,256]{2,1,0:T(8,128)S(1)}, f32[3,16,256]{2,1,0:T(8,128)S(1)}, f32[3,16,256]{2,1,0:T(8,128)S(1)}) custom-call(s32[3]{0:T(128)S(1)} %copy-done, f32[8,10,2,16,256]{4,3,2,1,0:T(8,128)S(1)} %get-tuple-element.48.geo), custom_call_target="tpu_custom_call" | custom-call | tf_op jit(solution)/shard_map/geometry/pallas_call | solution.py:504
  29.1 1.9 %change_sums.3.dsum = f32[8,6,2,16,256]{4,3,2,1,0:T(8,128)S(1)} custom-call(f32[3,12,2,16,256]{4,3,2,1,0:T(8,128)S(1)} %get-tuple-element.43.pos, f32[3,12,2,16,256]{4,3,2,1,0:T(8,128)S(1)} %get-tuple-element.49.thermal, s32[12,2,16,256]{3,2,1,0:T(8,128)S(1)} %get-tuple-element.45.code), custom_call_target="tpu_custom_call" | custom-call | tf_op jit(solution)/shard_map/change_sums/pallas_call | solution.py:493
  31.0 0.0 collective-permute-done.4.cprev
  31.0 0.0 collective-permute-done.3.xnext
  31.1 2.1 %step.2 = (f32[17,16,256]{2,1,0:T(8,128)S(1)}, f32[17,16,256]{2,1,0:T(8,128)S(1)}, f32[17,16,256]{2,1,0:T(8,128)S(1)}, f32[3,16,256]{2,1,0:T(8,128)S(1)}, f32[3,16,256]{2,1,0:T(8,128)S(1)}) custom-call(s32[3]{0:T(128)S(1)} %copy-done, f32[8,10,2,16,256]{4,3,2,1,0:T(8,128)S(1)} %get-tuple-element.48.geo, f32[8,6,2,16,256]{4,3,2,1,0:T(8,128)S(1)} %change_sums.3.dsum, ...), custom_call_target="tpu_custom_call" | custom-call | tf_op jit(solution)/shard_map/step/pallas_call | solution.py:546
  33.2 4.1 %collective-permute-start.9 = (f32[17,16,256]{2,1,0:T(8,128)S(1)}, f32[17,16,256]{2,1,0:T(8,128)S(1)}, u32[]{:S(2)}, u32[]{:S(2)}) collective-permute-start(f32[17,16,256]{2,1,0:T(8,128)S(1)} %get-tuple-element.62.own0), channel_id=1, source_target_pairs={{0,248},{8,0},{16,8},{24,16},{32,24},{40,32},{48,40},{56,48},{64,5... | collective-permute-start | bytes 835592 | tf_op jit(solution)/shard_map/ppermute | solution.py:515
  37.3 2.1 %collective-permute-start.6 = (f32[3,16,256]{2,1,0:T(8,128)S(1)}, f32[3,16,256]{2,1,0:T(8,128)S(1)}, u32[]{:S(2)}, u32[]{:S(2)}) collective-permute-start(f32[3,16,256]{2,1,0:T(8,128)S(1)} %get-tuple-element.65), channel_id=1, source_target_pairs={{0,1},{1,2},{2,3},{3,4},{4,5},{5,6},{6,7},{7,0},{8,9},{9,10},{10,1... | collective-permute-start | bytes 147464 | tf_op jit(solution)/shard_map/ppermute | solution.py:515
  39.5 2.0 %collective-permute-done.6.yprev = f32[3,16,256]{2,1,0:T(8,128)S(1)} collective-permute-done((f32[3,16,256]{2,1,0:T(8,128)S(1)}, f32[3,16,256]{2,1,0:T(8,128)S(1)}, u32[]{:S(2)}, u32[]{:S(2)}) %collective-permute-start.6) | collective-permute-done | bytes 49184 | tf_op jit(solution)/shard_map/ppermute | solution.py:515
  41.4 4.2 %collective-permute-done.7.ynext = f32[3,16,256]{2,1,0:T(8,128)S(1)} collective-permute-done((f32[3,16,256]{2,1,0:T(8,128)S(1)}, f32[3,16,256]{2,1,0:T(8,128)S(1)}, u32[]{:S(2)}, u32[]{:S(2)}) %collective-permute-start.7) | collective-permute-done | bytes 49184 | tf_op jit(solution)/shard_map/ppermute | solution.py:515
  45.7 5.4 %collective-permute-start.11 = (f32[2,16,256]{2,1,0:T(8,128)S(1)}, f32[2,16,256]{2,1,0:T(8,128)S(1)}, u32[]{:S(2)}, u32[]{:S(2)}) collective-permute-start(f32[2,16,256]{2,1,0:T(8,128)S(1)} %get-tuple-element.68), channel_id=1, source_target_pairs={{0,248},{8,0},{16,8},{24,16},{32,24},{40,32},{48,40},{56,48},{64,5... | collective-permute-start | bytes 98312 | tf_op jit(solution)/shard_map/ppermute | solution.py:515
  51.0 0.9 %geometry.3 = (f32[17,16,256]{2,1,0:T(8,128)S(1)}, f32[17,16,256]{2,1,0:T(8,128)S(1)}, f32[17,16,256]{2,1,0:T(8,128)S(1)}, f32[3,16,256]{2,1,0:T(8,128)S(1)}, f32[3,16,256]{2,1,0:T(8,128)S(1)}) custom-call(s32[3]{0:T(128)S(1)} %copy-done, f32[8,10,2,16,256]{4,3,2,1,0:T(8,128)S(1)} %get-tuple-element.48.geo), custom_call_target="tpu_custom_call" | custom-call | tf_op jit(solution)/shard_map/geometry/pallas_call | solution.py:504
  52.0 1.9 %change_sums.2.dsum = f32[8,6,2,16,256]{4,3,2,1,0:T(8,128)S(1)} custom-call(f32[3,12,2,16,256]{4,3,2,1,0:T(8,128)S(1)} %get-tuple-element.43.pos, f32[3,12,2,16,256]{4,3,2,1,0:T(8,128)S(1)} %get-tuple-element.49.thermal, s32[12,2,16,256]{3,2,1,0:T(8,128)S(1)} %get-tuple-element.45.code), custom_call_target="tpu_custom_call" | custom-call | tf_op jit(solution)/shard_map/change_sums/pallas_call | solution.py:493
  53.9 2.1 %step.3 = (f32[17,16,256]{2,1,0:T(8,128)S(1)}, f32[17,16,256]{2,1,0:T(8,128)S(1)}, f32[17,16,256]{2,1,0:T(8,128)S(1)}, f32[3,16,256]{2,1,0:T(8,128)S(1)}, f32[3,16,256]{2,1,0:T(8,128)S(1)}) custom-call(s32[3]{0:T(128)S(1)} %copy-done, f32[8,10,2,16,256]{4,3,2,1,0:T(8,128)S(1)} %get-tuple-element.48.geo, f32[8,6,2,16,256]{4,3,2,1,0:T(8,128)S(1)} %change_sums.2.dsum, ...), custom_call_target="tpu_custom_call" | custom-call | tf_op jit(solution)/shard_map/step/pallas_call | solution.py:546
  56.0 4.1 %collective-permute-start.15 = (f32[17,16,256]{2,1,0:T(8,128)S(1)}, f32[17,16,256]{2,1,0:T(8,128)S(1)}, u32[]{:S(2)}, u32[]{:S(2)}) collective-permute-start(f32[17,16,256]{2,1,0:T(8,128)S(1)} %get-tuple-element.74.own0), channel_id=1, source_target_pairs={{0,248},{8,0},{16,8},{24,16},{32,24},{40,32},{48,40},{56,48},{64,5... | collective-permute-start | bytes 835592 | tf_op jit(solution)/shard_map/ppermute | solution.py:515
  60.2 0.1 collective-permute-start.12
  60.3 1.9 %collective-permute-start.13 = (f32[3,16,256]{2,1,0:T(8,128)S(1)}, f32[3,16,256]{2,1,0:T(8,128)S(1)}, u32[]{:S(2)}, u32[]{:S(2)}) collective-permute-start(f32[3,16,256]{2,1,0:T(8,128)S(1)} %get-tuple-element.78), channel_id=1, source_target_pairs={{0,7},{1,0},{2,1},{3,2},{4,3},{5,4},{6,5},{7,6},{8,15},{9,8},{10,9... | collective-permute-start | bytes 147464 | tf_op jit(solution)/shard_map/ppermute | solution.py:515
  62.2 2.1 %collective-permute-done.12.yprev = f32[3,16,256]{2,1,0:T(8,128)S(1)} collective-permute-done((f32[3,16,256]{2,1,0:T(8,128)S(1)}, f32[3,16,256]{2,1,0:T(8,128)S(1)}, u32[]{:S(2)}, u32[]{:S(2)}) %collective-permute-start.12) | collective-permute-done | bytes 49184 | tf_op jit(solution)/shard_map/ppermute | solution.py:515
  64.3 2.5 %collective-permute-done.13.ynext = f32[3,16,256]{2,1,0:T(8,128)S(1)} collective-permute-done((f32[3,16,256]{2,1,0:T(8,128)S(1)}, f32[3,16,256]{2,1,0:T(8,128)S(1)}, u32[]{:S(2)}, u32[]{:S(2)}) %collective-permute-start.13) | collective-permute-done | bytes 49184 | tf_op jit(solution)/shard_map/ppermute | solution.py:515
  66.8 5.4 %collective-permute-start.17 = (f32[2,16,256]{2,1,0:T(8,128)S(1)}, f32[2,16,256]{2,1,0:T(8,128)S(1)}, u32[]{:S(2)}, u32[]{:S(2)}) collective-permute-start(f32[2,16,256]{2,1,0:T(8,128)S(1)} %get-tuple-element.80), channel_id=1, source_target_pairs={{0,248},{8,0},{16,8},{24,16},{32,24},{40,32},{48,40},{56,48},{64,5... | collective-permute-start | bytes 98312 | tf_op jit(solution)/shard_map/ppermute | solution.py:515
  72.2 1.6 %collective-permute-done.16.cprev = f32[2,16,256]{2,1,0:T(8,128)S(1)} collective-permute-done((f32[2,16,256]{2,1,0:T(8,128)S(1)}, f32[2,16,256]{2,1,0:T(8,128)S(1)}, u32[]{:S(2)}, u32[]{:S(2)}) %collective-permute-start.16) | collective-permute-done | bytes 32800 | tf_op jit(solution)/shard_map/ppermute | solution.py:515
  73.8 0.0 collective-permute-done.17.cnext
  73.8 0.4 last.1.table
  74.2 3.0 %particles.1 = f32[3,12,2,16,256]{4,3,2,1,0:T(8,128)} custom-call(s32[3]{0:T(128)S(1)} %copy-done, f32[2,6,3,24,256]{4,3,2,1,0:T(8,128)S(1)} %last.1.table, f32[3,12,2,16,256]{4,3,2,1,0:T(8,128)S(1)} %get-tuple-element.43.pos, f32[3,12,2,16,256]{4,3,2,1,0:T(8,128)S(1)} %get-tuple-element.49.thermal, s32[12,2,16,256]{3,2,1,0:T(8,128)S(1)} %get-tuple-element.45.code), custom_call_target="tpu_custom_call" | custom-call | tf_op jit(solution)/shard_map/particles/pallas_call | solution.py:566
  (19 shorter events, 0.1 us)
Async XLA Ops:
  0.0 3.9 %copy-start = (s32[3]{0:T(128)S(1)}, s32[3]{0:T(128)}, u32[]{:S(2)}) copy-start(s32[3]{0:T(128)} %shifts.11) | copy-start | bytes 40
  8.6 22.4 %collective-permute-start.3 = (f32[17,16,256]{2,1,0:T(8,128)S(1)}, f32[17,16,256]{2,1,0:T(8,128)S(1)}, u32[]{:S(2)}, u32[]{:S(2)}) collective-permute-start(f32[17,16,256]{2,1,0:T(8,128)S(1)} %get-tuple-element.50.own0), channel_id=1, source_target_pairs={{0,248},{8,0},{16,8},{24,16},{32,24},{40,32},{48,40},{56,48},{64,5... | collective-permute-start | bytes 835592 | tf_op jit(solution)/shard_map/ppermute | solution.py:515
  15.5 15.6 %collective-permute-start.2 = (f32[17,16,256]{2,1,0:T(8,128)S(1)}, f32[17,16,256]{2,1,0:T(8,128)S(1)}, u32[]{:S(2)}, u32[]{:S(2)}) collective-permute-start(f32[17,16,256]{2,1,0:T(8,128)S(1)} %get-tuple-element.52.own2), channel_id=1, source_target_pairs={{0,8},{8,16},{16,24},{24,32},{32,40},{40,48},{48,56},{56,64},{64,7... | collective-permute-start | bytes 835592 | tf_op jit(solution)/shard_map/ppermute | solution.py:515
  15.5 4.1 %collective-permute-start = (f32[3,16,256]{2,1,0:T(8,128)S(1)}, f32[3,16,256]{2,1,0:T(8,128)S(1)}, u32[]{:S(2)}, u32[]{:S(2)}) collective-permute-start(f32[3,16,256]{2,1,0:T(8,128)S(1)} %get-tuple-element.53), channel_id=1, source_target_pairs={{0,1},{1,2},{2,3},{3,4},{4,5},{5,6},{6,7},{7,0},{8,9},{9,10},{10,1... | collective-permute-start | bytes 147464 | tf_op jit(solution)/shard_map/ppermute | solution.py:515
  16.6 6.2 %collective-permute-start.1 = (f32[3,16,256]{2,1,0:T(8,128)S(1)}, f32[3,16,256]{2,1,0:T(8,128)S(1)}, u32[]{:S(2)}, u32[]{:S(2)}) collective-permute-start(f32[3,16,256]{2,1,0:T(8,128)S(1)} %get-tuple-element.54), channel_id=1, source_target_pairs={{0,7},{1,0},{2,1},{3,2},{4,3},{5,4},{6,5},{7,6},{8,15},{9,8},{10,9... | collective-permute-start | bytes 147464 | tf_op jit(solution)/shard_map/ppermute | solution.py:515
  22.8 8.2 %collective-permute-start.4 = (f32[2,16,256]{2,1,0:T(8,128)S(1)}, f32[2,16,256]{2,1,0:T(8,128)S(1)}, u32[]{:S(2)}, u32[]{:S(2)}) collective-permute-start(f32[2,16,256]{2,1,0:T(8,128)S(1)} %get-tuple-element.55), channel_id=1, source_target_pairs={{0,8},{8,16},{16,24},{24,32},{32,40},{40,48},{48,56},{56,64},{64,7... | collective-permute-start | bytes 98312 | tf_op jit(solution)/shard_map/ppermute | solution.py:515
  22.8 8.2 %collective-permute-start.5 = (f32[2,16,256]{2,1,0:T(8,128)S(1)}, f32[2,16,256]{2,1,0:T(8,128)S(1)}, u32[]{:S(2)}, u32[]{:S(2)}) collective-permute-start(f32[2,16,256]{2,1,0:T(8,128)S(1)} %get-tuple-element.56), channel_id=1, source_target_pairs={{0,248},{8,0},{16,8},{24,16},{32,24},{40,32},{48,40},{56,48},{64,5... | collective-permute-start | bytes 98312 | tf_op jit(solution)/shard_map/ppermute | solution.py:515
  33.2 20.7 %collective-permute-start.9 = (f32[17,16,256]{2,1,0:T(8,128)S(1)}, f32[17,16,256]{2,1,0:T(8,128)S(1)}, u32[]{:S(2)}, u32[]{:S(2)}) collective-permute-start(f32[17,16,256]{2,1,0:T(8,128)S(1)} %get-tuple-element.62.own0), channel_id=1, source_target_pairs={{0,248},{8,0},{16,8},{24,16},{32,24},{40,32},{48,40},{56,48},{64,5... | collective-permute-start | bytes 835592 | tf_op jit(solution)/shard_map/ppermute | solution.py:515
  37.3 16.6 %collective-permute-start.8 = (f32[17,16,256]{2,1,0:T(8,128)S(1)}, f32[17,16,256]{2,1,0:T(8,128)S(1)}, u32[]{:S(2)}, u32[]{:S(2)}) collective-permute-start(f32[17,16,256]{2,1,0:T(8,128)S(1)} %get-tuple-element.64.own2), channel_id=1, source_target_pairs={{0,8},{8,16},{16,24},{24,32},{32,40},{40,48},{48,56},{56,64},{64,7... | collective-permute-start | bytes 835592 | tf_op jit(solution)/shard_map/ppermute | solution.py:515
  37.3 4.1 %collective-permute-start.6 = (f32[3,16,256]{2,1,0:T(8,128)S(1)}, f32[3,16,256]{2,1,0:T(8,128)S(1)}, u32[]{:S(2)}, u32[]{:S(2)}) collective-permute-start(f32[3,16,256]{2,1,0:T(8,128)S(1)} %get-tuple-element.65), channel_id=1, source_target_pairs={{0,1},{1,2},{2,3},{3,4},{4,5},{5,6},{6,7},{7,0},{8,9},{9,10},{10,1... | collective-permute-start | bytes 147464 | tf_op jit(solution)/shard_map/ppermute | solution.py:515
  39.4 6.2 %collective-permute-start.7 = (f32[3,16,256]{2,1,0:T(8,128)S(1)}, f32[3,16,256]{2,1,0:T(8,128)S(1)}, u32[]{:S(2)}, u32[]{:S(2)}) collective-permute-start(f32[3,16,256]{2,1,0:T(8,128)S(1)} %get-tuple-element.66), channel_id=1, source_target_pairs={{0,7},{1,0},{2,1},{3,2},{4,3},{5,4},{6,5},{7,6},{8,15},{9,8},{10,9... | collective-permute-start | bytes 147464 | tf_op jit(solution)/shard_map/ppermute | solution.py:515
  45.7 8.2 %collective-permute-start.10 = (f32[2,16,256]{2,1,0:T(8,128)S(1)}, f32[2,16,256]{2,1,0:T(8,128)S(1)}, u32[]{:S(2)}, u32[]{:S(2)}) collective-permute-start(f32[2,16,256]{2,1,0:T(8,128)S(1)} %get-tuple-element.67), channel_id=1, source_target_pairs={{0,8},{8,16},{16,24},{24,32},{32,40},{40,48},{48,56},{56,64},{64,7... | collective-permute-start | bytes 98312 | tf_op jit(solution)/shard_map/ppermute | solution.py:515
  45.7 8.2 %collective-permute-start.11 = (f32[2,16,256]{2,1,0:T(8,128)S(1)}, f32[2,16,256]{2,1,0:T(8,128)S(1)}, u32[]{:S(2)}, u32[]{:S(2)}) collective-permute-start(f32[2,16,256]{2,1,0:T(8,128)S(1)} %get-tuple-element.68), channel_id=1, source_target_pairs={{0,248},{8,0},{16,8},{24,16},{32,24},{40,32},{48,40},{56,48},{64,5... | collective-permute-start | bytes 98312 | tf_op jit(solution)/shard_map/ppermute | solution.py:515
  56.0 17.7 %collective-permute-start.15 = (f32[17,16,256]{2,1,0:T(8,128)S(1)}, f32[17,16,256]{2,1,0:T(8,128)S(1)}, u32[]{:S(2)}, u32[]{:S(2)}) collective-permute-start(f32[17,16,256]{2,1,0:T(8,128)S(1)} %get-tuple-element.74.own0), channel_id=1, source_target_pairs={{0,248},{8,0},{16,8},{24,16},{32,24},{40,32},{48,40},{56,48},{64,5... | collective-permute-start | bytes 835592 | tf_op jit(solution)/shard_map/ppermute | solution.py:515
  60.2 13.6 %collective-permute-start.14 = (f32[17,16,256]{2,1,0:T(8,128)S(1)}, f32[17,16,256]{2,1,0:T(8,128)S(1)}, u32[]{:S(2)}, u32[]{:S(2)}) collective-permute-start(f32[17,16,256]{2,1,0:T(8,128)S(1)} %get-tuple-element.76.own2), channel_id=1, source_target_pairs={{0,8},{8,16},{16,24},{24,32},{32,40},{40,48},{48,56},{56,64},{64,7... | collective-permute-start | bytes 835592 | tf_op jit(solution)/shard_map/ppermute | solution.py:515
  60.2 4.1 %collective-permute-start.12 = (f32[3,16,256]{2,1,0:T(8,128)S(1)}, f32[3,16,256]{2,1,0:T(8,128)S(1)}, u32[]{:S(2)}, u32[]{:S(2)}) collective-permute-start(f32[3,16,256]{2,1,0:T(8,128)S(1)} %get-tuple-element.77), channel_id=1, source_target_pairs={{0,1},{1,2},{2,3},{3,4},{4,5},{5,6},{6,7},{7,0},{8,9},{9,10},{10,1... | collective-permute-start | bytes 147464 | tf_op jit(solution)/shard_map/ppermute | solution.py:515
  60.3 6.6 %collective-permute-start.13 = (f32[3,16,256]{2,1,0:T(8,128)S(1)}, f32[3,16,256]{2,1,0:T(8,128)S(1)}, u32[]{:S(2)}, u32[]{:S(2)}) collective-permute-start(f32[3,16,256]{2,1,0:T(8,128)S(1)} %get-tuple-element.78), channel_id=1, source_target_pairs={{0,7},{1,0},{2,1},{3,2},{4,3},{5,4},{6,5},{7,6},{8,15},{9,8},{10,9... | collective-permute-start | bytes 147464 | tf_op jit(solution)/shard_map/ppermute | solution.py:515
  66.8 7.0 %collective-permute-start.16 = (f32[2,16,256]{2,1,0:T(8,128)S(1)}, f32[2,16,256]{2,1,0:T(8,128)S(1)}, u32[]{:S(2)}, u32[]{:S(2)}) collective-permute-start(f32[2,16,256]{2,1,0:T(8,128)S(1)} %get-tuple-element.79), channel_id=1, source_target_pairs={{0,8},{8,16},{16,24},{24,32},{32,40},{40,48},{48,56},{56,64},{64,7... | collective-permute-start | bytes 98312 | tf_op jit(solution)/shard_map/ppermute | solution.py:515
  66.8 6.9 %collective-permute-start.17 = (f32[2,16,256]{2,1,0:T(8,128)S(1)}, f32[2,16,256]{2,1,0:T(8,128)S(1)}, u32[]{:S(2)}, u32[]{:S(2)}) collective-permute-start(f32[2,16,256]{2,1,0:T(8,128)S(1)} %get-tuple-element.80), channel_id=1, source_target_pairs={{0,248},{8,0},{16,8},{24,16},{32,24},{40,32},{48,40},{56,48},{64,5... | collective-permute-start | bytes 98312 | tf_op jit(solution)/shard_map/ppermute | solution.py:515

commit v2 on v1

--- a/solution.py
+++ b/solution.py
@@ -18,19 +18,16 @@
     return code // 4, code // 2 % 2, code % 2
 
 
+def is_even(axis):
+    return lax.axis_index(axis) % 2 == 0
+
+
 def cross(u, v):
     return [
         u[1] * v[2] - u[2] * v[1],
         u[2] * v[0] - u[0] * v[2],
         u[0] * v[1] - u[1] * v[0],
     ]
-
-
-def plus(terms):
-    total = None
-    for term in terms:
-        total = term if total is None else total + term
-    return total
 
 
 def accumulate(value_ref, codes, groups, names, store):
@@ -85,7 +82,7 @@
 
 def near_sums_kernel(
     shifts_in, pos_in, vel_in, thermal_in, offsets_in, occupancy_in,
-    pos, thermal, rel, code, geo, wsum, yup, ydn,
+    pos, thermal, rel, code, geo, wsum, y_in, y_out,
     vel, offsets, occupancy, value, ends, shifts, sems, shift_sem,
 ):
     slots, rows, cols, depth = code.shape
@@ -123,42 +120,38 @@
                         vel[c, slot, row, at, lanes] - thermal[c, slot, row, at, lanes]
                     )
             chunk_sums(pos, rel, code, value, geo, wsum, groups, row, at, lanes)
-    for out, by, col in ((yup, 0, cols - 1), (ydn, 1, 0)):
-        for bz in range(2):
-            for bx in range(2):
-                frame = 4 * bx + 2 * by + bz
-                o = frame ^ shifts[0]
-                for row in range(rows):
-                    own = geo_frame(geo, o, frame, row, pl.ds(col, 1))
-                    own.update(vel_frame(wsum, o, frame, row, pl.ds(col, 1)))
-                    for v in range(16):
-                        if bx == 1 and row == 1:
-                            ends[bz, 1, v : v + 1, :] += own[v]
-                        else:
-                            ends[bz, row + 1 - bx, v : v + 1, :] = own[v]
-        for r in range(3):
-            out[r] = ends[0, r] + roll(ends[1, r], -1)
+
+    def frame_of(*where):
+        return {**geo_frame(geo, *where), **vel_frame(wsum, *where)}
+
+    up, down = edges(frame_of, range(16), shifts[0], ends, cols)
+    even = is_even("gy")
+    for r in range(3):
+        y_in[r] = jnp.where(even, up[r], down[r])
+        y_out[r] = jnp.where(even, down[r], up[r])
 
 
 def rest_sums_kernel(
-    shifts, pos, rel, code, geo_near, wsum_near, geo, wsum, row0, row1, row2, value, part, shifted
+    shifts, pos, rel, code, geo_near, wsum_near,
+    geo, wsum, far, mid, near, value, low, high, part, shifted,
 ):
     _, rows, cols, depth = code.shape
     for row in range(rows):
         for tile in range(cols // 8):
             at = pl.ds(8 * tile, 8)
-            far = 0 if tile == 0 else 1
-            for o in four(1 - far, shifts[0]):
+            by = 0 if tile == 0 else 1
+            for o in four(1 - by, shifts[0]):
                 for v in range(10):
                     geo[o, v, row, at, :] = geo_near[o, v, row, at, :]
                 for v in range(6):
                     wsum[o, v, row, at, :] = wsum_near[o, v, row, at, :]
-            groups = four(far, shifts[0])
+            groups = four(by, shifts[0])
             for lanes in halves(depth):
                 chunk_sums(pos, rel, code, value, geo, wsum, groups, row, at, lanes)
-    outs = (row0, row1, row2)
+    outs = (low, mid, high)
     expand(lambda *where: geo_frame(geo, *where), GEO, shifts[0], outs, None, None, part, shifted)
     expand(lambda *where: vel_frame(wsum, *where), VEL, shifts[0], outs, None, None, part, shifted)
+    by_role(is_even("gx"), low, high, far, near)
 
 
 def change_sums_kernel(step, pos, thermal, code, dsum, value):
@@ -255,27 +248,58 @@
                 ydn[r, v : v + 1, :] = beyond[0:1]
 
 
+def edges(frame_of, names, shift, ends, cols):
+    found = []
+    for by, col in ((0, cols - 1), (1, 0)):
+        for bz in range(2):
+            for bx in range(2):
+                frame = 4 * bx + 2 * by + bz
+                for row in range(2):
+                    own = frame_of(frame ^ shift, frame, row, pl.ds(col, 1))
+                    for v in names:
+                        if bx == 1 and row == 1:
+                            ends[bz, 1, v : v + 1, :] += own[v]
+                        else:
+                            ends[bz, row + 1 - bx, v : v + 1, :] = own[v]
+        found.append([ends[0, r] + roll(ends[1, r], -1) for r in range(3)])
+    return found
+
+
 def geometry_kernel(step, shifts, geo, row0, row1, row2, yup, ydn, part, shifted):
     outs = (row0, row1, row2)
+    yup[...] = jnp.zeros_like(yup)
+    ydn[...] = jnp.zeros_like(ydn)
     expand(
         lambda *where: geo_frame(geo, *where), GEO, shifts[step], outs, yup, ydn, part, shifted
     )
 
 
-def corner_kernel(yprev, ynext, low, high):
-    for out, r in ((low, 0), (high, 2)):
-        out[0] = yprev[r]
-        out[1] = ynext[r]
-
-
-def complete_row(row, ends, out):
+def by_role(even, first, second, one, two):
+    for at in range(first.shape[0]):
+        one[at] = jnp.where(even, first[at], second[at])
+        two[at] = jnp.where(even, second[at], first[at])
+
+
+def y_parts(y_in, y_out, r):
+    even = is_even("gy")
+    return jnp.where(even, y_out[r], y_in[r]), jnp.where(even, y_in[r], y_out[r])
+
+
+def complete_row(row, low, high, out):
     last = out.shape[1] - 1
+    out[...] = row[...]
+    out[16] = row[16] + low
     for v in range(16):
-        out[v] = plus([part[v] for part in row])
-    out[16] = plus([part[16] for part in row] + [low for low, _ in ends])
-    add = plus([high for _, high in ends])
-    for v in range(16):
-        out[v, last : last + 1, :] += add[v : v + 1]
+        out[v, last : last + 1, :] = row[v, last : last + 1, :] + high[v : v + 1]
+
+
+def fold_kernel(far, near, y_in, y_out, far_out, near_out):
+    even = is_even("gx")
+    low, high = y_parts(y_in, y_out, 0), y_parts(y_in, y_out, 2)
+    far_ends = [jnp.where(even, low[at], high[at]) for at in range(2)]
+    near_ends = [jnp.where(even, high[at], low[at]) for at in range(2)]
+    complete_row(far, *far_ends, far_out)
+    complete_row(near, *near_ends, near_out)
 
 
 def solve(sums):
@@ -312,22 +336,26 @@
 
 
 def fill_table(own, around, table, total):
-    yprev, ynext, xprev, xnext, cprev, cnext = around
-    cols = own[0].shape[1]
+    far, mid, near = own
+    y_in, y_out, x_far, x_near = around
+    cols = mid.shape[1]
+    even = is_even("gx")
+    complete_row(mid, *y_parts(y_in, y_out, 1), total)
     for r in range(3):
-        row, ends = [own[r]], [(yprev[r], ynext[r])]
-        if r != 1:
-            row.append(xprev if r == 0 else xnext)
-            corner = cprev if r == 0 else cnext
-            ends.append((corner[0], corner[1]))
-        complete_row(row, ends, total)
+        if r == 1:
+            read = lambda v, at: total[v, at, :]
+        else:
+            mine = even if r == 0 else jnp.logical_not(even)
+            read = lambda v, at: jnp.where(
+                mine, far[v, at, :] + x_far[v, at, :], near[v, at, :] + x_near[v, at, :]
+            )
         for t in range(cols // 8):
             at = pl.ds(8 * t, 8)
-            state = solve([total[v, at, :] for v in range(16)])
+            state = solve([read(v, at) for v in range(16)])
             for v in range(6):
                 table[0, v, r, 8 + 8 * t : 16 + 8 * t, :] = state[v]
                 table[1, v, r, 8 + 8 * t : 16 + 8 * t, :] = roll(state[v], 1)
-        state = solve([total[16, v : v + 1, :] for v in range(16)])
+        state = solve([read(16, pl.ds(v, 1)) for v in range(16)])
         for v in range(6):
             wide = jnp.broadcast_to(state[v], (8, state[v].shape[1]))
             table[0, v, r, 0:8, :] = wide
@@ -373,56 +401,82 @@
 
 
 def step_kernel(
-    step, shifts, geo, dsum, own0, own1, own2, yprev, ynext, xprev, xnext, cprev, cnext,
-    geo0, geo1, geo2, geoup, geodn,
-    row0, row1, row2, yup, ydn, total, table, wsum, part, shifted,
+    step, shifts, geo, dsum, far, mid, near, y_in, y_out, x_far, x_near, geoup, geodn,
+    wsum, next_in, next_out, total, table, ends,
 ):
-    fill_table((own0, own1, own2), (yprev, ynext, xprev, xnext, cprev, cnext), table, total)
+    cols = mid.shape[1]
+    fill_table((far, mid, near), (y_in, y_out, x_far, x_near), table, total)
     update_groups(geo, dsum, shifts[step], table, wsum)
-    rows = (row0, row1, row2)
+    for bz in range(2):
+        for r in range(3):
+            ends[bz, r] = jnp.zeros_like(ends[bz, r])
+    up, down = edges(
+        lambda *where: vel_frame(wsum, *where), VEL, shifts[step + 1], ends, cols
+    )
+    even = is_even("gy")
+    for r in range(3):
+        up_r, down_r = geoup[r] + up[r], geodn[r] + down[r]
+        next_in[r] = jnp.where(even, up_r, down_r)
+        next_out[r] = jnp.where(even, down_r, up_r)
+
+
+def rows_kernel(
+    step, shifts, wsum, geo0, geo1, geo2, far, mid, near, low, high, part, shifted
+):
+    rows = (low, mid, high)
     for target, source in zip(rows, (geo0, geo1, geo2)):
         for v in GEO:
             target[v] = source[v]
         target[16] = source[16]
-    yup[...] = geoup[...]
-    ydn[...] = geodn[...]
-    expand(lambda *where: vel_frame(wsum, *where), VEL, shifts[step + 1], rows, yup, ydn, part, shifted)
-
-
-def last_kernel(own0, own1, own2, yprev, ynext, xprev, xnext, cprev, cnext, table, total):
-    fill_table((own0, own1, own2), (yprev, ynext, xprev, xnext, cprev, cnext), table, total)
-
-
-def particles_kernel(shifts, table, pos, thermal, code, out, variants):
-    slots = code.shape[0]
-    row = pl.program_id(0)
-    tile = pl.program_id(1)
-    for half in range(pos.shape[4] // 128):
-        lanes = pl.ds(half * 128, 128)
-        for frame in range(GROUPS):
-            bx, by, bz = bits(frame)
-            values = [
-                table[bz, v, row + 1 - bx, pl.ds(8 * tile, 16), lanes][8 - by : 16 - by]
-                for v in range(6)
-            ]
-            values[:3] = shift_a(values[:3], values[3:], (bx, by, bz))
-            for v in range(6):
-                variants[frame, v] = values[v]
-        for slot in range(slots):
-            base = code[slot, 0, :, lanes]
-            k = base ^ shifts[STEPS - 1]
-            isx, isy, isz = (k & 4) != 0, (k & 2) != 0, (k & 1) != 0
-            used = base < GROUPS
-            state = []
-            for v in range(6):
-                level = [jnp.where(isx, variants[4 + i, v], variants[i, v]) for i in range(4)]
-                level = [jnp.where(isy, level[2 + i], level[i]) for i in range(2)]
-                state.append(jnp.where(isz, level[1], level[0]))
-            p = [pos[c, slot, 0, :, lanes] for c in range(3)]
-            turn = cross(state[3:], p)
-            for c in range(3):
-                fresh = thermal[c, (slot + STEPS - 1) % slots, 0, :, lanes] + (state[c] + turn[c])
-                out[c, slot, 0, :, lanes] = jnp.where(used, fresh, 0.0)
+    expand(
+        lambda *where: vel_frame(wsum, *where), VEL, shifts[step + 1], rows, None, None, part, shifted
+    )
+    by_role(is_even("gx"), low, high, far, near)
+
+
+def particles_kernel(
+    shifts, far, mid, near, y_in, y_out, x_far, x_near, pos, thermal, code,
+    out, total, table, variants, fresh, sems,
+):
+    slots, rows, cols, depth = code.shape
+    fill_table((far, mid, near), (y_in, y_out, x_far, x_near), table, total)
+    copies = []
+    for row in range(rows):
+        for tile in range(cols // 8):
+            at = pl.ds(8 * tile, 8)
+            for lanes in halves(depth):
+                for frame in range(GROUPS):
+                    bx, by, bz = bits(frame)
+                    first = 8 + 8 * tile - by
+                    values = [
+                        table[bz, v, row + 1 - bx, first : first + 8, lanes] for v in range(6)
+                    ]
+                    values[:3] = shift_a(values[:3], values[3:], (bx, by, bz))
+                    for v in range(6):
+                        variants[frame, v] = values[v]
+                for slot in range(slots):
+                    base = code[slot, row, at, lanes]
+                    k = base ^ shifts[STEPS - 1]
+                    isx, isy, isz = (k & 4) != 0, (k & 2) != 0, (k & 1) != 0
+                    used = base < GROUPS
+                    state = []
+                    for v in range(6):
+                        level = [jnp.where(isx, variants[4 + i, v], variants[i, v]) for i in range(4)]
+                        level = [jnp.where(isy, level[2 + i], level[i]) for i in range(2)]
+                        state.append(jnp.where(isz, level[1], level[0]))
+                    turn = cross(state[3:], [pos[c, slot, row, at, lanes] for c in range(3)])
+                    for c in range(3):
+                        hot = thermal[c, (slot + STEPS - 1) % slots, row, at, lanes]
+                        new = hot + (state[c] + turn[c])
+                        fresh[c, slot, row, at, lanes] = jnp.where(used, new, 0.0)
+            index = len(copies)
+            copy = pltpu.make_async_copy(
+                fresh.at[:, :, row, at, :], out.at[:, :, row, at, :], sems.at[index]
+            )
+            copy.start()
+            copies.append(copy)
+    for copy in copies:
+        copy.wait()
 
 
 VMEM = pl.BlockSpec(memory_space=pltpu.VMEM)
@@ -442,16 +496,8 @@
     return jax.ShapeDtypeStruct(dims, F32)
 
 
-def big_spec(lead):
-    return pl.BlockSpec((*lead, 1, 8, 256), lambda r, t: (*([0] * len(lead)), r, t, 0))
-
-
 def local(positions, velocities, thermal, offsets, occupancy, shift_codes):
     slots, rows, cols, depth = offsets.shape
-    grid = (rows, cols // 8)
-    vec = big_spec((3, slots))
-    flat = big_spec((slots,))
-    group = lambda count: pltpu.VMEM((GROUPS, count, rows, cols, depth), F32)
     group_shape = lambda count: shape(GROUPS, count, rows, cols, depth)
     value = lambda count: pltpu.VMEM((count, slots, 8, 128), F32)
     vec_shape = shape(3, slots, rows, cols, depth)
@@ -466,7 +512,7 @@
     total = pltpu.VMEM((17, cols, depth), F32)
     table_shape = (2, 6, 3, cols + 8, depth)
 
-    pos, hot, rel, code, geo_near, wsum_near, yup, ydn = pl.pallas_call(
+    pos, hot, rel, code, geo_near, wsum_near, y_in, y_out = pl.pallas_call(
         near_sums_kernel,
         in_specs=[HBM] * 6,
         out_specs=[VMEM] * 8,
@@ -485,9 +531,10 @@
         name="near_sums",
     )(*map(in_hbm, (shift_codes, positions, velocities, thermal, offsets, occupancy)))
 
-    def ring(axis, by):
+    def swap(value, axis, odd):
         count = lax.axis_size(axis)
-        return [(i, (i + by) % count) for i in range(count)]
+        partner = [(((i + odd) ^ 1) - odd) % count for i in range(count)]
+        return lax.ppermute(value, axis, list(enumerate(partner)))
 
     def change_sums(step):
         return pl.pallas_call(
@@ -511,68 +558,70 @@
             name="geometry",
         )(shift_codes, geo)
 
-    def send(value, axis, by):
-        return lax.ppermute(value, axis, ring(axis, by))
+    row_scratch = pltpu.VMEM(row_shape.shape, F32)
 
     for step in range(STEPS):
-        yprev = send(yup, "gy", 1)
-        ynext = send(ydn, "gy", -1)
+        got_out = swap(y_out, "gy", 1)
+        got_in = swap(y_in, "gy", 0)
         if step == 0:
-            geo, _, row0, row1, row2 = pl.pallas_call(
+            geo, wsum, far, mid, near = pl.pallas_call(
                 rest_sums_kernel,
                 in_specs=[SMEM] + [VMEM] * 5,
                 out_specs=[VMEM] * 5,
                 out_shape=[group_shape(10), group_shape(6)] + [row_shape] * 3,
-                scratch_shapes=[value(15)] + expand_scratch,
+                scratch_shapes=[value(15), row_scratch, row_scratch] + expand_scratch,
                 compiler_params=params(16),
                 name="rest_sums",
             )(shift_codes, pos, rel, code, geo_near, wsum_near)
-        xprev = send(row2, "gx", 1)
-        xnext = send(row0, "gx", -1)
-        low, high = pl.pallas_call(
-            corner_kernel,
-            in_specs=[VMEM] * 2,
+        else:
+            far, mid, near = pl.pallas_call(
+                functools.partial(rows_kernel, step - 1),
+                in_specs=[SMEM] + [VMEM] * 4,
+                out_specs=[VMEM] * 3,
+                out_shape=[row_shape] * 3,
+                scratch_shapes=[row_scratch, row_scratch] + expand_scratch,
+                compiler_params=params(12),
+                name="rows",
+            )(shift_codes, wsum, *ahead)
+        far, near = pl.pallas_call(
+            fold_kernel,
+            in_specs=[VMEM] * 4,
             out_specs=[VMEM] * 2,
-            out_shape=[shape(2, 16, depth)] * 2,
+            out_shape=[row_shape] * 2,
             compiler_params=params(2),
-            name="corners",
-        )(yprev, ynext)
-        cprev = send(high, "gx", 1)
-        cnext = send(low, "gx", -1)
-        found = (row0, row1, row2, yprev, ynext, xprev, xnext, cprev, cnext)
+            name="fold",
+        )(far, near, got_in, got_out)
+        x_far = swap(far, "gx", 1)
+        x_near = swap(near, "gx", 0)
+        found = (far, mid, near, got_in, got_out, x_far, x_near)
         if step + 1 < STEPS:
             dsum = change_sums(step)
-            ahead = geometry(step + 1)
-            row0, row1, row2, yup, ydn = pl.pallas_call(
+            *ahead, geoup, geodn = geometry(step + 1)
+            wsum, y_in, y_out = pl.pallas_call(
                 functools.partial(step_kernel, step),
-                in_specs=[SMEM] + [VMEM] * 16,
-                out_specs=[VMEM] * 5,
-                out_shape=expand_out,
-                scratch_shapes=[total, pltpu.VMEM(table_shape, F32), group(6)] + expand_scratch,
-                compiler_params=params(16),
+                in_specs=[SMEM] + [VMEM] * 11,
+                out_specs=[VMEM] * 3,
+                out_shape=[group_shape(6)] + [col_shape] * 2,
+                scratch_shapes=[
+                    total, pltpu.VMEM(table_shape, F32), pltpu.VMEM((2, 3, 16, depth), F32)
+                ],
+                compiler_params=params(12),
                 name="step",
-            )(shift_codes, geo, dsum, *found, *ahead)
-
-    table = pl.pallas_call(
-        last_kernel,
-        in_specs=[VMEM] * 9,
-        out_specs=VMEM,
-        out_shape=shape(*table_shape),
-        scratch_shapes=[total],
-        compiler_params=params(6),
-        name="last",
-    )(*found)
-
+            )(shift_codes, geo, dsum, *found, geoup, geodn)
+
+    sem_count = rows * cols // 8
     return pl.pallas_call(
         particles_kernel,
-        grid=grid,
-        in_specs=[SMEM, VMEM, vec, vec, flat],
-        out_specs=vec,
+        in_specs=[SMEM] + [VMEM] * 10,
+        out_specs=HBM,
         out_shape=vec_shape,
-        scratch_shapes=[pltpu.VMEM((GROUPS, 6, 8, 128), F32)],
+        scratch_shapes=[
+            total, pltpu.VMEM(table_shape, F32), pltpu.VMEM((GROUPS, 6, 8, 128), F32),
+            pltpu.VMEM(vec_shape.shape, F32), pltpu.SemaphoreType.DMA((sem_count,)),
+        ],
         compiler_params=params(12),
         name="particles",
-    )(shift_codes, table, pos, hot, code)
+    )(shift_codes, *found, pos, hot, code)
 
 
 def solution(mesh):

time: 77.3 us -> 64.7 us (0.84)
  the two profiles are of different devices: /device:TPU:26 before, /device:TPU:102 now
where the time goes in v2:
time: 64.7 us; the launch traced here: 64.6 us
  waiting for transfers between devices  23.9 us (37%)
  Pallas kernels  23.1 us (36%)
  starting transfers between devices  17.4 us (27%)
    ppermute x12, waiting for transfers between devices, swap(): return lax.ppermute(value, axis, list(enumerate(partner)))  23.9 us
    ppermute x12, starting transfers between devices, swap(): return lax.ppermute(value, axis, list(enumerate(partner)))  17.4 us
    pallas_call x1, Pallas kernels, local(): pl.pallas_call(rest_sums_kernel, in_specs=[SMEM] + [VMEM] * 5, out_specs=...  4.68 us
    pallas_call x2, Pallas kernels, local(): pl.pallas_call(functools.partial(step_kernel, step), in_specs=[SMEM] + [V...  4.15 us
    pallas_call x1, Pallas kernels, local(): pl.pallas_call(near_sums_kernel, in_specs=[HBM] * 6, out_specs=[VMEM] * 8...  3.93 us
    pallas_call x2, Pallas kernels, change_sums(): pl.pallas_call(functools.partial(change_sums_kernel, step), in_specs=[VME...  3.81 us
    pallas_call x1, Pallas kernels, local(): pl.pallas_call(particles_kernel, in_specs=[SMEM] + [VMEM] * 10, out_specs...  2.89 us
    pallas_call x2, Pallas kernels, geometry(): pl.pallas_call(functools.partial(geometry_kernel, step), in_specs=[SMEM,...  1.88 us
  transfers between devices with their start and end apart: 12, of which 7 were waited for; matrix products, arithmetic and copies ran while one was open for 0% of the time, Pallas kernels for 19%

profile of v2, /device:TPU:102, one launch (start us, length us, event | category | flops | bytes accessed | tf_op | source)
XLA Modules:
  0.0 64.6 jit_solution(3514235281504670997)
XLA Ops:
  0.0 3.9 %near_sums.1 = (f32[3,12,2,16,256]{4,3,2,1,0:T(8,128)S(1)}, f32[3,12,2,16,256]{4,3,2,1,0:T(8,128)S(1)}, f32[3,12,2,16,256]{4,3,2,1,0:T(8,128)S(1)}, s32[12,2,16,...) custom-call(s32[3]{0:T(128)} %shifts.15, ...), custom_call_target="tpu_custom_call" | custom-call | tf_op jit(solution)/shard_map/near_sums/pallas_call | solution.py:515
  3.9 1.7 %collective-permute-start = (f32[3,16,256]{2,1,0:T(8,128)S(1)}, f32[3,16,256]{2,1,0:T(8,128)S(1)}, u32[]{:S(2)}, u32[]{:S(2)}) collective-permute-start(f32[3,16,256]{2,1,0:T(8,128)S(1)} %get-tuple-element.54), channel_id=1, source_target_pairs={{0,1},{1,0},{2,3},{3,2},{4,5},{5,4},{6,7},{7,6},{8,9},{9,8},{10,11... | collective-permute-start | bytes 147464 | tf_op jit(solution)/shard_map/ppermute | solution.py:537
  5.6 2.4 %collective-permute-start.1 = (f32[3,16,256]{2,1,0:T(8,128)S(1)}, f32[3,16,256]{2,1,0:T(8,128)S(1)}, u32[]{:S(2)}, u32[]{:S(2)}) collective-permute-start(f32[3,16,256]{2,1,0:T(8,128)S(1)} %get-tuple-element.55), channel_id=1, source_target_pairs={{0,7},{1,2},{2,1},{3,4},{4,3},{5,6},{6,5},{7,0},{8,15},{9,10},{10,... | collective-permute-start | bytes 147464 | tf_op jit(solution)/shard_map/ppermute | solution.py:537
  8.1 4.7 %rest_sums.1 = (f32[8,10,2,16,256]{4,3,2,1,0:T(8,128)S(1)}, f32[8,6,2,16,256]{4,3,2,1,0:T(8,128)}, f32[17,16,256]{2,1,0:T(8,128)S(1)}, f32[17,16,256]{2,1,0:T(8,128)S(1)}, f32[17,16,256]{2,1,0:T(8,128)S(1)}) custom-call(s32[3]{0:T(128)S(1)} %copy-done, f32[3,12,2,16,256]{4,3,2,1,0:T(8,128)S(1)} %get-tuple-element.45.pos, ...), custom_call_target="tpu_custom_call" | custom-call | tf_op jit(solution)/shard_map/rest_sums/pallas_call | solution.py:567
  12.7 0.1 fold.3
  12.8 0.1 collective-permute-start.2
  12.9 3.8 %collective-permute-start.3 = (f32[17,16,256]{2,1,0:T(8,128)S(1)}, f32[17,16,256]{2,1,0:T(8,128)S(1)}, u32[]{:S(2)}, u32[]{:S(2)}) collective-permute-start(f32[17,16,256]{2,1,0:T(8,128)S(1)} %get-tuple-element.58.near), channel_id=1, source_target_pairs={{0,8},{8,0},{16,24},{24,16},{32,40},{40,32},{48,56},{56,48},{64,72... | collective-permute-start | bytes 835592 | tf_op jit(solution)/shard_map/ppermute | solution.py:537
  16.7 0.9 %geometry.2 = (f32[17,16,256]{2,1,0:T(8,128)S(1)}, f32[17,16,256]{2,1,0:T(8,128)S(1)}, f32[17,16,256]{2,1,0:T(8,128)S(1)}, f32[3,16,256]{2,1,0:T(8,128)S(1)}, f32[3,16,256]{2,1,0:T(8,128)S(1)}) custom-call(s32[3]{0:T(128)S(1)} %copy-done, f32[8,10,2,16,256]{4,3,2,1,0:T(8,128)S(1)} %get-tuple-element.50.geo), custom_call_target="tpu_custom_call" | custom-call | tf_op jit(solution)/shard_map/geometry/pallas_call | solution.py:551
  17.6 1.9 %change_sums.3.dsum = f32[8,6,2,16,256]{4,3,2,1,0:T(8,128)S(1)} custom-call(f32[3,12,2,16,256]{4,3,2,1,0:T(8,128)S(1)} %get-tuple-element.45.pos, f32[3,12,2,16,256]{4,3,2,1,0:T(8,128)S(1)} %get-tuple-element.51.thermal, s32[12,2,16,256]{3,2,1,0:T(8,128)S(1)} %get-tuple-element.47.code), custom_call_target="tpu_custom_call" | custom-call | tf_op jit(solution)/shard_map/change_sums/pallas_call | solution.py:540
  19.5 3.8 %collective-permute-done.2.x_far = f32[17,16,256]{2,1,0:T(8,128)S(1)} collective-permute-done((f32[17,16,256]{2,1,0:T(8,128)S(1)}, f32[17,16,256]{2,1,0:T(8,128)S(1)}, u32[]{:S(2)}, u32[]{:S(2)}) %collective-permute-start.2) | collective-permute-done | bytes 278560 | tf_op jit(solution)/shard_map/ppermute | solution.py:537
  23.3 2.1 %step.2 = (f32[8,6,2,16,256]{4,3,2,1,0:T(8,128)S(1)}, f32[3,16,256]{2,1,0:T(8,128)S(1)}, f32[3,16,256]{2,1,0:T(8,128)S(1)}) custom-call(s32[3]{0:T(128)S(1)} %copy-done, f32[8,10,2,16,256]{4,3,2,1,0:T(8,128)S(1)} %get-tuple-element.50.geo, f32[8,6,2,16,256]{4,3,2,1,0:T(8,128)S(1)} %change_sums.3.dsum, f32[17,16,256]{2,1,0:T(8,128)S(1)} %get-tuple-element.56.far, ...), custom_call_target="tpu_custom_call" | custom-call | tf_op jit(solution)/shard_map/step/pallas_call | solution.py:600
  25.4 0.5 collective-permute-start.4
  25.9 1.4 %collective-permute-start.5 = (f32[3,16,256]{2,1,0:T(8,128)S(1)}, f32[3,16,256]{2,1,0:T(8,128)S(1)}, u32[]{:S(2)}, u32[]{:S(2)}) collective-permute-start(f32[3,16,256]{2,1,0:T(8,128)S(1)} %get-tuple-element.68), channel_id=1, source_target_pairs={{0,7},{1,2},{2,1},{3,4},{4,3},{5,6},{6,5},{7,0},{8,15},{9,10},{10,... | collective-permute-start | bytes 147464 | tf_op jit(solution)/shard_map/ppermute | solution.py:537
  27.3 0.8 %rows.2 = (f32[17,16,256]{2,1,0:T(8,128)S(1)}, f32[17,16,256]{2,1,0:T(8,128)S(1)}, f32[17,16,256]{2,1,0:T(8,128)S(1)}) custom-call(s32[3]{0:T(128)S(1)} %copy-done, f32[8,6,2,16,256]{4,3,2,1,0:T(8,128)S(1)} %get-tuple-element.61.wsum, f32[17,16,256]{2,1,0:T(8,128)S(1)} %get-tuple-element.62.geo0, f32[17,16,256]{2,1,0:T(8,128)S(1)} %get-tuple-element.63.geo1, ...), custom_call_target="tpu_custom_call" | custom-call | tf_op jit(solution)/shard_map/rows/pallas_call | solution.py:577
  28.1 1.5 %collective-permute-done.4.y_in = f32[3,16,256]{2,1,0:T(8,128)S(1)} collective-permute-done((f32[3,16,256]{2,1,0:T(8,128)S(1)}, f32[3,16,256]{2,1,0:T(8,128)S(1)}, u32[]{:S(2)}, u32[]{:S(2)}) %collective-permute-start.4) | collective-permute-done | bytes 49184 | tf_op jit(solution)/shard_map/ppermute | solution.py:537
  29.6 2.5 %collective-permute-done.5.y_out = f32[3,16,256]{2,1,0:T(8,128)S(1)} collective-permute-done((f32[3,16,256]{2,1,0:T(8,128)S(1)}, f32[3,16,256]{2,1,0:T(8,128)S(1)}, u32[]{:S(2)}, u32[]{:S(2)}) %collective-permute-start.5) | collective-permute-done | bytes 49184 | tf_op jit(solution)/shard_map/ppermute | solution.py:537
  32.1 0.1 fold.4
  32.2 0.3 collective-permute-start.6
  32.5 3.3 %collective-permute-start.7 = (f32[17,16,256]{2,1,0:T(8,128)S(1)}, f32[17,16,256]{2,1,0:T(8,128)S(1)}, u32[]{:S(2)}, u32[]{:S(2)}) collective-permute-start(f32[17,16,256]{2,1,0:T(8,128)S(1)} %get-tuple-element.71.near), channel_id=1, source_target_pairs={{0,8},{8,0},{16,24},{24,16},{32,40},{40,32},{48,56},{56,48},{64,72... | collective-permute-start | bytes 835592 | tf_op jit(solution)/shard_map/ppermute | solution.py:537
  35.8 0.9 %geometry.3 = (f32[17,16,256]{2,1,0:T(8,128)S(1)}, f32[17,16,256]{2,1,0:T(8,128)S(1)}, f32[17,16,256]{2,1,0:T(8,128)S(1)}, f32[3,16,256]{2,1,0:T(8,128)S(1)}, f32[3,16,256]{2,1,0:T(8,128)S(1)}) custom-call(s32[3]{0:T(128)S(1)} %copy-done, f32[8,10,2,16,256]{4,3,2,1,0:T(8,128)S(1)} %get-tuple-element.50.geo), custom_call_target="tpu_custom_call" | custom-call | tf_op jit(solution)/shard_map/geometry/pallas_call | solution.py:551
  36.7 1.9 %change_sums.2.dsum = f32[8,6,2,16,256]{4,3,2,1,0:T(8,128)S(1)} custom-call(f32[3,12,2,16,256]{4,3,2,1,0:T(8,128)S(1)} %get-tuple-element.45.pos, f32[3,12,2,16,256]{4,3,2,1,0:T(8,128)S(1)} %get-tuple-element.51.thermal, s32[12,2,16,256]{3,2,1,0:T(8,128)S(1)} %get-tuple-element.47.code), custom_call_target="tpu_custom_call" | custom-call | tf_op jit(solution)/shard_map/change_sums/pallas_call | solution.py:540
  38.6 4.3 %collective-permute-done.6.x_far = f32[17,16,256]{2,1,0:T(8,128)S(1)} collective-permute-done((f32[17,16,256]{2,1,0:T(8,128)S(1)}, f32[17,16,256]{2,1,0:T(8,128)S(1)}, u32[]{:S(2)}, u32[]{:S(2)}) %collective-permute-start.6) | collective-permute-done | bytes 278560 | tf_op jit(solution)/shard_map/ppermute | solution.py:537
  42.9 2.1 %step.3 = (f32[8,6,2,16,256]{4,3,2,1,0:T(8,128)S(1)}, f32[3,16,256]{2,1,0:T(8,128)S(1)}, f32[3,16,256]{2,1,0:T(8,128)S(1)}) custom-call(s32[3]{0:T(128)S(1)} %copy-done, f32[8,10,2,16,256]{4,3,2,1,0:T(8,128)S(1)} %get-tuple-element.50.geo, f32[8,6,2,16,256]{4,3,2,1,0:T(8,128)S(1)} %change_sums.2.dsum, f32[17,16,256]{2,1,0:T(8,128)S(1)} %get-tuple-element.69.far, ...), custom_call_target="tpu_custom_call" | custom-call | tf_op jit(solution)/shard_map/step/pallas_call | solution.py:600
  45.0 0.1 collective-permute-start.8
  45.1 1.1 %collective-permute-start.9 = (f32[3,16,256]{2,1,0:T(8,128)S(1)}, f32[3,16,256]{2,1,0:T(8,128)S(1)}, u32[]{:S(2)}, u32[]{:S(2)}) collective-permute-start(f32[3,16,256]{2,1,0:T(8,128)S(1)} %get-tuple-element.81), channel_id=1, source_target_pairs={{0,7},{1,2},{2,1},{3,4},{4,3},{5,6},{6,5},{7,0},{8,15},{9,10},{10,... | collective-permute-start | bytes 147464 | tf_op jit(solution)/shard_map/ppermute | solution.py:537
  46.2 0.8 %rows.3 = (f32[17,16,256]{2,1,0:T(8,128)S(1)}, f32[17,16,256]{2,1,0:T(8,128)S(1)}, f32[17,16,256]{2,1,0:T(8,128)S(1)}) custom-call(s32[3]{0:T(128)S(1)} %copy-done, f32[8,6,2,16,256]{4,3,2,1,0:T(8,128)S(1)} %get-tuple-element.74.wsum, f32[17,16,256]{2,1,0:T(8,128)S(1)} %get-tuple-element.75.geo0, f32[17,16,256]{2,1,0:T(8,128)S(1)} %get-tuple-element.76.geo1, ...), custom_call_target="tpu_custom_call" | custom-call | tf_op jit(solution)/shard_map/rows/pallas_call | solution.py:577
  47.0 2.2 %collective-permute-done.8.y_in = f32[3,16,256]{2,1,0:T(8,128)S(1)} collective-permute-done((f32[3,16,256]{2,1,0:T(8,128)S(1)}, f32[3,16,256]{2,1,0:T(8,128)S(1)}, u32[]{:S(2)}, u32[]{:S(2)}) %collective-permute-start.8) | collective-permute-done | bytes 49184 | tf_op jit(solution)/shard_map/ppermute | solution.py:537
  49.2 2.2 %collective-permute-done.9.y_out = f32[3,16,256]{2,1,0:T(8,128)S(1)} collective-permute-done((f32[3,16,256]{2,1,0:T(8,128)S(1)}, f32[3,16,256]{2,1,0:T(8,128)S(1)}, u32[]{:S(2)}, u32[]{:S(2)}) %collective-permute-start.9) | collective-permute-done | bytes 49184 | tf_op jit(solution)/shard_map/ppermute | solution.py:537
  51.4 0.1 collective-permute-start.10
  51.5 2.6 %collective-permute-start.11 = (f32[17,16,256]{2,1,0:T(8,128)S(1)}, f32[17,16,256]{2,1,0:T(8,128)S(1)}, u32[]{:S(2)}, u32[]{:S(2)}) collective-permute-start(f32[17,16,256]{2,1,0:T(8,128)S(1)} %get-tuple-element.84.near), channel_id=1, source_target_pairs={{0,8},{8,0},{16,24},{24,16},{32,40},{40,32},{48,56},{56,48},{64,72... | collective-permute-start | bytes 835592 | tf_op jit(solution)/shard_map/ppermute | solution.py:537
  54.2 7.4 %collective-permute-done.10.x_far = f32[17,16,256]{2,1,0:T(8,128)S(1)} collective-permute-done((f32[17,16,256]{2,1,0:T(8,128)S(1)}, f32[17,16,256]{2,1,0:T(8,128)S(1)}, u32[]{:S(2)}, u32[]{:S(2)}) %collective-permute-start.10) | collective-permute-done | bytes 278560 | tf_op jit(solution)/shard_map/ppermute | solution.py:537
  61.6 2.9 %particles.1 = f32[3,12,2,16,256]{4,3,2,1,0:T(8,128)} custom-call(s32[3]{0:T(128)S(1)} %copy-done, f32[17,16,256]{2,1,0:T(8,128)S(1)} %get-tuple-element.82.far, f32[17,16,256]{2,1,0:T(8,128)S(1)} %get-tuple-element.83.mid, f32[17,16,256]{2,1,0:T(8,128)S(1)} %get-tuple-element.84.near, f32[3,16,256]{2,1,0:T(8,128)S(1)} %collective-permute-done.8.y_in, ...), custom_call_target="tpu_custom_call" | custom-call | tf_op jit(solution)/shard_map/particles/pallas_call | solution.py:613
  (8 shorter events, 0.1 us)
Async XLA Ops:
  0.0 8.0 %copy-start = (s32[3]{0:T(128)S(1)}, s32[3]{0:T(128)}, u32[]{:S(2)}) copy-start(s32[3]{0:T(128)} %shifts.15) | copy-start | bytes 40
  3.9 8.8 %collective-permute-start = (f32[3,16,256]{2,1,0:T(8,128)S(1)}, f32[3,16,256]{2,1,0:T(8,128)S(1)}, u32[]{:S(2)}, u32[]{:S(2)}) collective-permute-start(f32[3,16,256]{2,1,0:T(8,128)S(1)} %get-tuple-element.54), channel_id=1, source_target_pairs={{0,1},{1,0},{2,3},{3,2},{4,5},{5,4},{6,7},{7,6},{8,9},{9,8},{10,11... | collective-permute-start | bytes 147464 | tf_op jit(solution)/shard_map/ppermute | solution.py:537
  5.6 7.1 %collective-permute-start.1 = (f32[3,16,256]{2,1,0:T(8,128)S(1)}, f32[3,16,256]{2,1,0:T(8,128)S(1)}, u32[]{:S(2)}, u32[]{:S(2)}) collective-permute-start(f32[3,16,256]{2,1,0:T(8,128)S(1)} %get-tuple-element.55), channel_id=1, source_target_pairs={{0,7},{1,2},{2,1},{3,4},{4,3},{5,6},{6,5},{7,0},{8,15},{9,10},{10,... | collective-permute-start | bytes 147464 | tf_op jit(solution)/shard_map/ppermute | solution.py:537
  12.8 10.5 %collective-permute-start.2 = (f32[17,16,256]{2,1,0:T(8,128)S(1)}, f32[17,16,256]{2,1,0:T(8,128)S(1)}, u32[]{:S(2)}, u32[]{:S(2)}) collective-permute-start(f32[17,16,256]{2,1,0:T(8,128)S(1)} %get-tuple-element.56.far), channel_id=1, source_target_pairs={{0,248},{8,16},{16,8},{24,32},{32,24},{40,48},{48,40},{56,64},{64,... | collective-permute-start | bytes 835592 | tf_op jit(solution)/shard_map/ppermute | solution.py:537
  12.9 10.5 %collective-permute-start.3 = (f32[17,16,256]{2,1,0:T(8,128)S(1)}, f32[17,16,256]{2,1,0:T(8,128)S(1)}, u32[]{:S(2)}, u32[]{:S(2)}) collective-permute-start(f32[17,16,256]{2,1,0:T(8,128)S(1)} %get-tuple-element.58.near), channel_id=1, source_target_pairs={{0,8},{8,0},{16,24},{24,16},{32,40},{40,32},{48,56},{56,48},{64,72... | collective-permute-start | bytes 835592 | tf_op jit(solution)/shard_map/ppermute | solution.py:537
  25.4 4.2 %collective-permute-start.4 = (f32[3,16,256]{2,1,0:T(8,128)S(1)}, f32[3,16,256]{2,1,0:T(8,128)S(1)}, u32[]{:S(2)}, u32[]{:S(2)}) collective-permute-start(f32[3,16,256]{2,1,0:T(8,128)S(1)} %get-tuple-element.67), channel_id=1, source_target_pairs={{0,1},{1,0},{2,3},{3,2},{4,5},{5,4},{6,7},{7,6},{8,9},{9,8},{10,11... | collective-permute-start | bytes 147464 | tf_op jit(solution)/shard_map/ppermute | solution.py:537
  25.9 6.2 %collective-permute-start.5 = (f32[3,16,256]{2,1,0:T(8,128)S(1)}, f32[3,16,256]{2,1,0:T(8,128)S(1)}, u32[]{:S(2)}, u32[]{:S(2)}) collective-permute-start(f32[3,16,256]{2,1,0:T(8,128)S(1)} %get-tuple-element.68), channel_id=1, source_target_pairs={{0,7},{1,2},{2,1},{3,4},{4,3},{5,6},{6,5},{7,0},{8,15},{9,10},{10,... | collective-permute-start | bytes 147464 | tf_op jit(solution)/shard_map/ppermute | solution.py:537
  32.2 10.7 %collective-permute-start.6 = (f32[17,16,256]{2,1,0:T(8,128)S(1)}, f32[17,16,256]{2,1,0:T(8,128)S(1)}, u32[]{:S(2)}, u32[]{:S(2)}) collective-permute-start(f32[17,16,256]{2,1,0:T(8,128)S(1)} %get-tuple-element.69.far), channel_id=1, source_target_pairs={{0,248},{8,16},{16,8},{24,32},{32,24},{40,48},{48,40},{56,64},{64,... | collective-permute-start | bytes 835592 | tf_op jit(solution)/shard_map/ppermute | solution.py:537
  32.5 10.5 %collective-permute-start.7 = (f32[17,16,256]{2,1,0:T(8,128)S(1)}, f32[17,16,256]{2,1,0:T(8,128)S(1)}, u32[]{:S(2)}, u32[]{:S(2)}) collective-permute-start(f32[17,16,256]{2,1,0:T(8,128)S(1)} %get-tuple-element.71.near), channel_id=1, source_target_pairs={{0,8},{8,0},{16,24},{24,16},{32,40},{40,32},{48,56},{56,48},{64,72... | collective-permute-start | bytes 835592 | tf_op jit(solution)/shard_map/ppermute | solution.py:537
  45.0 4.2 %collective-permute-start.8 = (f32[3,16,256]{2,1,0:T(8,128)S(1)}, f32[3,16,256]{2,1,0:T(8,128)S(1)}, u32[]{:S(2)}, u32[]{:S(2)}) collective-permute-start(f32[3,16,256]{2,1,0:T(8,128)S(1)} %get-tuple-element.80), channel_id=1, source_target_pairs={{0,1},{1,0},{2,3},{3,2},{4,5},{5,4},{6,7},{7,6},{8,9},{9,8},{10,11... | collective-permute-start | bytes 147464 | tf_op jit(solution)/shard_map/ppermute | solution.py:537
  45.1 6.3 %collective-permute-start.9 = (f32[3,16,256]{2,1,0:T(8,128)S(1)}, f32[3,16,256]{2,1,0:T(8,128)S(1)}, u32[]{:S(2)}, u32[]{:S(2)}) collective-permute-start(f32[3,16,256]{2,1,0:T(8,128)S(1)} %get-tuple-element.81), channel_id=1, source_target_pairs={{0,7},{1,2},{2,1},{3,4},{4,3},{5,6},{6,5},{7,0},{8,15},{9,10},{10,... | collective-permute-start | bytes 147464 | tf_op jit(solution)/shard_map/ppermute | solution.py:537
  51.4 10.1 %collective-permute-start.10 = (f32[17,16,256]{2,1,0:T(8,128)S(1)}, f32[17,16,256]{2,1,0:T(8,128)S(1)}, u32[]{:S(2)}, u32[]{:S(2)}) collective-permute-start(f32[17,16,256]{2,1,0:T(8,128)S(1)} %get-tuple-element.82.far), channel_id=1, source_target_pairs={{0,248},{8,16},{16,8},{24,32},{32,24},{40,48},{48,40},{56,64},{64,... | collective-permute-start | bytes 835592 | tf_op jit(solution)/shard_map/ppermute | solution.py:537
  51.5 10.0 %collective-permute-start.11 = (f32[17,16,256]{2,1,0:T(8,128)S(1)}, f32[17,16,256]{2,1,0:T(8,128)S(1)}, u32[]{:S(2)}, u32[]{:S(2)}) collective-permute-start(f32[17,16,256]{2,1,0:T(8,128)S(1)} %get-tuple-element.84.near), channel_id=1, source_target_pairs={{0,8},{8,0},{16,24},{24,16},{32,40},{40,32},{48,56},{56,48},{64,72... | collective-permute-start | bytes 835592 | tf_op jit(solution)/shard_map/ppermute | solution.py:537

commit v3 on v2

--- a/solution.py
+++ b/solution.py
@@ -335,13 +335,14 @@
     return [drift[c] - turned[c] for c in range(3)] + spin
 
 
-def fill_table(own, around, table, total):
+def fill_table(own, around, table, total, which):
     far, mid, near = own
     y_in, y_out, x_far, x_near = around
-    cols = mid.shape[1]
+    cols = (mid if far is None else far).shape[1]
     even = is_even("gx")
-    complete_row(mid, *y_parts(y_in, y_out, 1), total)
-    for r in range(3):
+    if 1 in which:
+        complete_row(mid, *y_parts(y_in, y_out, 1), total)
+    for r in which:
         if r == 1:
             read = lambda v, at: total[v, at, :]
         else:
@@ -373,12 +374,17 @@
     return a
 
 
-def update_groups(geo, dsum, shift, table, wsum):
+def update_groups(geo, dsum, shift, table, wsum, inner, done=None):
     cols = geo.shape[3]
     for code in range(GROUPS):
         bx, by, bz = bits(code)
         o = code ^ shift
         for row in range(2):
+            if (bx == row) != inner:
+                if done is not None:
+                    for c in range(6):
+                        wsum[o, c, row] = done[o, c, row]
+                continue
             for t in range(cols // 8):
                 at = pl.ds(8 * t, 8)
                 from_col = 8 + 8 * t - by
@@ -401,12 +407,12 @@
 
 
 def step_kernel(
-    step, shifts, geo, dsum, far, mid, near, y_in, y_out, x_far, x_near, geoup, geodn,
-    wsum, next_in, next_out, total, table, ends,
+    step, shifts, geo, dsum, far, near, x_far, x_near, geoup, geodn, done,
+    wsum, next_in, next_out, table, ends,
 ):
-    cols = mid.shape[1]
-    fill_table((far, mid, near), (y_in, y_out, x_far, x_near), table, total)
-    update_groups(geo, dsum, shifts[step], table, wsum)
+    cols = far.shape[1]
+    fill_table((far, None, near), (None, None, x_far, x_near), table, None, (0, 2))
+    update_groups(geo, dsum, shifts[step], table, wsum, False, done)
     for bz in range(2):
         for r in range(3):
             ends[bz, r] = jnp.zeros_like(ends[bz, r])
@@ -418,6 +424,11 @@
         up_r, down_r = geoup[r] + up[r], geodn[r] + down[r]
         next_in[r] = jnp.where(even, up_r, down_r)
         next_out[r] = jnp.where(even, down_r, up_r)
+
+
+def inner_step_kernel(step, shifts, geo, dsum, mid, y_in, y_out, wsum, total, table):
+    fill_table((None, mid, None), (y_in, y_out, None, None), table, total, (1,))
+    update_groups(geo, dsum, shifts[step], table, wsum, True)
 
 
 def rows_kernel(
@@ -434,44 +445,79 @@
     by_role(is_even("gx"), low, high, far, near)
 
 
+def particle_block(shift, table, pos, thermal, code, variants, bx, row, tile, lanes, store):
+    slots = code.shape[0]
+    at = pl.ds(8 * tile, 8)
+    for low in range(4):
+        by, bz = low // 2, low % 2
+        first = 8 + 8 * tile - by
+        values = [table[bz, v, row + 1 - bx, first : first + 8, lanes] for v in range(6)]
+        values[:3] = shift_a(values[:3], values[3:], (bx, by, bz))
+        for v in range(6):
+            variants[low, v] = values[v]
+    for begin in range(0, slots, 4):
+        block = range(begin, min(begin + 4, slots))
+        base = [code[slot, row, at, lanes] for slot in block]
+        k = [value ^ shift for value in base]
+        isy = [(value & 2) != 0 for value in k]
+        isz = [(value & 1) != 0 for value in k]
+        state = [[] for _ in block]
+        for v in range(6):
+            four_ = [variants[low, v] for low in range(4)]
+            for index in range(len(block)):
+                lower = jnp.where(isy[index], four_[2], four_[0])
+                upper = jnp.where(isy[index], four_[3], four_[1])
+                state[index].append(jnp.where(isz[index], upper, lower))
+        for index, slot in enumerate(block):
+            mine = ((k[index] & 4) == 4 * bx) & (base[index] < GROUPS)
+            turn = cross(state[index][3:], [pos[c, slot, row, at, lanes] for c in range(3)])
+            hot = [thermal[c, (slot + STEPS - 1) % slots, row, at, lanes] for c in range(3)]
+            store(slot, mine, [hot[c] + (state[index][c] + turn[c]) for c in range(3)])
+
+
+def inner_particles_kernel(
+    shifts, mid, y_in, y_out, pos, thermal, code, inner, total, table, variants
+):
+    _, rows, cols, depth = code.shape
+    fill_table((None, mid, None), (y_in, y_out, None, None), table, total, (1,))
+    for row in range(rows):
+        for tile in range(cols // 8):
+            at = pl.ds(8 * tile, 8)
+            for lanes in halves(depth):
+
+                def store(slot, mine, new):
+                    for c in range(3):
+                        inner[c, slot, row, at, lanes] = jnp.where(mine, new[c], 0.0)
+
+                particle_block(
+                    shifts[STEPS - 1], table, pos, thermal, code, variants, row, row, tile, lanes, store
+                )
+
+
 def particles_kernel(
-    shifts, far, mid, near, y_in, y_out, x_far, x_near, pos, thermal, code,
-    out, total, table, variants, fresh, sems,
+    shifts, far, near, x_far, x_near, pos, thermal, code, inner,
+    out, table, variants, fresh, sems,
 ):
-    slots, rows, cols, depth = code.shape
-    fill_table((far, mid, near), (y_in, y_out, x_far, x_near), table, total)
+    _, rows, cols, depth = code.shape
+    fill_table((far, None, near), (None, None, x_far, x_near), table, None, (0, 2))
     copies = []
     for row in range(rows):
         for tile in range(cols // 8):
             at = pl.ds(8 * tile, 8)
             for lanes in halves(depth):
-                for frame in range(GROUPS):
-                    bx, by, bz = bits(frame)
-                    first = 8 + 8 * tile - by
-                    values = [
-                        table[bz, v, row + 1 - bx, first : first + 8, lanes] for v in range(6)
-                    ]
-                    values[:3] = shift_a(values[:3], values[3:], (bx, by, bz))
-                    for v in range(6):
-                        variants[frame, v] = values[v]
-                for slot in range(slots):
-                    base = code[slot, row, at, lanes]
-                    k = base ^ shifts[STEPS - 1]
-                    isx, isy, isz = (k & 4) != 0, (k & 2) != 0, (k & 1) != 0
-                    used = base < GROUPS
-                    state = []
-                    for v in range(6):
-                        level = [jnp.where(isx, variants[4 + i, v], variants[i, v]) for i in range(4)]
-                        level = [jnp.where(isy, level[2 + i], level[i]) for i in range(2)]
-                        state.append(jnp.where(isz, level[1], level[0]))
-                    turn = cross(state[3:], [pos[c, slot, row, at, lanes] for c in range(3)])
+
+                def store(slot, mine, new):
                     for c in range(3):
-                        hot = thermal[c, (slot + STEPS - 1) % slots, row, at, lanes]
-                        new = hot + (state[c] + turn[c])
-                        fresh[c, slot, row, at, lanes] = jnp.where(used, new, 0.0)
-            index = len(copies)
+                        fresh[c, slot, row, at, lanes] = jnp.where(
+                            mine, new[c], inner[c, slot, row, at, lanes]
+                        )
+
+                particle_block(
+                    shifts[STEPS - 1], table, pos, thermal, code, variants, 1 - row, row, tile, lanes,
+                    store,
+                )
             copy = pltpu.make_async_copy(
-                fresh.at[:, :, row, at, :], out.at[:, :, row, at, :], sems.at[index]
+                fresh.at[:, :, row, at, :], out.at[:, :, row, at, :], sems.at[len(copies)]
             )
             copy.start()
             copies.append(copy)
@@ -593,35 +639,52 @@
         )(far, near, got_in, got_out)
         x_far = swap(far, "gx", 1)
         x_near = swap(near, "gx", 0)
-        found = (far, mid, near, got_in, got_out, x_far, x_near)
+        found = (far, near, x_far, x_near)
+        inner_scratch = [total, pltpu.VMEM(table_shape, F32)]
         if step + 1 < STEPS:
             dsum = change_sums(step)
             *ahead, geoup, geodn = geometry(step + 1)
+            done = pl.pallas_call(
+                functools.partial(inner_step_kernel, step),
+                in_specs=[SMEM] + [VMEM] * 5,
+                out_specs=VMEM,
+                out_shape=group_shape(6),
+                scratch_shapes=inner_scratch,
+                compiler_params=params(8),
+                name="inner_step",
+            )(shift_codes, geo, dsum, mid, got_in, got_out)
             wsum, y_in, y_out = pl.pallas_call(
                 functools.partial(step_kernel, step),
-                in_specs=[SMEM] + [VMEM] * 11,
+                in_specs=[SMEM] + [VMEM] * 9,
                 out_specs=[VMEM] * 3,
                 out_shape=[group_shape(6)] + [col_shape] * 2,
-                scratch_shapes=[
-                    total, pltpu.VMEM(table_shape, F32), pltpu.VMEM((2, 3, 16, depth), F32)
-                ],
+                scratch_shapes=[pltpu.VMEM(table_shape, F32), pltpu.VMEM((2, 3, 16, depth), F32)],
                 compiler_params=params(12),
                 name="step",
-            )(shift_codes, geo, dsum, *found, geoup, geodn)
-
-    sem_count = rows * cols // 8
+            )(shift_codes, geo, dsum, *found, geoup, geodn, done)
+        else:
+            inner = pl.pallas_call(
+                inner_particles_kernel,
+                in_specs=[SMEM] + [VMEM] * 6,
+                out_specs=VMEM,
+                out_shape=vec_shape,
+                scratch_shapes=inner_scratch + [pltpu.VMEM((4, 6, 8, 128), F32)],
+                compiler_params=params(8),
+                name="inner_particles",
+            )(shift_codes, mid, got_in, got_out, pos, hot, code)
+
     return pl.pallas_call(
         particles_kernel,
-        in_specs=[SMEM] + [VMEM] * 10,
+        in_specs=[SMEM] + [VMEM] * 8,
         out_specs=HBM,
         out_shape=vec_shape,
         scratch_shapes=[
-            total, pltpu.VMEM(table_shape, F32), pltpu.VMEM((GROUPS, 6, 8, 128), F32),
-            pltpu.VMEM(vec_shape.shape, F32), pltpu.SemaphoreType.DMA((sem_count,)),
+            pltpu.VMEM(table_shape, F32), pltpu.VMEM((4, 6, 8, 128), F32),
+            pltpu.VMEM(vec_shape.shape, F32), pltpu.SemaphoreType.DMA((rows * cols // 8,)),
         ],
         compiler_params=params(12),
         name="particles",
-    )(shift_codes, *found, pos, hot, code)
+    )(shift_codes, *found, pos, hot, code, inner)
 
 
 def solution(mesh):

time: 64.7 us -> 63.6 us (0.983)
  waiting for transfers between devices: 23.9 us -> 20.3 us
  Pallas kernels: 23.1 us -> 25.6 us
    ppermute x12, waiting for transfers between devices: 23.9 us -> 20.3 us  [swap(): return lax.ppermute(value, axis, list(enumerate(partner)))]
    pallas_call x1 -> x4, Pallas kernels: 2.89 us -> 6.42 us  [the longest x1 2.86 us: local(): pl.pallas_call(particles_kernel, in_specs=[SMEM] + [VMEM] * 8, out_specs=...]
    pallas_call x2, Pallas kernels: 4.15 us -> 3.09 us  [local(): pl.pallas_call(functools.partial(step_kernel, step), in_specs=[SMEM] + [V...]
  transfers between devices with their start and end apart: 12 -> 12, of which waited for: 7 -> 7; matrix products, arithmetic and copies ran while one was open for 0% -> 0% of each run, Pallas kernels for 19% -> 24%
where the time goes in v3:
time: 63.6 us; the launch traced here: 63.5 us
  Pallas kernels  25.6 us (40%)
  waiting for transfers between devices  20.3 us (32%)
  starting transfers between devices  17.4 us (27%)
    ppermute x12, waiting for transfers between devices, swap(): return lax.ppermute(value, axis, list(enumerate(partner)))  20.3 us
    ppermute x12, starting transfers between devices, swap(): return lax.ppermute(value, axis, list(enumerate(partner)))  17.4 us
    pallas_call x1, Pallas kernels, local(): pl.pallas_call(rest_sums_kernel, in_specs=[SMEM] + [VMEM] * 5, out_specs=...  4.68 us
    pallas_call x1, Pallas kernels, local(): pl.pallas_call(near_sums_kernel, in_specs=[HBM] * 6, out_specs=[VMEM] * 8...  3.93 us
    pallas_call x2, Pallas kernels, change_sums(): pl.pallas_call(functools.partial(change_sums_kernel, step), in_specs=[VME...  3.81 us
    pallas_call x2, Pallas kernels, local(): pl.pallas_call(functools.partial(step_kernel, step), in_specs=[SMEM] + [V...  3.09 us
    pallas_call x1, Pallas kernels, local(): pl.pallas_call(particles_kernel, in_specs=[SMEM] + [VMEM] * 8, out_specs=...  2.86 us
    pallas_call x2, Pallas kernels, local(): pl.pallas_call(functools.partial(inner_step_kernel, step), in_specs=[SMEM...  2.19 us
  transfers between devices with their start and end apart: 12, of which 7 were waited for; matrix products, arithmetic and copies ran while one was open for 0% of the time, Pallas kernels for 24%

profile of v3, /device:TPU:102, one launch (start us, length us, event | category | flops | bytes accessed | tf_op | source)
XLA Modules:
  0.0 63.5 jit_solution(17294484025869581448)
XLA Ops:
  0.0 3.9 %near_sums.1 = (f32[3,12,2,16,256]{4,3,2,1,0:T(8,128)S(1)}, f32[3,12,2,16,256]{4,3,2,1,0:T(8,128)S(1)}, f32[3,12,2,16,256]{4,3,2,1,0:T(8,128)S(1)}, s32[12,2,16,...) custom-call(s32[3]{0:T(128)} %shifts.21, ...), custom_call_target="tpu_custom_call" | custom-call | tf_op jit(solution)/shard_map/near_sums/pallas_call | solution.py:561
  3.9 1.7 %collective-permute-start = (f32[3,16,256]{2,1,0:T(8,128)S(1)}, f32[3,16,256]{2,1,0:T(8,128)S(1)}, u32[]{:S(2)}, u32[]{:S(2)}) collective-permute-start(f32[3,16,256]{2,1,0:T(8,128)S(1)} %get-tuple-element.54), channel_id=1, source_target_pairs={{0,1},{1,0},{2,3},{3,2},{4,5},{5,4},{6,7},{7,6},{8,9},{9,8},{10,11... | collective-permute-start | bytes 147464 | tf_op jit(solution)/shard_map/ppermute | solution.py:583
  5.6 2.4 %collective-permute-start.1 = (f32[3,16,256]{2,1,0:T(8,128)S(1)}, f32[3,16,256]{2,1,0:T(8,128)S(1)}, u32[]{:S(2)}, u32[]{:S(2)}) collective-permute-start(f32[3,16,256]{2,1,0:T(8,128)S(1)} %get-tuple-element.55), channel_id=1, source_target_pairs={{0,7},{1,2},{2,1},{3,4},{4,3},{5,6},{6,5},{7,0},{8,15},{9,10},{10,... | collective-permute-start | bytes 147464 | tf_op jit(solution)/shard_map/ppermute | solution.py:583
  8.1 4.7 %rest_sums.1 = (f32[8,10,2,16,256]{4,3,2,1,0:T(8,128)S(1)}, f32[8,6,2,16,256]{4,3,2,1,0:T(8,128)}, f32[17,16,256]{2,1,0:T(8,128)S(1)}, f32[17,16,256]{2,1,0:T(8,128)S(1)}, f32[17,16,256]{2,1,0:T(8,128)S(1)}) custom-call(s32[3]{0:T(128)S(1)} %copy-done, f32[3,12,2,16,256]{4,3,2,1,0:T(8,128)S(1)} %get-tuple-element.45.pos, ...), custom_call_target="tpu_custom_call" | custom-call | tf_op jit(solution)/shard_map/rest_sums/pallas_call | solution.py:613
  12.8 0.1 collective-permute-start.2
  12.9 3.8 %collective-permute-start.3 = (f32[17,16,256]{2,1,0:T(8,128)S(1)}, f32[17,16,256]{2,1,0:T(8,128)S(1)}, u32[]{:S(2)}, u32[]{:S(2)}) collective-permute-start(f32[17,16,256]{2,1,0:T(8,128)S(1)} %get-tuple-element.57.near), channel_id=1, source_target_pairs={{0,8},{8,0},{16,24},{24,16},{32,40},{40,32},{48,56},{56,48},{64,72... | collective-permute-start | bytes 835592 | tf_op jit(solution)/shard_map/ppermute | solution.py:583
  16.7 0.9 %geometry.2 = (f32[17,16,256]{2,1,0:T(8,128)S(1)}, f32[17,16,256]{2,1,0:T(8,128)S(1)}, f32[17,16,256]{2,1,0:T(8,128)S(1)}, f32[3,16,256]{2,1,0:T(8,128)S(1)}, f32[3,16,256]{2,1,0:T(8,128)S(1)}) custom-call(s32[3]{0:T(128)S(1)} %copy-done, f32[8,10,2,16,256]{4,3,2,1,0:T(8,128)S(1)} %get-tuple-element.50.geo), custom_call_target="tpu_custom_call" | custom-call | tf_op jit(solution)/shard_map/geometry/pallas_call | solution.py:597
  17.6 1.9 %change_sums.3.dsum = f32[8,6,2,16,256]{4,3,2,1,0:T(8,128)S(1)} custom-call(f32[3,12,2,16,256]{4,3,2,1,0:T(8,128)S(1)} %get-tuple-element.45.pos, f32[3,12,2,16,256]{4,3,2,1,0:T(8,128)S(1)} %get-tuple-element.51.thermal, s32[12,2,16,256]{3,2,1,0:T(8,128)S(1)} %get-tuple-element.47.code), custom_call_target="tpu_custom_call" | custom-call | tf_op jit(solution)/shard_map/change_sums/pallas_call | solution.py:586
  19.5 1.1 %inner_step.2.done = f32[8,6,2,16,256]{4,3,2,1,0:T(8,128)S(1)} custom-call(s32[3]{0:T(128)S(1)} %copy-done, f32[8,10,2,16,256]{4,3,2,1,0:T(8,128)S(1)} %get-tuple-element.50.geo, f32[8,6,2,16,256]{4,3,2,1,0:T(8,128)S(1)} %change_sums.3.dsum, f32[17,16,256]{2,1,0:T(8,128)S(1)} %get-tuple-element.60.mid, f32[3,16,256]{2,1,0:T(8,128)S(1)} %collective-permute-done.y_in, ...), custom_call_target="tpu_custom_call" | custom-call | tf_op jit(solution)/shard_map/inner_step/pallas_call | solution.py:647
  20.6 2.7 %collective-permute-done.2.x_far = f32[17,16,256]{2,1,0:T(8,128)S(1)} collective-permute-done((f32[17,16,256]{2,1,0:T(8,128)S(1)}, f32[17,16,256]{2,1,0:T(8,128)S(1)}, u32[]{:S(2)}, u32[]{:S(2)}) %collective-permute-start.2) | collective-permute-done | bytes 278560 | tf_op jit(solution)/shard_map/ppermute | solution.py:583
  23.4 1.5 %step.2 = (f32[8,6,2,16,256]{4,3,2,1,0:T(8,128)S(1)}, f32[3,16,256]{2,1,0:T(8,128)S(1)}, f32[3,16,256]{2,1,0:T(8,128)S(1)}) custom-call(s32[3]{0:T(128)S(1)} %copy-done, f32[8,10,2,16,256]{4,3,2,1,0:T(8,128)S(1)} %get-tuple-element.50.geo, f32[8,6,2,16,256]{4,3,2,1,0:T(8,128)S(1)} %change_sums.3.dsum, f32[17,16,256]{2,1,0:T(8,128)S(1)} %get-tuple-element.56.far, ...), custom_call_target="tpu_custom_call" | custom-call | tf_op jit(solution)/shard_map/step/pallas_call | solution.py:656
  24.9 0.5 collective-permute-start.4
  25.4 1.4 %collective-permute-start.5 = (f32[3,16,256]{2,1,0:T(8,128)S(1)}, f32[3,16,256]{2,1,0:T(8,128)S(1)}, u32[]{:S(2)}, u32[]{:S(2)}) collective-permute-start(f32[3,16,256]{2,1,0:T(8,128)S(1)} %get-tuple-element.68), channel_id=1, source_target_pairs={{0,7},{1,2},{2,1},{3,4},{4,3},{5,6},{6,5},{7,0},{8,15},{9,10},{10,... | collective-permute-start | bytes 147464 | tf_op jit(solution)/shard_map/ppermute | solution.py:583
  26.8 0.8 %rows.2 = (f32[17,16,256]{2,1,0:T(8,128)S(1)}, f32[17,16,256]{2,1,0:T(8,128)S(1)}, f32[17,16,256]{2,1,0:T(8,128)S(1)}) custom-call(s32[3]{0:T(128)S(1)} %copy-done, f32[8,6,2,16,256]{4,3,2,1,0:T(8,128)S(1)} %get-tuple-element.61.wsum, f32[17,16,256]{2,1,0:T(8,128)S(1)} %get-tuple-element.62.geo0, f32[17,16,256]{2,1,0:T(8,128)S(1)} %get-tuple-element.63.geo1, ...), custom_call_target="tpu_custom_call" | custom-call | tf_op jit(solution)/shard_map/rows/pallas_call | solution.py:623
  27.6 1.5 %collective-permute-done.4.y_in = f32[3,16,256]{2,1,0:T(8,128)S(1)} collective-permute-done((f32[3,16,256]{2,1,0:T(8,128)S(1)}, f32[3,16,256]{2,1,0:T(8,128)S(1)}, u32[]{:S(2)}, u32[]{:S(2)}) %collective-permute-start.4) | collective-permute-done | bytes 49184 | tf_op jit(solution)/shard_map/ppermute | solution.py:583
  29.1 2.5 %collective-permute-done.5.y_out = f32[3,16,256]{2,1,0:T(8,128)S(1)} collective-permute-done((f32[3,16,256]{2,1,0:T(8,128)S(1)}, f32[3,16,256]{2,1,0:T(8,128)S(1)}, u32[]{:S(2)}, u32[]{:S(2)}) %collective-permute-start.5) | collective-permute-done | bytes 49184 | tf_op jit(solution)/shard_map/ppermute | solution.py:583
  31.7 0.3 collective-permute-start.6
  31.9 3.3 %collective-permute-start.7 = (f32[17,16,256]{2,1,0:T(8,128)S(1)}, f32[17,16,256]{2,1,0:T(8,128)S(1)}, u32[]{:S(2)}, u32[]{:S(2)}) collective-permute-start(f32[17,16,256]{2,1,0:T(8,128)S(1)} %get-tuple-element.70.near), channel_id=1, source_target_pairs={{0,8},{8,0},{16,24},{24,16},{32,40},{40,32},{48,56},{56,48},{64,72... | collective-permute-start | bytes 835592 | tf_op jit(solution)/shard_map/ppermute | solution.py:583
  35.3 0.9 %geometry.3 = (f32[17,16,256]{2,1,0:T(8,128)S(1)}, f32[17,16,256]{2,1,0:T(8,128)S(1)}, f32[17,16,256]{2,1,0:T(8,128)S(1)}, f32[3,16,256]{2,1,0:T(8,128)S(1)}, f32[3,16,256]{2,1,0:T(8,128)S(1)}) custom-call(s32[3]{0:T(128)S(1)} %copy-done, f32[8,10,2,16,256]{4,3,2,1,0:T(8,128)S(1)} %get-tuple-element.50.geo), custom_call_target="tpu_custom_call" | custom-call | tf_op jit(solution)/shard_map/geometry/pallas_call | solution.py:597
  36.2 1.9 %change_sums.2.dsum = f32[8,6,2,16,256]{4,3,2,1,0:T(8,128)S(1)} custom-call(f32[3,12,2,16,256]{4,3,2,1,0:T(8,128)S(1)} %get-tuple-element.45.pos, f32[3,12,2,16,256]{4,3,2,1,0:T(8,128)S(1)} %get-tuple-element.51.thermal, s32[12,2,16,256]{3,2,1,0:T(8,128)S(1)} %get-tuple-element.47.code), custom_call_target="tpu_custom_call" | custom-call | tf_op jit(solution)/shard_map/change_sums/pallas_call | solution.py:586
  38.1 1.1 %inner_step.3.done = f32[8,6,2,16,256]{4,3,2,1,0:T(8,128)S(1)} custom-call(s32[3]{0:T(128)S(1)} %copy-done, f32[8,10,2,16,256]{4,3,2,1,0:T(8,128)S(1)} %get-tuple-element.50.geo, f32[8,6,2,16,256]{4,3,2,1,0:T(8,128)S(1)} %change_sums.2.dsum, f32[17,16,256]{2,1,0:T(8,128)S(1)} %get-tuple-element.73.mid, f32[3,16,256]{2,1,0:T(8,128)S(1)} %collective-permute-done.4.y_in, ...), custom_call_target="tpu_custom_call" | custom-call | tf_op jit(solution)/shard_map/inner_step/pallas_call | solution.py:647
  39.2 3.2 %collective-permute-done.6.x_far = f32[17,16,256]{2,1,0:T(8,128)S(1)} collective-permute-done((f32[17,16,256]{2,1,0:T(8,128)S(1)}, f32[17,16,256]{2,1,0:T(8,128)S(1)}, u32[]{:S(2)}, u32[]{:S(2)}) %collective-permute-start.6) | collective-permute-done | bytes 278560 | tf_op jit(solution)/shard_map/ppermute | solution.py:583
  42.4 1.5 %step.3 = (f32[8,6,2,16,256]{4,3,2,1,0:T(8,128)S(1)}, f32[3,16,256]{2,1,0:T(8,128)S(1)}, f32[3,16,256]{2,1,0:T(8,128)S(1)}) custom-call(s32[3]{0:T(128)S(1)} %copy-done, f32[8,10,2,16,256]{4,3,2,1,0:T(8,128)S(1)} %get-tuple-element.50.geo, f32[8,6,2,16,256]{4,3,2,1,0:T(8,128)S(1)} %change_sums.2.dsum, f32[17,16,256]{2,1,0:T(8,128)S(1)} %get-tuple-element.69.far, ...), custom_call_target="tpu_custom_call" | custom-call | tf_op jit(solution)/shard_map/step/pallas_call | solution.py:656
  44.0 0.1 collective-permute-start.8
  44.1 1.1 %collective-permute-start.9 = (f32[3,16,256]{2,1,0:T(8,128)S(1)}, f32[3,16,256]{2,1,0:T(8,128)S(1)}, u32[]{:S(2)}, u32[]{:S(2)}) collective-permute-start(f32[3,16,256]{2,1,0:T(8,128)S(1)} %get-tuple-element.81), channel_id=1, source_target_pairs={{0,7},{1,2},{2,1},{3,4},{4,3},{5,6},{6,5},{7,0},{8,15},{9,10},{10,... | collective-permute-start | bytes 147464 | tf_op jit(solution)/shard_map/ppermute | solution.py:583
  45.2 0.8 %rows.3 = (f32[17,16,256]{2,1,0:T(8,128)S(1)}, f32[17,16,256]{2,1,0:T(8,128)S(1)}, f32[17,16,256]{2,1,0:T(8,128)S(1)}) custom-call(s32[3]{0:T(128)S(1)} %copy-done, f32[8,6,2,16,256]{4,3,2,1,0:T(8,128)S(1)} %get-tuple-element.74.wsum, f32[17,16,256]{2,1,0:T(8,128)S(1)} %get-tuple-element.75.geo0, f32[17,16,256]{2,1,0:T(8,128)S(1)} %get-tuple-element.76.geo1, ...), custom_call_target="tpu_custom_call" | custom-call | tf_op jit(solution)/shard_map/rows/pallas_call | solution.py:623
  46.0 2.2 %collective-permute-done.8.y_in = f32[3,16,256]{2,1,0:T(8,128)S(1)} collective-permute-done((f32[3,16,256]{2,1,0:T(8,128)S(1)}, f32[3,16,256]{2,1,0:T(8,128)S(1)}, u32[]{:S(2)}, u32[]{:S(2)}) %collective-permute-start.8) | collective-permute-done | bytes 49184 | tf_op jit(solution)/shard_map/ppermute | solution.py:583
  48.1 2.2 %collective-permute-done.9.y_out = f32[3,16,256]{2,1,0:T(8,128)S(1)} collective-permute-done((f32[3,16,256]{2,1,0:T(8,128)S(1)}, f32[3,16,256]{2,1,0:T(8,128)S(1)}, u32[]{:S(2)}, u32[]{:S(2)}) %collective-permute-start.9) | collective-permute-done | bytes 49184 | tf_op jit(solution)/shard_map/ppermute | solution.py:583
  50.5 2.6 %collective-permute-start.11 = (f32[17,16,256]{2,1,0:T(8,128)S(1)}, f32[17,16,256]{2,1,0:T(8,128)S(1)}, u32[]{:S(2)}, u32[]{:S(2)}) collective-permute-start(f32[17,16,256]{2,1,0:T(8,128)S(1)} %get-tuple-element.83.near), channel_id=1, source_target_pairs={{0,8},{8,0},{16,24},{24,16},{32,40},{40,32},{48,56},{56,48},{64,72... | collective-permute-start | bytes 835592 | tf_op jit(solution)/shard_map/ppermute | solution.py:583
  53.1 1.4 %inner_particles.1.inner = f32[3,12,2,16,256]{4,3,2,1,0:T(8,128)S(1)} custom-call(s32[3]{0:T(128)S(1)} %copy-done, f32[17,16,256]{2,1,0:T(8,128)S(1)} %get-tuple-element.84.mid, f32[3,16,256]{2,1,0:T(8,128)S(1)} %collective-permute-done.8.y_in, f32[3,16,256]{2,1,0:T(8,128)S(1)} %collective-permute-done.9.y_out, ...), custom_call_target="tpu_custom_call" | custom-call | tf_op jit(solution)/shard_map/inner_particles/pallas_call | solution.py:666
  54.5 6.0 %collective-permute-done.10.x_far = f32[17,16,256]{2,1,0:T(8,128)S(1)} collective-permute-done((f32[17,16,256]{2,1,0:T(8,128)S(1)}, f32[17,16,256]{2,1,0:T(8,128)S(1)}, u32[]{:S(2)}, u32[]{:S(2)}) %collective-permute-start.10) | collective-permute-done | bytes 278560 | tf_op jit(solution)/shard_map/ppermute | solution.py:583
  60.5 2.9 %particles.1 = f32[3,12,2,16,256]{4,3,2,1,0:T(8,128)} custom-call(s32[3]{0:T(128)S(1)} %copy-done, f32[17,16,256]{2,1,0:T(8,128)S(1)} %get-tuple-element.82.far, f32[17,16,256]{2,1,0:T(8,128)S(1)} %get-tuple-element.83.near, f32[17,16,256]{2,1,0:T(8,128)S(1)} %collective-permute-done.10.x_far, f32[17,16,256]{2,1,0:T(8,128)S(1)} %collective-permute-done.11.x_near, ...), custom_call_target="tpu_custom_call" | custom-call | tf_op jit(solution)/shard_map/particles/pallas_call | solution.py:676
  (11 shorter events, 0.3 us)
Async XLA Ops:
  0.0 8.0 %copy-start = (s32[3]{0:T(128)S(1)}, s32[3]{0:T(128)}, u32[]{:S(2)}) copy-start(s32[3]{0:T(128)} %shifts.21) | copy-start | bytes 40
  3.9 8.8 %collective-permute-start = (f32[3,16,256]{2,1,0:T(8,128)S(1)}, f32[3,16,256]{2,1,0:T(8,128)S(1)}, u32[]{:S(2)}, u32[]{:S(2)}) collective-permute-start(f32[3,16,256]{2,1,0:T(8,128)S(1)} %get-tuple-element.54), channel_id=1, source_target_pairs={{0,1},{1,0},{2,3},{3,2},{4,5},{5,4},{6,7},{7,6},{8,9},{9,8},{10,11... | collective-permute-start | bytes 147464 | tf_op jit(solution)/shard_map/ppermute | solution.py:583
  5.6 7.1 %collective-permute-start.1 = (f32[3,16,256]{2,1,0:T(8,128)S(1)}, f32[3,16,256]{2,1,0:T(8,128)S(1)}, u32[]{:S(2)}, u32[]{:S(2)}) collective-permute-start(f32[3,16,256]{2,1,0:T(8,128)S(1)} %get-tuple-element.55), channel_id=1, source_target_pairs={{0,7},{1,2},{2,1},{3,4},{4,3},{5,6},{6,5},{7,0},{8,15},{9,10},{10,... | collective-permute-start | bytes 147464 | tf_op jit(solution)/shard_map/ppermute | solution.py:583
  12.8 10.5 %collective-permute-start.2 = (f32[17,16,256]{2,1,0:T(8,128)S(1)}, f32[17,16,256]{2,1,0:T(8,128)S(1)}, u32[]{:S(2)}, u32[]{:S(2)}) collective-permute-start(f32[17,16,256]{2,1,0:T(8,128)S(1)} %get-tuple-element.56.far), channel_id=1, source_target_pairs={{0,248},{8,16},{16,8},{24,32},{32,24},{40,48},{48,40},{56,64},{64,... | collective-permute-start | bytes 835592 | tf_op jit(solution)/shard_map/ppermute | solution.py:583
  12.9 10.5 %collective-permute-start.3 = (f32[17,16,256]{2,1,0:T(8,128)S(1)}, f32[17,16,256]{2,1,0:T(8,128)S(1)}, u32[]{:S(2)}, u32[]{:S(2)}) collective-permute-start(f32[17,16,256]{2,1,0:T(8,128)S(1)} %get-tuple-element.57.near), channel_id=1, source_target_pairs={{0,8},{8,0},{16,24},{24,16},{32,40},{40,32},{48,56},{56,48},{64,72... | collective-permute-start | bytes 835592 | tf_op jit(solution)/shard_map/ppermute | solution.py:583
  24.9 4.2 %collective-permute-start.4 = (f32[3,16,256]{2,1,0:T(8,128)S(1)}, f32[3,16,256]{2,1,0:T(8,128)S(1)}, u32[]{:S(2)}, u32[]{:S(2)}) collective-permute-start(f32[3,16,256]{2,1,0:T(8,128)S(1)} %get-tuple-element.67), channel_id=1, source_target_pairs={{0,1},{1,0},{2,3},{3,2},{4,5},{5,4},{6,7},{7,6},{8,9},{9,8},{10,11... | collective-permute-start | bytes 147464 | tf_op jit(solution)/shard_map/ppermute | solution.py:583
  25.4 6.2 %collective-permute-start.5 = (f32[3,16,256]{2,1,0:T(8,128)S(1)}, f32[3,16,256]{2,1,0:T(8,128)S(1)}, u32[]{:S(2)}, u32[]{:S(2)}) collective-permute-start(f32[3,16,256]{2,1,0:T(8,128)S(1)} %get-tuple-element.68), channel_id=1, source_target_pairs={{0,7},{1,2},{2,1},{3,4},{4,3},{5,6},{6,5},{7,0},{8,15},{9,10},{10,... | collective-permute-start | bytes 147464 | tf_op jit(solution)/shard_map/ppermute | solution.py:583
  31.7 10.7 %collective-permute-start.6 = (f32[17,16,256]{2,1,0:T(8,128)S(1)}, f32[17,16,256]{2,1,0:T(8,128)S(1)}, u32[]{:S(2)}, u32[]{:S(2)}) collective-permute-start(f32[17,16,256]{2,1,0:T(8,128)S(1)} %get-tuple-element.69.far), channel_id=1, source_target_pairs={{0,248},{8,16},{16,8},{24,32},{32,24},{40,48},{48,40},{56,64},{64,... | collective-permute-start | bytes 835592 | tf_op jit(solution)/shard_map/ppermute | solution.py:583
  31.9 10.5 %collective-permute-start.7 = (f32[17,16,256]{2,1,0:T(8,128)S(1)}, f32[17,16,256]{2,1,0:T(8,128)S(1)}, u32[]{:S(2)}, u32[]{:S(2)}) collective-permute-start(f32[17,16,256]{2,1,0:T(8,128)S(1)} %get-tuple-element.70.near), channel_id=1, source_target_pairs={{0,8},{8,0},{16,24},{24,16},{32,40},{40,32},{48,56},{56,48},{64,72... | collective-permute-start | bytes 835592 | tf_op jit(solution)/shard_map/ppermute | solution.py:583
  44.0 4.2 %collective-permute-start.8 = (f32[3,16,256]{2,1,0:T(8,128)S(1)}, f32[3,16,256]{2,1,0:T(8,128)S(1)}, u32[]{:S(2)}, u32[]{:S(2)}) collective-permute-start(f32[3,16,256]{2,1,0:T(8,128)S(1)} %get-tuple-element.80), channel_id=1, source_target_pairs={{0,1},{1,0},{2,3},{3,2},{4,5},{5,4},{6,7},{7,6},{8,9},{9,8},{10,11... | collective-permute-start | bytes 147464 | tf_op jit(solution)/shard_map/ppermute | solution.py:583
  44.1 6.3 %collective-permute-start.9 = (f32[3,16,256]{2,1,0:T(8,128)S(1)}, f32[3,16,256]{2,1,0:T(8,128)S(1)}, u32[]{:S(2)}, u32[]{:S(2)}) collective-permute-start(f32[3,16,256]{2,1,0:T(8,128)S(1)} %get-tuple-element.81), channel_id=1, source_target_pairs={{0,7},{1,2},{2,1},{3,4},{4,3},{5,6},{6,5},{7,0},{8,15},{9,10},{10,... | collective-permute-start | bytes 147464 | tf_op jit(solution)/shard_map/ppermute | solution.py:583
  50.4 10.1 %collective-permute-start.10 = (f32[17,16,256]{2,1,0:T(8,128)S(1)}, f32[17,16,256]{2,1,0:T(8,128)S(1)}, u32[]{:S(2)}, u32[]{:S(2)}) collective-permute-start(f32[17,16,256]{2,1,0:T(8,128)S(1)} %get-tuple-element.82.far), channel_id=1, source_target_pairs={{0,248},{8,16},{16,8},{24,32},{32,24},{40,48},{48,40},{56,64},{64,... | collective-permute-start | bytes 835592 | tf_op jit(solution)/shard_map/ppermute | solution.py:583
  50.5 10.0 %collective-permute-start.11 = (f32[17,16,256]{2,1,0:T(8,128)S(1)}, f32[17,16,256]{2,1,0:T(8,128)S(1)}, u32[]{:S(2)}, u32[]{:S(2)}) collective-permute-start(f32[17,16,256]{2,1,0:T(8,128)S(1)} %get-tuple-element.83.near), channel_id=1, source_target_pairs={{0,8},{8,0},{16,24},{24,16},{32,40},{40,32},{48,56},{56,48},{64,72... | collective-permute-start | bytes 835592 | tf_op jit(solution)/shard_map/ppermute | solution.py:583

commit v4 on v3

--- a/solution.py
+++ b/solution.py
@@ -50,7 +50,7 @@
     return p + seconds + w + cross(p, w)
 
 
-def chunk_sums(pos, rel, code, value, geo, wsum, groups, row, at, lanes):
+def chunk_sums(pos, rel, code, value, geo, wsum, quads, row, at, lanes):
     slots = code.shape[0]
     for slot in range(slots):
         p = [pos[c, slot, row, at, lanes] for c in range(3)]
@@ -59,17 +59,19 @@
             value[name, slot] = term
     codes = [code[slot, row, at, lanes] for slot in range(slots)]
 
-    def store_first(index, g, total):
-        geo[groups[g], index, row, at, lanes] = total
-
-    def store_second(index, g, total):
-        if index < 2:
-            geo[groups[g], 8 + index, row, at, lanes] = total
-        else:
-            wsum[groups[g], index - 2, row, at, lanes] = total
-
-    accumulate(value, codes, groups, [None] + list(range(7)), store_first)
-    accumulate(value, codes, groups, list(range(7, 15)), store_second)
+    for groups in quads:
+
+        def store_first(index, g, total):
+            geo[groups[g], index, row, at, lanes] = total
+
+        def store_second(index, g, total):
+            if index < 2:
+                geo[groups[g], 8 + index, row, at, lanes] = total
+            else:
+                wsum[groups[g], index - 2, row, at, lanes] = total
+
+        accumulate(value, codes, groups, [None] + list(range(7)), store_first)
+        accumulate(value, codes, groups, list(range(7, 15)), store_second)
 
 
 def halves(depth):
@@ -109,7 +111,8 @@
         at = pl.ds(8 * tile, 8)
         for copy in copies[index]:
             copy.wait()
-        groups = four(1 if tile == 0 else 0, shifts[0])
+        bys = (1, 0) if index == 0 else ((1,) if tile == 0 else (0,))
+        quads = [four(by, shifts[0]) for by in bys]
         for lanes in halves(depth):
             for slot in range(slots):
                 code[slot, row, at, lanes] = jnp.where(
@@ -119,7 +122,7 @@
                     rel[c, slot, row, at, lanes] = (
                         vel[c, slot, row, at, lanes] - thermal[c, slot, row, at, lanes]
                     )
-            chunk_sums(pos, rel, code, value, geo, wsum, groups, row, at, lanes)
+            chunk_sums(pos, rel, code, value, geo, wsum, quads, row, at, lanes)
 
     def frame_of(*where):
         return {**geo_frame(geo, *where), **vel_frame(wsum, *where)}
@@ -140,14 +143,17 @@
         for tile in range(cols // 8):
             at = pl.ds(8 * tile, 8)
             by = 0 if tile == 0 else 1
-            for o in four(1 - by, shifts[0]):
+            whole = row == 0 and tile == 0
+            for o in range(GROUPS) if whole else four(1 - by, shifts[0]):
                 for v in range(10):
                     geo[o, v, row, at, :] = geo_near[o, v, row, at, :]
                 for v in range(6):
                     wsum[o, v, row, at, :] = wsum_near[o, v, row, at, :]
-            groups = four(by, shifts[0])
+            if whole:
+                continue
+            quads = [four(by, shifts[0])]
             for lanes in halves(depth):
-                chunk_sums(pos, rel, code, value, geo, wsum, groups, row, at, lanes)
+                chunk_sums(pos, rel, code, value, geo, wsum, quads, row, at, lanes)
     outs = (low, mid, high)
     expand(lambda *where: geo_frame(geo, *where), GEO, shifts[0], outs, None, None, part, shifted)
     expand(lambda *where: vel_frame(wsum, *where), VEL, shifts[0], outs, None, None, part, shifted)

time: 63.6 us -> 63.6 us (level)
  no operation moved by 1% of the time
where the time goes in v4:
time: 63.6 us; the launch traced here: 63.5 us
  Pallas kernels  25.5 us (40%)
  waiting for transfers between devices  19.7 us (31%)
  starting transfers between devices  17.9 us (28%)
    ppermute x12, waiting for transfers between devices, swap(): return lax.ppermute(value, axis, list(enumerate(partner)))  19.7 us
    ppermute x12, starting transfers between devices, swap(): return lax.ppermute(value, axis, list(enumerate(partner)))  17.9 us
    pallas_call x1, Pallas kernels, local(): pl.pallas_call(near_sums_kernel, in_specs=[HBM] * 6, out_specs=[VMEM] * 8...  4.37 us
    pallas_call x1, Pallas kernels, local(): pl.pallas_call(rest_sums_kernel, in_specs=[SMEM] + [VMEM] * 5, out_specs=...  4.17 us
    pallas_call x2, Pallas kernels, change_sums(): pl.pallas_call(functools.partial(change_sums_kernel, step), in_specs=[VME...  3.81 us
    pallas_call x2, Pallas kernels, local(): pl.pallas_call(functools.partial(step_kernel, step), in_specs=[SMEM] + [V...  3.09 us
    pallas_call x1, Pallas kernels, local(): pl.pallas_call(particles_kernel, in_specs=[SMEM] + [VMEM] * 8, out_specs=...  2.86 us
    pallas_call x2, Pallas kernels, local(): pl.pallas_call(functools.partial(inner_step_kernel, step), in_specs=[SMEM...  2.19 us
  transfers between devices with their start and end apart: 12, of which 7 were waited for; matrix products, arithmetic and copies ran while one was open for 0% of the time, Pallas kernels for 24%

profile of v4, /device:TPU:102, one launch (start us, length us, event | category | flops | bytes accessed | tf_op | source)
XLA Modules:
  0.0 63.5 jit_solution(2072088010258642213)
XLA Ops:
  0.0 4.4 %near_sums.1 = (f32[3,12,2,16,256]{4,3,2,1,0:T(8,128)S(1)}, f32[3,12,2,16,256]{4,3,2,1,0:T(8,128)S(1)}, f32[3,12,2,16,256]{4,3,2,1,0:T(8,128)S(1)}, s32[12,2,16,...) custom-call(s32[3]{0:T(128)} %shifts.21, ...), custom_call_target="tpu_custom_call" | custom-call | tf_op jit(solution)/shard_map/near_sums/pallas_call | solution.py:567
  4.4 1.7 %collective-permute-start = (f32[3,16,256]{2,1,0:T(8,128)S(1)}, f32[3,16,256]{2,1,0:T(8,128)S(1)}, u32[]{:S(2)}, u32[]{:S(2)}) collective-permute-start(f32[3,16,256]{2,1,0:T(8,128)S(1)} %get-tuple-element.54), channel_id=1, source_target_pairs={{0,1},{1,0},{2,3},{3,2},{4,5},{5,4},{6,7},{7,6},{8,9},{9,8},{10,11... | collective-permute-start | bytes 147464 | tf_op jit(solution)/shard_map/ppermute | solution.py:589
  6.0 2.4 %collective-permute-start.1 = (f32[3,16,256]{2,1,0:T(8,128)S(1)}, f32[3,16,256]{2,1,0:T(8,128)S(1)}, u32[]{:S(2)}, u32[]{:S(2)}) collective-permute-start(f32[3,16,256]{2,1,0:T(8,128)S(1)} %get-tuple-element.55), channel_id=1, source_target_pairs={{0,7},{1,2},{2,1},{3,4},{4,3},{5,6},{6,5},{7,0},{8,15},{9,10},{10,... | collective-permute-start | bytes 147464 | tf_op jit(solution)/shard_map/ppermute | solution.py:589
  8.5 4.2 %rest_sums.1 = (f32[8,10,2,16,256]{4,3,2,1,0:T(8,128)S(1)}, f32[8,6,2,16,256]{4,3,2,1,0:T(8,128)}, f32[17,16,256]{2,1,0:T(8,128)S(1)}, f32[17,16,256]{2,1,0:T(8,128)S(1)}, f32[17,16,256]{2,1,0:T(8,128)S(1)}) custom-call(s32[3]{0:T(128)S(1)} %copy-done, f32[3,12,2,16,256]{4,3,2,1,0:T(8,128)S(1)} %get-tuple-element.45.pos, ...), custom_call_target="tpu_custom_call" | custom-call | tf_op jit(solution)/shard_map/rest_sums/pallas_call | solution.py:619
  12.7 0.1 collective-permute-start.2
  12.8 3.8 %collective-permute-start.3 = (f32[17,16,256]{2,1,0:T(8,128)S(1)}, f32[17,16,256]{2,1,0:T(8,128)S(1)}, u32[]{:S(2)}, u32[]{:S(2)}) collective-permute-start(f32[17,16,256]{2,1,0:T(8,128)S(1)} %get-tuple-element.57.near), channel_id=1, source_target_pairs={{0,8},{8,0},{16,24},{24,16},{32,40},{40,32},{48,56},{56,48},{64,72... | collective-permute-start | bytes 835592 | tf_op jit(solution)/shard_map/ppermute | solution.py:589
  16.6 0.9 %geometry.2 = (f32[17,16,256]{2,1,0:T(8,128)S(1)}, f32[17,16,256]{2,1,0:T(8,128)S(1)}, f32[17,16,256]{2,1,0:T(8,128)S(1)}, f32[3,16,256]{2,1,0:T(8,128)S(1)}, f32[3,16,256]{2,1,0:T(8,128)S(1)}) custom-call(s32[3]{0:T(128)S(1)} %copy-done, f32[8,10,2,16,256]{4,3,2,1,0:T(8,128)S(1)} %get-tuple-element.50.geo), custom_call_target="tpu_custom_call" | custom-call | tf_op jit(solution)/shard_map/geometry/pallas_call | solution.py:603
  17.6 1.9 %change_sums.3.dsum = f32[8,6,2,16,256]{4,3,2,1,0:T(8,128)S(1)} custom-call(f32[3,12,2,16,256]{4,3,2,1,0:T(8,128)S(1)} %get-tuple-element.45.pos, f32[3,12,2,16,256]{4,3,2,1,0:T(8,128)S(1)} %get-tuple-element.51.thermal, s32[12,2,16,256]{3,2,1,0:T(8,128)S(1)} %get-tuple-element.47.code), custom_call_target="tpu_custom_call" | custom-call | tf_op jit(solution)/shard_map/change_sums/pallas_call | solution.py:592
  19.5 1.1 %inner_step.2.done = f32[8,6,2,16,256]{4,3,2,1,0:T(8,128)S(1)} custom-call(s32[3]{0:T(128)S(1)} %copy-done, f32[8,10,2,16,256]{4,3,2,1,0:T(8,128)S(1)} %get-tuple-element.50.geo, f32[8,6,2,16,256]{4,3,2,1,0:T(8,128)S(1)} %change_sums.3.dsum, f32[17,16,256]{2,1,0:T(8,128)S(1)} %get-tuple-element.60.mid, f32[3,16,256]{2,1,0:T(8,128)S(1)} %collective-permute-done.y_in, ...), custom_call_target="tpu_custom_call" | custom-call | tf_op jit(solution)/shard_map/inner_step/pallas_call | solution.py:653
  20.6 2.7 %collective-permute-done.2.x_far = f32[17,16,256]{2,1,0:T(8,128)S(1)} collective-permute-done((f32[17,16,256]{2,1,0:T(8,128)S(1)}, f32[17,16,256]{2,1,0:T(8,128)S(1)}, u32[]{:S(2)}, u32[]{:S(2)}) %collective-permute-start.2) | collective-permute-done | bytes 278560 | tf_op jit(solution)/shard_map/ppermute | solution.py:589
  23.3 1.5 %step.2 = (f32[8,6,2,16,256]{4,3,2,1,0:T(8,128)S(1)}, f32[3,16,256]{2,1,0:T(8,128)S(1)}, f32[3,16,256]{2,1,0:T(8,128)S(1)}) custom-call(s32[3]{0:T(128)S(1)} %copy-done, f32[8,10,2,16,256]{4,3,2,1,0:T(8,128)S(1)} %get-tuple-element.50.geo, f32[8,6,2,16,256]{4,3,2,1,0:T(8,128)S(1)} %change_sums.3.dsum, f32[17,16,256]{2,1,0:T(8,128)S(1)} %get-tuple-element.56.far, ...), custom_call_target="tpu_custom_call" | custom-call | tf_op jit(solution)/shard_map/step/pallas_call | solution.py:662
  24.8 0.5 collective-permute-start.4
  25.3 1.7 %collective-permute-start.5 = (f32[3,16,256]{2,1,0:T(8,128)S(1)}, f32[3,16,256]{2,1,0:T(8,128)S(1)}, u32[]{:S(2)}, u32[]{:S(2)}) collective-permute-start(f32[3,16,256]{2,1,0:T(8,128)S(1)} %get-tuple-element.68), channel_id=1, source_target_pairs={{0,7},{1,2},{2,1},{3,4},{4,3},{5,6},{6,5},{7,0},{8,15},{9,10},{10,... | collective-permute-start | bytes 147464 | tf_op jit(solution)/shard_map/ppermute | solution.py:589
  27.0 0.8 %rows.2 = (f32[17,16,256]{2,1,0:T(8,128)S(1)}, f32[17,16,256]{2,1,0:T(8,128)S(1)}, f32[17,16,256]{2,1,0:T(8,128)S(1)}) custom-call(s32[3]{0:T(128)S(1)} %copy-done, f32[8,6,2,16,256]{4,3,2,1,0:T(8,128)S(1)} %get-tuple-element.61.wsum, f32[17,16,256]{2,1,0:T(8,128)S(1)} %get-tuple-element.62.geo0, f32[17,16,256]{2,1,0:T(8,128)S(1)} %get-tuple-element.63.geo1, ...), custom_call_target="tpu_custom_call" | custom-call | tf_op jit(solution)/shard_map/rows/pallas_call | solution.py:629
  27.9 1.2 %collective-permute-done.4.y_in = f32[3,16,256]{2,1,0:T(8,128)S(1)} collective-permute-done((f32[3,16,256]{2,1,0:T(8,128)S(1)}, f32[3,16,256]{2,1,0:T(8,128)S(1)}, u32[]{:S(2)}, u32[]{:S(2)}) %collective-permute-start.4) | collective-permute-done | bytes 49184 | tf_op jit(solution)/shard_map/ppermute | solution.py:589
  29.0 2.5 %collective-permute-done.5.y_out = f32[3,16,256]{2,1,0:T(8,128)S(1)} collective-permute-done((f32[3,16,256]{2,1,0:T(8,128)S(1)}, f32[3,16,256]{2,1,0:T(8,128)S(1)}, u32[]{:S(2)}, u32[]{:S(2)}) %collective-permute-start.5) | collective-permute-done | bytes 49184 | tf_op jit(solution)/shard_map/ppermute | solution.py:589
  31.6 0.3 collective-permute-start.6
  31.9 3.3 %collective-permute-start.7 = (f32[17,16,256]{2,1,0:T(8,128)S(1)}, f32[17,16,256]{2,1,0:T(8,128)S(1)}, u32[]{:S(2)}, u32[]{:S(2)}) collective-permute-start(f32[17,16,256]{2,1,0:T(8,128)S(1)} %get-tuple-element.70.near), channel_id=1, source_target_pairs={{0,8},{8,0},{16,24},{24,16},{32,40},{40,32},{48,56},{56,48},{64,72... | collective-permute-start | bytes 835592 | tf_op jit(solution)/shard_map/ppermute | solution.py:589
  35.2 0.9 %geometry.3 = (f32[17,16,256]{2,1,0:T(8,128)S(1)}, f32[17,16,256]{2,1,0:T(8,128)S(1)}, f32[17,16,256]{2,1,0:T(8,128)S(1)}, f32[3,16,256]{2,1,0:T(8,128)S(1)}, f32[3,16,256]{2,1,0:T(8,128)S(1)}) custom-call(s32[3]{0:T(128)S(1)} %copy-done, f32[8,10,2,16,256]{4,3,2,1,0:T(8,128)S(1)} %get-tuple-element.50.geo), custom_call_target="tpu_custom_call" | custom-call | tf_op jit(solution)/shard_map/geometry/pallas_call | solution.py:603
  36.1 1.9 %change_sums.2.dsum = f32[8,6,2,16,256]{4,3,2,1,0:T(8,128)S(1)} custom-call(f32[3,12,2,16,256]{4,3,2,1,0:T(8,128)S(1)} %get-tuple-element.45.pos, f32[3,12,2,16,256]{4,3,2,1,0:T(8,128)S(1)} %get-tuple-element.51.thermal, s32[12,2,16,256]{3,2,1,0:T(8,128)S(1)} %get-tuple-element.47.code), custom_call_target="tpu_custom_call" | custom-call | tf_op jit(solution)/shard_map/change_sums/pallas_call | solution.py:592
  38.0 1.1 %inner_step.3.done = f32[8,6,2,16,256]{4,3,2,1,0:T(8,128)S(1)} custom-call(s32[3]{0:T(128)S(1)} %copy-done, f32[8,10,2,16,256]{4,3,2,1,0:T(8,128)S(1)} %get-tuple-element.50.geo, f32[8,6,2,16,256]{4,3,2,1,0:T(8,128)S(1)} %change_sums.2.dsum, f32[17,16,256]{2,1,0:T(8,128)S(1)} %get-tuple-element.73.mid, f32[3,16,256]{2,1,0:T(8,128)S(1)} %collective-permute-done.4.y_in, ...), custom_call_target="tpu_custom_call" | custom-call | tf_op jit(solution)/shard_map/inner_step/pallas_call | solution.py:653
  39.1 3.2 %collective-permute-done.6.x_far = f32[17,16,256]{2,1,0:T(8,128)S(1)} collective-permute-done((f32[17,16,256]{2,1,0:T(8,128)S(1)}, f32[17,16,256]{2,1,0:T(8,128)S(1)}, u32[]{:S(2)}, u32[]{:S(2)}) %collective-permute-start.6) | collective-permute-done | bytes 278560 | tf_op jit(solution)/shard_map/ppermute | solution.py:589
  42.3 1.5 %step.3 = (f32[8,6,2,16,256]{4,3,2,1,0:T(8,128)S(1)}, f32[3,16,256]{2,1,0:T(8,128)S(1)}, f32[3,16,256]{2,1,0:T(8,128)S(1)}) custom-call(s32[3]{0:T(128)S(1)} %copy-done, f32[8,10,2,16,256]{4,3,2,1,0:T(8,128)S(1)} %get-tuple-element.50.geo, f32[8,6,2,16,256]{4,3,2,1,0:T(8,128)S(1)} %change_sums.2.dsum, f32[17,16,256]{2,1,0:T(8,128)S(1)} %get-tuple-element.69.far, ...), custom_call_target="tpu_custom_call" | custom-call | tf_op jit(solution)/shard_map/step/pallas_call | solution.py:662
  43.9 0.1 collective-permute-start.8
  44.0 1.4 %collective-permute-start.9 = (f32[3,16,256]{2,1,0:T(8,128)S(1)}, f32[3,16,256]{2,1,0:T(8,128)S(1)}, u32[]{:S(2)}, u32[]{:S(2)}) collective-permute-start(f32[3,16,256]{2,1,0:T(8,128)S(1)} %get-tuple-element.81), channel_id=1, source_target_pairs={{0,7},{1,2},{2,1},{3,4},{4,3},{5,6},{6,5},{7,0},{8,15},{9,10},{10,... | collective-permute-start | bytes 147464 | tf_op jit(solution)/shard_map/ppermute | solution.py:589
  45.4 0.8 %rows.3 = (f32[17,16,256]{2,1,0:T(8,128)S(1)}, f32[17,16,256]{2,1,0:T(8,128)S(1)}, f32[17,16,256]{2,1,0:T(8,128)S(1)}) custom-call(s32[3]{0:T(128)S(1)} %copy-done, f32[8,6,2,16,256]{4,3,2,1,0:T(8,128)S(1)} %get-tuple-element.74.wsum, f32[17,16,256]{2,1,0:T(8,128)S(1)} %get-tuple-element.75.geo0, f32[17,16,256]{2,1,0:T(8,128)S(1)} %get-tuple-element.76.geo1, ...), custom_call_target="tpu_custom_call" | custom-call | tf_op jit(solution)/shard_map/rows/pallas_call | solution.py:629
  46.2 1.9 %collective-permute-done.8.y_in = f32[3,16,256]{2,1,0:T(8,128)S(1)} collective-permute-done((f32[3,16,256]{2,1,0:T(8,128)S(1)}, f32[3,16,256]{2,1,0:T(8,128)S(1)}, u32[]{:S(2)}, u32[]{:S(2)}) %collective-permute-start.8) | collective-permute-done | bytes 49184 | tf_op jit(solution)/shard_map/ppermute | solution.py:589
  48.1 2.2 %collective-permute-done.9.y_out = f32[3,16,256]{2,1,0:T(8,128)S(1)} collective-permute-done((f32[3,16,256]{2,1,0:T(8,128)S(1)}, f32[3,16,256]{2,1,0:T(8,128)S(1)}, u32[]{:S(2)}, u32[]{:S(2)}) %collective-permute-start.9) | collective-permute-done | bytes 49184 | tf_op jit(solution)/shard_map/ppermute | solution.py:589
  50.4 2.6 %collective-permute-start.11 = (f32[17,16,256]{2,1,0:T(8,128)S(1)}, f32[17,16,256]{2,1,0:T(8,128)S(1)}, u32[]{:S(2)}, u32[]{:S(2)}) collective-permute-start(f32[17,16,256]{2,1,0:T(8,128)S(1)} %get-tuple-element.83.near), channel_id=1, source_target_pairs={{0,8},{8,0},{16,24},{24,16},{32,40},{40,32},{48,56},{56,48},{64,72... | collective-permute-start | bytes 835592 | tf_op jit(solution)/shard_map/ppermute | solution.py:589
  53.1 1.4 %inner_particles.1.inner = f32[3,12,2,16,256]{4,3,2,1,0:T(8,128)S(1)} custom-call(s32[3]{0:T(128)S(1)} %copy-done, f32[17,16,256]{2,1,0:T(8,128)S(1)} %get-tuple-element.84.mid, f32[3,16,256]{2,1,0:T(8,128)S(1)} %collective-permute-done.8.y_in, f32[3,16,256]{2,1,0:T(8,128)S(1)} %collective-permute-done.9.y_out, ...), custom_call_target="tpu_custom_call" | custom-call | tf_op jit(solution)/shard_map/inner_particles/pallas_call | solution.py:672
  54.4 6.0 %collective-permute-done.10.x_far = f32[17,16,256]{2,1,0:T(8,128)S(1)} collective-permute-done((f32[17,16,256]{2,1,0:T(8,128)S(1)}, f32[17,16,256]{2,1,0:T(8,128)S(1)}, u32[]{:S(2)}, u32[]{:S(2)}) %collective-permute-start.10) | collective-permute-done | bytes 278560 | tf_op jit(solution)/shard_map/ppermute | solution.py:589
  60.5 2.9 %particles.1 = f32[3,12,2,16,256]{4,3,2,1,0:T(8,128)} custom-call(s32[3]{0:T(128)S(1)} %copy-done, f32[17,16,256]{2,1,0:T(8,128)S(1)} %get-tuple-element.82.far, f32[17,16,256]{2,1,0:T(8,128)S(1)} %get-tuple-element.83.near, f32[17,16,256]{2,1,0:T(8,128)S(1)} %collective-permute-done.10.x_far, f32[17,16,256]{2,1,0:T(8,128)S(1)} %collective-permute-done.11.x_near, ...), custom_call_target="tpu_custom_call" | custom-call | tf_op jit(solution)/shard_map/particles/pallas_call | solution.py:682
  (11 shorter events, 0.3 us)
Async XLA Ops:
  0.0 8.5 %copy-start = (s32[3]{0:T(128)S(1)}, s32[3]{0:T(128)}, u32[]{:S(2)}) copy-start(s32[3]{0:T(128)} %shifts.21) | copy-start | bytes 40
  4.4 8.3 %collective-permute-start = (f32[3,16,256]{2,1,0:T(8,128)S(1)}, f32[3,16,256]{2,1,0:T(8,128)S(1)}, u32[]{:S(2)}, u32[]{:S(2)}) collective-permute-start(f32[3,16,256]{2,1,0:T(8,128)S(1)} %get-tuple-element.54), channel_id=1, source_target_pairs={{0,1},{1,0},{2,3},{3,2},{4,5},{5,4},{6,7},{7,6},{8,9},{9,8},{10,11... | collective-permute-start | bytes 147464 | tf_op jit(solution)/shard_map/ppermute | solution.py:589
  6.0 6.6 %collective-permute-start.1 = (f32[3,16,256]{2,1,0:T(8,128)S(1)}, f32[3,16,256]{2,1,0:T(8,128)S(1)}, u32[]{:S(2)}, u32[]{:S(2)}) collective-permute-start(f32[3,16,256]{2,1,0:T(8,128)S(1)} %get-tuple-element.55), channel_id=1, source_target_pairs={{0,7},{1,2},{2,1},{3,4},{4,3},{5,6},{6,5},{7,0},{8,15},{9,10},{10,... | collective-permute-start | bytes 147464 | tf_op jit(solution)/shard_map/ppermute | solution.py:589
  12.7 10.5 %collective-permute-start.2 = (f32[17,16,256]{2,1,0:T(8,128)S(1)}, f32[17,16,256]{2,1,0:T(8,128)S(1)}, u32[]{:S(2)}, u32[]{:S(2)}) collective-permute-start(f32[17,16,256]{2,1,0:T(8,128)S(1)} %get-tuple-element.56.far), channel_id=1, source_target_pairs={{0,248},{8,16},{16,8},{24,32},{32,24},{40,48},{48,40},{56,64},{64,... | collective-permute-start | bytes 835592 | tf_op jit(solution)/shard_map/ppermute | solution.py:589
  12.8 10.5 %collective-permute-start.3 = (f32[17,16,256]{2,1,0:T(8,128)S(1)}, f32[17,16,256]{2,1,0:T(8,128)S(1)}, u32[]{:S(2)}, u32[]{:S(2)}) collective-permute-start(f32[17,16,256]{2,1,0:T(8,128)S(1)} %get-tuple-element.57.near), channel_id=1, source_target_pairs={{0,8},{8,0},{16,24},{24,16},{32,40},{40,32},{48,56},{56,48},{64,72... | collective-permute-start | bytes 835592 | tf_op jit(solution)/shard_map/ppermute | solution.py:589
  24.8 4.2 %collective-permute-start.4 = (f32[3,16,256]{2,1,0:T(8,128)S(1)}, f32[3,16,256]{2,1,0:T(8,128)S(1)}, u32[]{:S(2)}, u32[]{:S(2)}) collective-permute-start(f32[3,16,256]{2,1,0:T(8,128)S(1)} %get-tuple-element.67), channel_id=1, source_target_pairs={{0,1},{1,0},{2,3},{3,2},{4,5},{5,4},{6,7},{7,6},{8,9},{9,8},{10,11... | collective-permute-start | bytes 147464 | tf_op jit(solution)/shard_map/ppermute | solution.py:589
  25.3 6.2 %collective-permute-start.5 = (f32[3,16,256]{2,1,0:T(8,128)S(1)}, f32[3,16,256]{2,1,0:T(8,128)S(1)}, u32[]{:S(2)}, u32[]{:S(2)}) collective-permute-start(f32[3,16,256]{2,1,0:T(8,128)S(1)} %get-tuple-element.68), channel_id=1, source_target_pairs={{0,7},{1,2},{2,1},{3,4},{4,3},{5,6},{6,5},{7,0},{8,15},{9,10},{10,... | collective-permute-start | bytes 147464 | tf_op jit(solution)/shard_map/ppermute | solution.py:589
  31.6 10.7 %collective-permute-start.6 = (f32[17,16,256]{2,1,0:T(8,128)S(1)}, f32[17,16,256]{2,1,0:T(8,128)S(1)}, u32[]{:S(2)}, u32[]{:S(2)}) collective-permute-start(f32[17,16,256]{2,1,0:T(8,128)S(1)} %get-tuple-element.69.far), channel_id=1, source_target_pairs={{0,248},{8,16},{16,8},{24,32},{32,24},{40,48},{48,40},{56,64},{64,... | collective-permute-start | bytes 835592 | tf_op jit(solution)/shard_map/ppermute | solution.py:589
  31.9 10.5 %collective-permute-start.7 = (f32[17,16,256]{2,1,0:T(8,128)S(1)}, f32[17,16,256]{2,1,0:T(8,128)S(1)}, u32[]{:S(2)}, u32[]{:S(2)}) collective-permute-start(f32[17,16,256]{2,1,0:T(8,128)S(1)} %get-tuple-element.70.near), channel_id=1, source_target_pairs={{0,8},{8,0},{16,24},{24,16},{32,40},{40,32},{48,56},{56,48},{64,72... | collective-permute-start | bytes 835592 | tf_op jit(solution)/shard_map/ppermute | solution.py:589
  43.9 4.2 %collective-permute-start.8 = (f32[3,16,256]{2,1,0:T(8,128)S(1)}, f32[3,16,256]{2,1,0:T(8,128)S(1)}, u32[]{:S(2)}, u32[]{:S(2)}) collective-permute-start(f32[3,16,256]{2,1,0:T(8,128)S(1)} %get-tuple-element.80), channel_id=1, source_target_pairs={{0,1},{1,0},{2,3},{3,2},{4,5},{5,4},{6,7},{7,6},{8,9},{9,8},{10,11... | collective-permute-start | bytes 147464 | tf_op jit(solution)/shard_map/ppermute | solution.py:589
  44.0 6.3 %collective-permute-start.9 = (f32[3,16,256]{2,1,0:T(8,128)S(1)}, f32[3,16,256]{2,1,0:T(8,128)S(1)}, u32[]{:S(2)}, u32[]{:S(2)}) collective-permute-start(f32[3,16,256]{2,1,0:T(8,128)S(1)} %get-tuple-element.81), channel_id=1, source_target_pairs={{0,7},{1,2},{2,1},{3,4},{4,3},{5,6},{6,5},{7,0},{8,15},{9,10},{10,... | collective-permute-start | bytes 147464 | tf_op jit(solution)/shard_map/ppermute | solution.py:589
  50.3 10.1 %collective-permute-start.10 = (f32[17,16,256]{2,1,0:T(8,128)S(1)}, f32[17,16,256]{2,1,0:T(8,128)S(1)}, u32[]{:S(2)}, u32[]{:S(2)}) collective-permute-start(f32[17,16,256]{2,1,0:T(8,128)S(1)} %get-tuple-element.82.far), channel_id=1, source_target_pairs={{0,248},{8,16},{16,8},{24,32},{32,24},{40,48},{48,40},{56,64},{64,... | collective-permute-start | bytes 835592 | tf_op jit(solution)/shard_map/ppermute | solution.py:589
  50.4 10.0 %collective-permute-start.11 = (f32[17,16,256]{2,1,0:T(8,128)S(1)}, f32[17,16,256]{2,1,0:T(8,128)S(1)}, u32[]{:S(2)}, u32[]{:S(2)}) collective-permute-start(f32[17,16,256]{2,1,0:T(8,128)S(1)} %get-tuple-element.83.near), channel_id=1, source_target_pairs={{0,8},{8,0},{16,24},{24,16},{32,40},{40,32},{48,56},{56,48},{64,72... | collective-permute-start | bytes 835592 | tf_op jit(solution)/shard_map/ppermute | solution.py:589
